TPU v7x, 32 devices: a whole 2x2x4 slice. The times are simulated.
32 devices in a mesh: band: 8 (over z, y), grid: 4 (over x, core).
Axes of the slice: x: 2, y: 2, z: 4, core: 2. Of those that a mesh axis runs over, the one named last changes fastest.
Arguments:
- orbitals: float32 [24, 64, 4096], P('band', 'grid'), may hold values from -6 to 6
- pair_mask: int32 [24, 24], replicated, may hold values from 0 to 1, as said below
Outputs:
- exchange_term: float32 [24, 64, 4096], P('band', 'grid')
Inputs may be any that keep to these rules, and one draw needn't show every extreme that they name: pair_mask is symmetric; entries outside the candidate pairs of every block (and their transposes) are 0; each block has at most 12 candidate pairs with mask 1, and some block has exactly 12.
All inputs are finite; a program needn't handle non-finite values.
Results may differ from a plain program's by a relative error of at most 0.00027.
Values sent between devices are 32-bit elements; how exact they have to be, the bound alone decides.
No kernel may reach another device: no remote copies, remote signals or barrier semaphores. Data moves between devices by JAX's collectives and lax.ppermute only.
A program may use at most 64 MiB of HBM per device.

v0:
```python
import math

import jax
import jax.numpy as jnp
import numpy as np
from jax import lax
from jax.sharding import PartitionSpec as P

NG = 64
ORB_DEV = 3
REACH = 2
NCAND = 24
CAP = 12


MIXING = 0.25
BOX_LENGTH = 16.0
EXACT_PRECISION = lax.Precision.HIGHEST
turn_pairs = 4


def shifted(block, axis, distance):
    devices = range(lax.axis_size(axis))
    route = [((i - distance) % len(devices), i) for i in devices]
    return lax.ppermute(block, axis, route)


def pair_table():
    entries = []
    for distance in range(REACH + 1):
        for leading_orbital in range(ORB_DEV):
            for second_orb in range(ORB_DEV):
                if distance > 0 or leading_orbital <= second_orb:
                    entries.append((leading_orbital, distance, second_orb))
    return np.array(entries, dtype=np.int32)


def dft_tables(length):
    positions = jnp.arange(length, dtype=jnp.int32)
    product_mod = positions[:, None] * positions[None, :] % length
    angles = product_mod.astype(jnp.float32) * (2.0 * math.pi / length)
    return (jnp.cos(angles), jnp.sin(angles))


def rotate_parts(values_in):
    half_width = values_in.shape[-1] // 2
    return jnp.concatenate([values_in[..., half_width:], -values_in[..., :half_width]], axis=-1)


def transform_axis(values_in, tables, formula, sweep_direction):
    cosine_table, sine_table = tables
    direct_part = jnp.einsum(formula, cosine_table, values_in, precision=EXACT_PRECISION)
    crossed_part = jnp.einsum(formula, sine_table, values_in, precision=EXACT_PRECISION)
    return direct_part + sweep_direction * rotate_parts(crossed_part)


def signed_frequency(positions):
    return jnp.where(positions < NG // 2, positions, positions - NG)


def coulomb_values(squared):
    safe_values = jnp.maximum(squared, 1).astype(jnp.float32)
    return jnp.where(squared > 0, BOX_LENGTH * BOX_LENGTH / math.pi / safe_values, 0.0)


def solve_poisson(density, tables, kernel_pair, z_tables):
    count_pairs = density.shape[0]
    planes = density.shape[1]
    cubes = density.reshape(count_pairs, planes, NG, NG)
    spectrum = jnp.einsum("pxyz,zk->pxyk", cubes, z_tables[1], precision=EXACT_PRECISION)
    spectrum = transform_axis(spectrum, tables, "ky,pxyc->pxkc", 1.0)
    columns = lax.all_to_all(spectrum, "grid", split_axis=2, concat_axis=1, tiled=True)
    columns = transform_axis(columns, tables, "kx,pxyc->pkyc", 1.0)
    columns = columns * kernel_pair[None]
    columns = transform_axis(columns, tables, "kx,pxyc->pkyc", -1.0)
    returned = lax.all_to_all(columns, "grid", split_axis=1, concat_axis=2, tiled=True)
    returned = transform_axis(returned, tables, "ky,pxyc->pxkc", -1.0)
    potential = jnp.einsum("pxyc,ck->pxyk", returned, z_tables[3], precision=EXACT_PRECISION)
    return potential.reshape(count_pairs, planes, NG * NG)


def local(orbitals, pair_mask):
    orb_count, planes, cells = orbitals.shape
    groups = lax.axis_size("band")
    band_index = lax.axis_index("band")
    grid_index = lax.axis_index("grid")
    visits = [orbitals]
    for distance in range(1, REACH + 1):
        visits.append(shifted(orbitals, "band", -distance))
    flat_count = (REACH + 1) * orb_count
    flat_visiting = jnp.stack(visits).reshape(flat_count, planes, cells)
    pair_list = pair_table()
    first_ids = jnp.asarray(pair_list[:, 0])
    offsets = jnp.asarray(pair_list[:, 1])
    second_ids = jnp.asarray(pair_list[:, 2])
    row_ids = band_index * ORB_DEV + first_ids
    col_ids = (band_index + offsets) % groups * ORB_DEV + second_ids
    live_flags = pair_mask[row_ids, col_ids]
    sort_keys = (1 - live_flags) * NCAND + jnp.arange(NCAND, dtype=jnp.int32)
    live_order = jnp.argsort(sort_keys)[:CAP]
    first_ids = first_ids[live_order]
    offsets = offsets[live_order]
    second_ids = second_ids[live_order]
    live_flags = live_flags[live_order]
    padding = -first_ids.shape[0] % turn_pairs

    def padded(values_in):
        return jnp.concatenate([values_in, jnp.zeros((padding,), jnp.int32)])

    first_ids = padded(first_ids)
    offsets = padded(offsets)
    second_ids = padded(second_ids)
    live_flags = padded(live_flags)
    slot_ids = offsets * ORB_DEV + second_ids
    weights = live_flags.astype(jnp.float32)
    self_flags = 1.0 - ((offsets == 0) & (first_ids == second_ids)).astype(jnp.float32)
    turns = first_ids.shape[0] // turn_pairs
    tables = dft_tables(NG)
    cosine_table, sine_table = tables
    forward_complex = jnp.block([[cosine_table, -sine_table], [sine_table, cosine_table]])
    forward_real = jnp.concatenate([cosine_table, -sine_table], axis=1)
    inverse_complex = jnp.block([[cosine_table, sine_table], [-sine_table, cosine_table]])
    inverse_real = jnp.concatenate([cosine_table, -sine_table], axis=0)
    z_tables = (forward_complex, forward_real, inverse_complex, inverse_real)
    waves_first = signed_frequency(jnp.arange(NG, dtype=jnp.int32))[:, None, None]
    waves_second = signed_frequency(grid_index * planes + jnp.arange(planes, dtype=jnp.int32))[
        None, :, None
    ]
    waves_third = signed_frequency(jnp.arange(NG, dtype=jnp.int32))[None, None, :]
    kernel = coulomb_values(
        waves_first * waves_first + waves_second * waves_second + waves_third * waves_third
    ) / float(NG**3)
    kernel_pair = jnp.concatenate([kernel, kernel], axis=-1)

    def one_turn(totals, turn_input):
        owned_total, visit_total = totals
        first_turn, slot_turn, weight_turn, self_turn = turn_input
        leading_orbital = orbitals[first_turn]
        second_orb = flat_visiting[slot_turn]
        potential = solve_poisson(leading_orbital * second_orb, tables, kernel_pair, z_tables)
        weighted_density = potential * weight_turn[:, None, None]
        owner_hot = (first_turn[:, None] == jnp.arange(orb_count, dtype=jnp.int32)[None, :]).astype(
            jnp.float32
        )
        visit_onehot_mask = (
            slot_turn[:, None] == jnp.arange(flat_count, dtype=jnp.int32)[None, :]
        ).astype(jnp.float32) * self_turn[:, None]
        owned_total = owned_total + jnp.einsum(
            "pa,pxc->axc", owner_hot, weighted_density * second_orb, precision=EXACT_PRECISION
        )
        visit_total = visit_total + jnp.einsum(
            "sq,swt->qwt",
            visit_onehot_mask,
            weighted_density * leading_orbital,
            precision=EXACT_PRECISION,
        )
        return ((owned_total, visit_total), None)

    start_totals = (
        jnp.zeros((orb_count, planes, cells), jnp.float32),
        jnp.zeros((flat_count, planes, cells), jnp.float32),
    )
    turn_inputs = (
        first_ids.reshape(turns, turn_pairs),
        slot_ids.reshape(turns, turn_pairs),
        weights.reshape(turns, turn_pairs),
        self_flags.reshape(turns, turn_pairs),
    )
    (owned_total, visit_total), discarded_value = lax.scan(one_turn, start_totals, turn_inputs)
    visit_total = visit_total.reshape(REACH + 1, orb_count, planes, cells)
    owned = owned_total + visit_total[0]
    for distance in range(1, REACH + 1):
        owned = owned + shifted(visit_total[distance], "band", distance)
    return -MIXING * owned


def solution(mesh):
    return jax.shard_map(
        local,
        mesh=mesh,
        in_specs=(P("band", "grid", None), P()),
        out_specs=P("band", "grid", None),
        check_vma=False,
    )
```

profile of v0, /device:TPU:4, one launch (start us, length us, event | category | flops | bytes accessed | tf_op | source)
XLA Modules:
  0.0 429.0 jit_solution(6110495410781894998)
XLA Ops:
  0.0 4.1 collective-permute-start.1
  14.0 7.5 %collective-permute-done = f32[3,16,4096]{2,1,0:T(8,128)S(1)} collective-permute-done((f32[3,16,4096]{2,1,0:T(8,128)}, f32[3,16,4096]{2,1,0:T(8,128)S(1)}, u32[]{:S(2)}, u32[]{:S(2)}) %collective-permute-start) | collective-permute-done | bytes 786464 | tf_op jit(solution)/shard_map/ppermute | solution.py:25
  23.2 345.8 %while.14 = (s32[]{:T(128)}, f32[3,16,4096]{2,0,1:T(4,128)}, f32[9,16,4096]{2,0,1:T(8,128)}, s32[3,4]{1,0:T(4,128)S(1)}, f32[3,16,4096]{2,1,0:T(8,128)S(1)}, /*i...) while((s32[]{:T(128)}, f32[3,16,4096]{2,0,1:T(4,128)}, ...), condition=%wide.region_2.3_spmd.clone.clone, body=%wide.region_1.2_spmd.clone.clone.sunk | while | flops 4074178560 | bytes 148447920 | solution.py:169
  23.8 2.3 gather_fusion.1
  26.2 2.2 mul.821
  28.5 3.5 fusion.191
  34.9 2.8 maximum_add_fusion.3
  38.9 28.2 %all_to_all.48 = f32[4,16,64,128]{3,1,0,2:T(8,128)S(1)} all-to-all(f32[4,16,64,128]{3,1,0,2:T(8,128)S(1)} %copy.52), channel_id=1, replica_groups=mesh['band'=8,'grid'=4] {'grid'}, dimensions={2} | all-to-all | bytes 4194304 | tf_op jit(solution)/shard_map/while/body/eval_jaxpr/all_to_all | solution.py:72
  70.6 3.0 fusion.194
  76.7 2.8 fusion.196
  79.4 3.2 copy.54
  82.6 4.5 %all-to-all-start.1 = ((f32[4,64,16,128]{3,2,0,1:T(8,128)}), f32[4,64,16,128]{3,2,0,1:T(8,128)}, u32[]{:S(2)}, u32[]{:S(2)}) async-start(f32[4,64,16,128]{3,2,0,1:T(8,128)} %copy.54), calls=%async_computation.1 | async-start | bytes 4194304 | tf_op jit(solution)/shard_map/while/body/eval_jaxpr/all_to_all | solution.py:76
  87.1 25.7 %all-to-all-done.1 = f32[4,64,16,128]{3,2,0,1:T(8,128)} async-done(((f32[4,64,16,128]{3,2,0,1:T(8,128)}), f32[4,64,16,128]{3,2,0,1:T(8,128)}, u32[]{:S(2)}, u32[]{:S(2)}) %all-to-all-start.1) | async-done | bytes 2097184 | tf_op jit(solution)/shard_map/while/body/eval_jaxpr/all_to_all | solution.py:76
  119.8 3.4 fusion.199
  123.3 2.3 reshape.255
  126.8 2.5 convolution_add_fusion.4
  129.3 6.4 %convolution_add_fusion.5 = f32[9,16,4096]{2,0,1:T(8,128)S(1)} fusion(f32[9,16,4096]{2,0,1:T(8,128)S(1)} %copy-done.2, pred[]{:T(512)S(6)} %compare.9, f32[4,16,4096]{2,1,0:T(8,128)S(1)} %get-tuple-element.364, f32[4]{0:T(128)S(1)} %get-tuple-element.365, s32[4]{0:T(128)S(1)} %get-tuple-element.366), kind=kOutput, calls=%fused_computation.9.clone.1 | convolution fusion | flops 29491272 | bytes 5767201 | tf_op jit(solution)/shard_map/while/body/eval_jaxpr/sq,swt->qwt/dot_general | solution.py:151
  138.5 2.3 gather_fusion.1
  140.9 2.2 mul.821
  143.2 3.5 fusion.191
  149.6 2.8 maximum_add_fusion.3
  153.6 28.1 %all_to_all.48 = f32[4,16,64,128]{3,1,0,2:T(8,128)S(1)} all-to-all(f32[4,16,64,128]{3,1,0,2:T(8,128)S(1)} %copy.52), channel_id=1, replica_groups=mesh['band'=8,'grid'=4] {'grid'}, dimensions={2} | all-to-all | bytes 4194304 | tf_op jit(solution)/shard_map/while/body/eval_jaxpr/all_to_all | solution.py:72
  185.2 3.1 fusion.194
  191.3 2.8 fusion.196
  194.0 2.8 copy.54
  196.8 4.5 %all-to-all-start.1 = ((f32[4,64,16,128]{3,2,0,1:T(8,128)}), f32[4,64,16,128]{3,2,0,1:T(8,128)}, u32[]{:S(2)}, u32[]{:S(2)}) async-start(f32[4,64,16,128]{3,2,0,1:T(8,128)} %copy.54), calls=%async_computation.1 | async-start | bytes 4194304 | tf_op jit(solution)/shard_map/while/body/eval_jaxpr/all_to_all | solution.py:76
  201.3 25.7 %all-to-all-done.1 = f32[4,64,16,128]{3,2,0,1:T(8,128)} async-done(((f32[4,64,16,128]{3,2,0,1:T(8,128)}), f32[4,64,16,128]{3,2,0,1:T(8,128)}, u32[]{:S(2)}, u32[]{:S(2)}) %all-to-all-start.1) | async-done | bytes 2097184 | tf_op jit(solution)/shard_map/while/body/eval_jaxpr/all_to_all | solution.py:76
  234.0 3.4 fusion.199
  237.4 2.3 reshape.255
  241.0 2.5 convolution_add_fusion.4
  243.5 6.4 %convolution_add_fusion.5 = f32[9,16,4096]{2,0,1:T(8,128)S(1)} fusion(f32[9,16,4096]{2,0,1:T(8,128)S(1)} %copy-done.2, pred[]{:T(512)S(6)} %compare.9, f32[4,16,4096]{2,1,0:T(8,128)S(1)} %get-tuple-element.364, f32[4]{0:T(128)S(1)} %get-tuple-element.365, s32[4]{0:T(128)S(1)} %get-tuple-element.366), kind=kOutput, calls=%fused_computation.9.clone.1 | convolution fusion | flops 29491272 | bytes 5767201 | tf_op jit(solution)/shard_map/while/body/eval_jaxpr/sq,swt->qwt/dot_general | solution.py:151
  252.9 2.3 gather_fusion.1
  257.6 3.5 fusion.191
  264.0 2.8 maximum_add_fusion.3
  268.0 28.1 %all_to_all.48 = f32[4,16,64,128]{3,1,0,2:T(8,128)S(1)} all-to-all(f32[4,16,64,128]{3,1,0,2:T(8,128)S(1)} %copy.52), channel_id=1, replica_groups=mesh['band'=8,'grid'=4] {'grid'}, dimensions={2} | all-to-all | bytes 4194304 | tf_op jit(solution)/shard_map/while/body/eval_jaxpr/all_to_all | solution.py:72
  299.6 3.1 fusion.194
  305.7 2.8 fusion.196
  308.4 2.8 copy.54
  311.2 4.5 %all-to-all-start.1 = ((f32[4,64,16,128]{3,2,0,1:T(8,128)}), f32[4,64,16,128]{3,2,0,1:T(8,128)}, u32[]{:S(2)}, u32[]{:S(2)}) async-start(f32[4,64,16,128]{3,2,0,1:T(8,128)} %copy.54), calls=%async_computation.1 | async-start | bytes 4194304 | tf_op jit(solution)/shard_map/while/body/eval_jaxpr/all_to_all | solution.py:76
  315.7 25.7 %all-to-all-done.1 = f32[4,64,16,128]{3,2,0,1:T(8,128)} async-done(((f32[4,64,16,128]{3,2,0,1:T(8,128)}), f32[4,64,16,128]{3,2,0,1:T(8,128)}, u32[]{:S(2)}, u32[]{:S(2)}) %all-to-all-start.1) | async-done | bytes 2097184 | tf_op jit(solution)/shard_map/while/body/eval_jaxpr/all_to_all | solution.py:76
  348.5 3.4 fusion.199
  351.9 2.5 reshape.255
  355.7 2.5 convolution_add_fusion.4
  358.1 6.4 %convolution_add_fusion.5 = f32[9,16,4096]{2,0,1:T(8,128)S(1)} fusion(f32[9,16,4096]{2,0,1:T(8,128)S(1)} %copy-done.2, pred[]{:T(512)S(6)} %compare.9, f32[4,16,4096]{2,1,0:T(8,128)S(1)} %get-tuple-element.364, f32[4]{0:T(128)S(1)} %get-tuple-element.365, s32[4]{0:T(128)S(1)} %get-tuple-element.366), kind=kOutput, calls=%fused_computation.9.clone.1 | convolution fusion | flops 29491272 | bytes 5767201 | tf_op jit(solution)/shard_map/while/body/eval_jaxpr/sq,swt->qwt/dot_general | solution.py:151
  369.0 3.6 copy.31
  372.7 17.3 %collective-permute-start.2 = (f32[3,16,4096]{2,1,0:T(8,128)S(1)}, f32[3,16,4096]{2,1,0:T(8,128)S(1)}, u32[]{:S(2)}, u32[]{:S(2)}) collective-permute-start(f32[3,16,4096]{2,1,0:T(8,128)S(1)} %get-tuple-element.258), channel_id=1, source_target_pairs={{28,0},{0,4},{4,8},{8,12},{12,16},{16,20},{20,24},{24,28},{29,1},{... | collective-permute-start | bytes 2359304 | tf_op jit(solution)/shard_map/ppermute | solution.py:25
  391.6 16.4 %collective-permute-done.2 = f32[3,16,4096]{2,1,0:T(8,128)S(1)} collective-permute-done((f32[3,16,4096]{2,1,0:T(8,128)S(1)}, f32[3,16,4096]{2,1,0:T(8,128)S(1)}, u32[]{:S(2)}, u32[]{:S(2)}) %collective-permute-start.2) | collective-permute-done | bytes 786464 | tf_op jit(solution)/shard_map/ppermute | solution.py:25
  408.0 19.3 %collective-permute-done.3 = f32[3,16,4096]{2,1,0:T(8,128)S(1)} collective-permute-done((f32[3,16,4096]{2,1,0:T(8,128)S(1)}, f32[3,16,4096]{2,1,0:T(8,128)S(1)}, u32[]{:S(2)}, u32[]{:S(2)}) %collective-permute-start.3) | collective-permute-done | bytes 786464 | tf_op jit(solution)/shard_map/ppermute | solution.py:25
  (143 shorter events, 81.4 us)
Async XLA Ops:
  0.0 4.8 %copy-start = (s32[24,24]{1,0:T(8,128)S(1)}, s32[24,24]{1,0:T(8,128)}, u32[]{:S(2)}) copy-start(s32[24,24]{1,0:T(8,128)} %param.8) | copy-start | bytes 6916
  0.0 21.5 %collective-permute-start = (f32[3,16,4096]{2,1,0:T(8,128)}, f32[3,16,4096]{2,1,0:T(8,128)S(1)}, u32[]{:S(2)}, u32[]{:S(2)}) collective-permute-start(f32[3,16,4096]{2,1,0:T(8,128)} %param.7), channel_id=1, source_target_pairs={{4,0},{8,4},{12,8},{16,12},{20,16},{24,20},{28,24},{0,28},{5,1},{9... | collective-permute-start | bytes 2359304 | tf_op jit(solution)/shard_map/ppermute | solution.py:25
  0.0 21.5 %collective-permute-start.1 = (f32[3,16,4096]{2,1,0:T(8,128)}, f32[3,16,4096]{2,1,0:T(8,128)S(1)}, u32[]{:S(2)}, u32[]{:S(2)}) collective-permute-start(f32[3,16,4096]{2,1,0:T(8,128)} %param.7), channel_id=1, source_target_pairs={{8,0},{12,4},{16,8},{20,12},{24,16},{28,20},{0,24},{4,28},{9,1},{1... | collective-permute-start | bytes 2359304 | tf_op jit(solution)/shard_map/ppermute | solution.py:25
  5.6 15.9 %copy-start.4 = (f32[3,16,4096]{2,1,0:T(8,128)S(1)}, f32[3,16,4096]{2,1,0:T(8,128)}, u32[]{:S(2)}) copy-start(f32[3,16,4096]{2,1,0:T(8,128)} %param.7) | copy-start | bytes 2359300
  69.6 1.0 copy-start.9
  82.6 30.2 %all-to-all-start.1 = ((f32[4,64,16,128]{3,2,0,1:T(8,128)}), f32[4,64,16,128]{3,2,0,1:T(8,128)}, u32[]{:S(2)}, u32[]{:S(2)}) async-start(f32[4,64,16,128]{3,2,0,1:T(8,128)} %copy.54), calls=%async_computation.1 | async-start | bytes 4194304 | tf_op jit(solution)/shard_map/while/body/eval_jaxpr/all_to_all | solution.py:76
  125.6 1.2 copy-start.6
  125.6 3.7 copy-start.2
  129.3 6.4 %copy-start.7 = (f32[3,16,4096]{2,0,1:T(4,128)}, f32[3,16,4096]{2,0,1:T(4,128)S(1)}, u32[]{:S(2)}) copy-start(f32[3,16,4096]{2,0,1:T(4,128)S(1)} %convolution_add_fusion.4) | copy-start | bytes 2359300 | tf_op jit(solution)/shard_map/while
  129.3 8.4 %copy-start.5 = (f32[3,16,4096]{2,1,0:T(8,128)S(1)}, f32[3,16,4096]{2,1,0:T(8,128)}, u32[]{:S(2)}) copy-start(f32[3,16,4096]{2,1,0:T(8,128)} %get-tuple-element.427) | copy-start | bytes 2359300 | tf_op jit(solution)/shard_map/while
  135.7 2.0 copy-start.3
  184.2 1.0 copy-start.9
  196.8 30.2 %all-to-all-start.1 = ((f32[4,64,16,128]{3,2,0,1:T(8,128)}), f32[4,64,16,128]{3,2,0,1:T(8,128)}, u32[]{:S(2)}, u32[]{:S(2)}) async-start(f32[4,64,16,128]{3,2,0,1:T(8,128)} %copy.54), calls=%async_computation.1 | async-start | bytes 4194304 | tf_op jit(solution)/shard_map/while/body/eval_jaxpr/all_to_all | solution.py:76
  239.8 1.2 copy-start.6
  239.8 3.7 copy-start.2
  243.5 6.4 %copy-start.7 = (f32[3,16,4096]{2,0,1:T(4,128)}, f32[3,16,4096]{2,0,1:T(4,128)S(1)}, u32[]{:S(2)}) copy-start(f32[3,16,4096]{2,0,1:T(4,128)S(1)} %convolution_add_fusion.4) | copy-start | bytes 2359300 | tf_op jit(solution)/shard_map/while
  243.5 8.4 %copy-start.5 = (f32[3,16,4096]{2,1,0:T(8,128)S(1)}, f32[3,16,4096]{2,1,0:T(8,128)}, u32[]{:S(2)}) copy-start(f32[3,16,4096]{2,1,0:T(8,128)} %get-tuple-element.427) | copy-start | bytes 2359300 | tf_op jit(solution)/shard_map/while
  249.9 2.0 copy-start.3
  298.6 1.0 copy-start.9
  311.2 30.2 %all-to-all-start.1 = ((f32[4,64,16,128]{3,2,0,1:T(8,128)}), f32[4,64,16,128]{3,2,0,1:T(8,128)}, u32[]{:S(2)}, u32[]{:S(2)}) async-start(f32[4,64,16,128]{3,2,0,1:T(8,128)} %copy.54), calls=%async_computation.1 | async-start | bytes 4194304 | tf_op jit(solution)/shard_map/while/body/eval_jaxpr/all_to_all | solution.py:76
  354.4 1.2 copy-start.6
  354.4 3.7 copy-start.2
  358.1 6.4 %copy-start.7 = (f32[3,16,4096]{2,0,1:T(4,128)}, f32[3,16,4096]{2,0,1:T(4,128)S(1)}, u32[]{:S(2)}) copy-start(f32[3,16,4096]{2,0,1:T(4,128)S(1)} %convolution_add_fusion.4) | copy-start | bytes 2359300 | tf_op jit(solution)/shard_map/while
  358.1 8.4 %copy-start.5 = (f32[3,16,4096]{2,1,0:T(8,128)S(1)}, f32[3,16,4096]{2,1,0:T(8,128)}, u32[]{:S(2)}) copy-start(f32[3,16,4096]{2,1,0:T(8,128)} %get-tuple-element.427) | copy-start | bytes 2359300 | tf_op jit(solution)/shard_map/while
  364.6 2.0 copy-start.3
  372.6 54.8 %copy-start.8 = (f32[3,16,4096]{2,0,1:T(4,128)S(1)}, f32[3,16,4096]{2,0,1:T(4,128)}, u32[]{:S(2)}) copy-start(f32[3,16,4096]{2,0,1:T(4,128)} %get-tuple-element.414) | copy-start | bytes 2359300
  372.7 35.3 %collective-permute-start.2 = (f32[3,16,4096]{2,1,0:T(8,128)S(1)}, f32[3,16,4096]{2,1,0:T(8,128)S(1)}, u32[]{:S(2)}, u32[]{:S(2)}) collective-permute-start(f32[3,16,4096]{2,1,0:T(8,128)S(1)} %get-tuple-element.258), channel_id=1, source_target_pairs={{28,0},{0,4},{4,8},{8,12},{12,16},{16,20},{20,24},{24,28},{29,1},{... | collective-permute-start | bytes 2359304 | tf_op jit(solution)/shard_map/ppermute | solution.py:25
  390.0 37.3 %collective-permute-start.3 = (f32[3,16,4096]{2,1,0:T(8,128)S(1)}, f32[3,16,4096]{2,1,0:T(8,128)S(1)}, u32[]{:S(2)}, u32[]{:S(2)}) collective-permute-start(f32[3,16,4096]{2,1,0:T(8,128)S(1)} %get-tuple-element.259), channel_id=1, source_target_pairs={{24,0},{28,4},{0,8},{4,12},{8,16},{12,20},{16,24},{20,28},{25,1},{... | collective-permute-start | bytes 2359304 | tf_op jit(solution)/shard_map/ppermute | solution.py:25
  427.3 1.5 copy-start.1
where the time goes:
time: 432 us; the launch traced here: 429 us
  waiting for transfers between devices  120 us (28%)
  matrix products  105 us (24%)
  blocking collectives  84.5 us (20%)
  local copies, waits for them, and re-layouts  59.8 us (14%)
  starting transfers between devices  36.4 us (8%)
  other arithmetic  18.6 us (4%)
    all_to_all x3, blocking collectives, solve_poisson(): lax.all_to_all(spectrum, 'grid', split_axis=2, concat_axis=1, tiled=True)  84.5 us
    all_to_all x3, waiting for transfers between devices, solve_poisson(): lax.all_to_all(columns, 'grid', split_axis=1, concat_axis=2, tiled=True)  77.1 us
    ppermute x4, waiting for transfers between devices, shifted(): return lax.ppermute(block, axis, route)  43.2 us
    dot_general x12, matrix products, transform_axis(): jnp.einsum(formula, cosine_table, values_in, precision=EXACT_PRECISION)  32.2 us
    dot_general x12, matrix products, transform_axis(): jnp.einsum(formula, sine_table, values_in, precision=EXACT_PRECISION)  25.6 us
    ppermute x4, starting transfers between devices, shifted(): return lax.ppermute(block, axis, route)  23 us
    dot_general x3, matrix products, one_turn(): jnp.einsum('sq,swt->qwt', visit_onehot_mask, weighted_density * leading_o...  19.2 us
    all_to_all x3, starting transfers between devices, solve_poisson(): lax.all_to_all(columns, 'grid', split_axis=1, concat_axis=2, tiled=True)  13.4 us
  transfers between devices with their start and end apart: 7, of which 6 were waited for; matrix products, arithmetic and copies ran while one was open for 2% of the time, Pallas kernels for 0%

commit v1 on v0

v1 whole, which is shorter than its diff:
```python
import math

import jax
import jax.numpy as jnp
import numpy as np
from jax import lax
from jax.experimental import pallas as pl
from jax.experimental.pallas import tpu as pltpu
from jax.sharding import PartitionSpec as P

ORB_DEV = 3
REACH = 2
CAP = 12
MIXING = 0.25
BOX_LENGTH = 16.0
GROUP = 4
BLOCK_PLANES = 8


def shifted(block, axis, distance):
    count = lax.axis_size(axis)
    return lax.ppermute(block, axis, [((i - distance) % count, i) for i in range(count)])


def pair_table():
    entries = []
    for distance in range(REACH + 1):
        for leading in range(ORB_DEV):
            for second in range(ORB_DEV):
                if distance > 0 or leading <= second:
                    entries.append((leading, distance, second))
    return np.array(entries, dtype=np.int32)


def split_table(table):
    high = table.astype(np.float32).astype(jnp.bfloat16)
    low = (table - high.astype(np.float64)).astype(np.float32).astype(jnp.bfloat16)
    return jnp.asarray(high), jnp.asarray(low)


def dft_tables(n):
    k = np.arange(n)
    angles = (k[:, None] * k[None, :] % n) * (2.0 * math.pi / n)
    c, s = np.cos(angles), np.sin(angles)
    forward = np.array([[c, -s], [s, c]])
    inverse = np.array([[c, s], [-s, c]])
    e = np.eye(2)
    z_forward = np.einsum("cdzk,qr,yw->cqyzdwrk", forward, e, e).reshape(8 * n, 8 * n)
    z_inverse = np.einsum("cdkz,qr,yw->cyqkdrwz", inverse, e, e).reshape(8 * n, 8 * n)
    f4 = forward.reshape(2, 2, n // 2, 2, n)
    y_forward = f4.transpose(1, 4, 0, 3, 2).reshape(2 * n, 2 * n)
    i4 = inverse.reshape(2, 2, n, n // 2, 2)
    y_inverse = i4.transpose(1, 4, 3, 0, 2).reshape(2 * n, 2 * n)
    x_forward = forward.transpose(1, 3, 0, 2).reshape(2 * n, 2 * n)
    x_inverse = inverse.transpose(1, 3, 0, 2).reshape(2 * n, 2 * n)
    named = (z_forward, y_forward, x_forward, x_inverse, y_inverse, z_inverse)
    return [split_table(t) for t in named]


def dot(a, b):
    return jnp.dot(a, b, preferred_element_type=jnp.float32)


def halves(x):
    high = x.astype(jnp.bfloat16)
    return high, (x - high.astype(jnp.float32)).astype(jnp.bfloat16)


def left(th, tl, x):
    xh, xl = halves(x)
    return dot(th[...], xh) + (dot(tl[...], xh) + dot(th[...], xl))


def right(x, th, tl):
    xh, xl = halves(x)
    return dot(xh, th[...]) + (dot(xh, tl[...]) + dot(xl, th[...]))


def whole_spec(table):
    return pl.BlockSpec(table.shape, lambda *_: (0,) * table.ndim)


def orbital_specs(group, bx, rows, lanes):
    def spec(which, p):
        return pl.BlockSpec(
            (1, bx, rows, lanes), lambda i, *s: (s[which][group * GROUP + p], i, 0, 0)
        )

    return [spec(0, p) for p in range(GROUP)] + [spec(1, p) for p in range(GROUP)]


def forward_planes(group, scalars, flat, tables, parts):
    _, planes, rows, lanes = flat.shape
    n = lanes // 2
    width = n // parts
    bx = BLOCK_PLANES

    def body(*refs):
        refs = refs[len(scalars):]
        leads, seconds = refs[:GROUP], refs[GROUP : 2 * GROUP]
        zh, zl, yh, yl, out = refs[2 * GROUP :]
        rho = [(a[0] * b[0]).reshape(bx * rows, lanes) for a, b in zip(leads, seconds)]
        z = right(jnp.concatenate(rho, axis=1), zh, zl)
        cols = [
            jnp.concatenate(
                [z[x * rows : (x + 1) * rows, i * lanes : (i + 1) * lanes] for i in range(4)],
                axis=0,
            )
            for x in range(bx)
        ]
        y = left(yh, yl, jnp.concatenate(cols, axis=1))
        stacked = jnp.stack([y[:, x * lanes : (x + 1) * lanes] for x in range(bx)], axis=0)
        turned = jnp.swapaxes(stacked, 0, 1)
        for d in range(parts):
            for c in range(2):
                start = c * n + d * width
                out[d, c] = turned[start : start + width]

    ops = [*tables[0], *tables[1]]
    return pl.pallas_call(
        body,
        grid_spec=pltpu.PrefetchScalarGridSpec(
            num_scalar_prefetch=len(scalars),
            grid=(planes // bx,),
            in_specs=orbital_specs(group, bx, rows, lanes) + [whole_spec(t) for t in ops],
            out_specs=pl.BlockSpec((parts, 2, width, bx, lanes), lambda i, *_: (0, 0, 0, i, 0)),
        ),
        out_shape=jax.ShapeDtypeStruct((parts, 2, width, planes, lanes), jnp.float32),
        name=f"forward_planes_{group}",
    )(*scalars, *([flat] * (2 * GROUP)), *ops)


def solve_columns(group, columns, kernel, tables):
    parts, _, width, planes, lanes = columns.shape
    n = parts * planes
    bk = BLOCK_PLANES

    def body(data, kern, fh, fl, ih, il, out):
        cols = []
        for k in range(bk):
            pieces = [data[d, c, k] for c in range(2) for d in range(parts)]
            cols.append(jnp.concatenate(pieces, axis=0))
        spectrum = left(fh, fl, jnp.concatenate(cols, axis=1))
        weights = jnp.concatenate([kern[k] for k in range(bk)], axis=1)
        spectrum = spectrum * jnp.concatenate([weights, weights], axis=0)
        back = left(ih, il, spectrum)
        for k in range(bk):
            for c in range(2):
                for d in range(parts):
                    start = c * n + d * planes
                    out[d, c, k] = back[start : start + planes, k * lanes : (k + 1) * lanes]

    ops = [*tables[2], *tables[3]]
    block = pl.BlockSpec((parts, 2, bk, planes, lanes), lambda i: (0, 0, i, 0, 0))
    return pl.pallas_call(
        body,
        grid=(width // bk,),
        in_specs=[block, pl.BlockSpec((bk, n, lanes), lambda i: (i, 0, 0))]
        + [whole_spec(t) for t in ops],
        out_specs=block,
        out_shape=jax.ShapeDtypeStruct(columns.shape, jnp.float32),
        name=f"solve_columns_{group}",
    )(columns, kernel, *ops)


def add_exchange(group, scalars, returned, flat, totals, tables):
    slots, planes, rows, lanes = flat.shape
    parts, _, width, _, _ = returned.shape
    bx = BLOCK_PLANES

    def body(*refs):
        first, slot, weight, cross = refs[: len(scalars)]
        refs = refs[len(scalars):]
        data = refs[0]
        leads, seconds = refs[1 : 1 + GROUP], refs[1 + GROUP : 1 + 2 * GROUP]
        yh, yl, zh, zl = refs[1 + 2 * GROUP : 5 + 2 * GROUP]
        out = refs[-1]
        pieces = [data[d, c] for c in range(2) for d in range(parts)]
        turned = jnp.swapaxes(jnp.concatenate(pieces, axis=0), 0, 1)
        y = left(yh, yl, jnp.concatenate([turned[x] for x in range(bx)], axis=1))
        lines = [
            jnp.concatenate(
                [y[i * rows : (i + 1) * rows, x * lanes : (x + 1) * lanes] for i in range(4)],
                axis=1,
            )
            for x in range(bx)
        ]
        v = right(jnp.concatenate(lines, axis=0), zh, zl)
        if totals is None:
            out[...] = jnp.zeros_like(out)
        else:
            out[...] = refs[-2][...]
        for p in range(GROUP):
            at = group * GROUP + p
            potential = v[:, p * lanes : (p + 1) * lanes].reshape(bx, rows, lanes)
            out[first[at]] += weight[at] * potential * seconds[p][0]
            out[slot[at]] += cross[at] * potential * leads[p][0]

    ops = [*tables[4], *tables[5]]
    total_spec = pl.BlockSpec((slots, bx, rows, lanes), lambda i, *_: (0, i, 0, 0))
    in_specs = [pl.BlockSpec((parts, 2, width, bx, lanes), lambda i, *_: (0, 0, 0, i, 0))]
    in_specs += orbital_specs(group, bx, rows, lanes) + [whole_spec(t) for t in ops]
    args = [*scalars, returned, *([flat] * (2 * GROUP)), *ops]
    aliases = {}
    if totals is not None:
        in_specs.append(total_spec)
        aliases = {len(args): 0}
        args.append(totals)
    return pl.pallas_call(
        body,
        grid_spec=pltpu.PrefetchScalarGridSpec(
            num_scalar_prefetch=len(scalars),
            grid=(planes // bx,),
            in_specs=in_specs,
            out_specs=total_spec,
        ),
        out_shape=jax.ShapeDtypeStruct(flat.shape, jnp.float32),
        input_output_aliases=aliases,
        name=f"add_exchange_{group}",
    )(*args)


def live_pairs(pair_mask):
    pairs = pair_table()
    count = pairs.shape[0]
    slots = -(-CAP // GROUP) * GROUP
    band = lax.axis_index("band")
    groups = lax.axis_size("band")
    rows = band * ORB_DEV + jnp.asarray(pairs[:, 0])
    cols = (band + jnp.asarray(pairs[:, 1])) % groups * ORB_DEV + jnp.asarray(pairs[:, 2])
    live = pair_mask[rows, cols]
    earlier = np.tril(np.ones((count, count), np.int32), -1)
    rank = jnp.sum(jnp.asarray(earlier) * live[None, :], axis=1)
    hot = (rank[None, :] == jnp.arange(slots, dtype=jnp.int32)[:, None]) * live[None, :]
    slot_of = pairs[:, 1] * ORB_DEV + pairs[:, 2]
    cross_of = (slot_of != pairs[:, 0]).astype(np.int32)
    first = jnp.sum(hot * jnp.asarray(pairs[:, 0])[None, :], axis=1)
    slot = jnp.sum(hot * jnp.asarray(slot_of.astype(np.int32))[None, :], axis=1)
    weight = jnp.sum(hot, axis=1).astype(jnp.float32)
    cross = jnp.sum(hot * jnp.asarray(cross_of)[None, :], axis=1).astype(jnp.float32)
    return first, slot, weight, cross


def green_kernel(n, width):
    def wave(positions):
        return jnp.where(positions < n // 2, positions, positions - n)

    ky = wave(lax.axis_index("grid") * width + jnp.arange(width, dtype=jnp.int32))
    k = wave(jnp.arange(n, dtype=jnp.int32))
    kz = wave(jnp.arange(2 * n, dtype=jnp.int32) % n)
    squared = (ky * ky)[:, None, None] + (k * k)[None, :, None] + (kz * kz)[None, None, :]
    safe = jnp.maximum(squared, 1).astype(jnp.float32)
    scale = BOX_LENGTH * BOX_LENGTH / math.pi / float(n**3)
    return jnp.where(squared > 0, scale / safe, 0.0)


def local(orbitals, pair_mask):
    orb_count, planes, cells = orbitals.shape
    n = math.isqrt(cells)
    parts = lax.axis_size("grid")
    tables = dft_tables(n)
    own = orbitals.reshape(orb_count, planes, n // 2, 2 * n)
    visits = [own] + [shifted(own, "band", -d) for d in range(1, REACH + 1)]
    flat = jnp.concatenate(visits, axis=0)
    scalars = live_pairs(pair_mask)
    kernel = green_kernel(n, n // parts)

    def exchange(block):
        return lax.all_to_all(block, "grid", split_axis=0, concat_axis=0, tiled=True)

    turns = range(-(-CAP // GROUP))
    spectra = [forward_planes(g, scalars[:2], flat, tables, parts) for g in turns]
    columns = [exchange(s) for s in spectra]
    solved = [solve_columns(g, columns[g], kernel, tables) for g in turns]
    returned = [exchange(s) for s in solved]
    totals = None
    for g in turns:
        totals = add_exchange(g, scalars, returned[g], flat, totals, tables)
    owned = totals[:orb_count]
    for d in range(1, REACH + 1):
        owned = owned + shifted(totals[d * orb_count : (d + 1) * orb_count], "band", d)
    return (-MIXING * owned).reshape(orb_count, planes, cells)


def solution(mesh):
    return jax.shard_map(
        local,
        mesh=mesh,
        in_specs=(P("band", "grid", None), P()),
        out_specs=P("band", "grid", None),
        check_vma=False,
    )
```

time: 432 us -> 206 us (0.48)
  matrix products: 105 us -> 0 us
  blocking collectives: 84.5 us -> 0 us
  local copies, waits for them, and re-layouts: 59.8 us -> 9.43 us
  Pallas kernels: 0 us -> 44.9 us
  waiting for transfers between devices: 120 us -> 101 us
  other arithmetic: 18.6 us -> 6.46 us
  starting transfers between devices: 36.4 us -> 43 us
    dot_general x36 -> x0, matrix products: 105 us -> none  [the longest x12 32.2 us: transform_axis(): jnp.einsum(formula, cosine_table, values_in, precision=EXACT_PRECISION)]
    all_to_all x3 -> x0, blocking collectives: 84.5 us -> none  [solve_poisson(): lax.all_to_all(spectrum, 'grid', split_axis=2, concat_axis=1, tiled=True)]
    pallas_call x0 -> x9, Pallas kernels: none -> 44.9 us  [the longest x3 19 us: add_exchange(): pl.pallas_call(body, grid_spec=pltpu.PrefetchScalarGridSpec(num_scalar_pr...]
    all_to_all x3 -> x6, waiting for transfers between devices: 77.1 us -> 51 us  [exchange(): lax.all_to_all(block, 'grid', split_axis=0, concat_axis=0, tiled=True)]
    gather x12 -> x1, local copies, waits for them, and re-layouts: 14.2 us -> 0.79 us  [live_pairs(): live = pair_mask[rows, cols]]
    while x37 -> x0, local copies, waits for them, and re-layouts: 12.6 us -> none
    add x6 -> x0, local copies, waits for them, and re-layouts: 12.4 us -> none  [transform_axis(): return direct_part + sweep_direction * rotate_parts(crossed_part)]
    slice x12 -> x0, other arithmetic: 10.2 us -> none  [rotate_parts(): values_in[..., half_width:]]
  transfers between devices with their start and end apart: 7 -> 10, of which waited for: 6 -> 9; matrix products, arithmetic and copies ran while one was open for 2% -> 3% of each run, Pallas kernels for 0% -> 16%
where the time goes in v1:
time: 206 us; the launch traced here: 205 us
  waiting for transfers between devices  101 us (49%)
  Pallas kernels  44.9 us (22%)
  starting transfers between devices  43 us (21%)
  local copies, waits for them, and re-layouts  9.43 us (5%)
  other arithmetic  6.46 us (3%)
    all_to_all x6, waiting for transfers between devices, exchange(): lax.all_to_all(block, 'grid', split_axis=0, concat_axis=0, tiled=True)  51 us
    ppermute x4, waiting for transfers between devices, shifted(): lax.ppermute(block, axis, [((i - distance) % count, i) for i in range(cou...  49.6 us
    ppermute x4, starting transfers between devices, shifted(): lax.ppermute(block, axis, [((i - distance) % count, i) for i in range(cou...  21.9 us
    all_to_all x6, starting transfers between devices, exchange(): lax.all_to_all(block, 'grid', split_axis=0, concat_axis=0, tiled=True)  21.1 us
    pallas_call x3, Pallas kernels, add_exchange(): pl.pallas_call(body, grid_spec=pltpu.PrefetchScalarGridSpec(num_scalar_pr...  19 us
    pallas_call x3, Pallas kernels, forward_planes(): pl.pallas_call(body, grid_spec=pltpu.PrefetchScalarGridSpec(num_scalar_pr...  15.9 us
    pallas_call x3, Pallas kernels, solve_columns(): pl.pallas_call(body, grid=(width // bk,), in_specs=[block, pl.BlockSpec((...  9.99 us
    unnamed x19, local copies, waits for them, and re-layouts  4.94 us
  transfers between devices with their start and end apart: 10, of which 9 were waited for; matrix products, arithmetic and copies ran while one was open for 3% of the time, Pallas kernels for 16%

profile of v1, /device:TPU:4, one launch (start us, length us, event | category | flops | bytes accessed | tf_op | source)
XLA Modules:
  0.0 204.5 jit_solution(3614422816079063942)
XLA Ops:
  0.0 1.3 copy.24
  1.3 0.1 collective-permute-start
  1.4 4.1 %collective-permute-start.1 = (f32[3,16,32,128]{3,2,1,0:T(8,128)S(1)}, f32[3,16,32,128]{3,2,1,0:T(8,128)}, u32[]{:S(2)}, u32[]{:S(2)}) collective-permute-start(f32[3,16,32,128]{3,2,1,0:T(8,128)S(1)} %bitcast.9), channel_id=1, source_target_pairs={{8,0},{12,4},{16,8},{20,12},{24,16},{28,20},{0,24},{4,28},{9,1},{1... | collective-permute-start | bytes 2359304 | tf_op jit(solution)/shard_map/ppermute | solution.py:22
  5.5 0.7 fusion.13
  6.2 0.0 copy-done
  6.2 0.8 gather_fusion
  7.0 0.8 multiply_reduce_fusion
  7.8 1.4 fusion.7
  9.2 0.1 constant_dynamic-update-slice_fusion.2
  9.2 13.5 %collective-permute-done = f32[3,16,32,128]{3,2,1,0:T(8,128)} collective-permute-done((f32[3,16,32,128]{3,2,1,0:T(8,128)S(1)}, f32[3,16,32,128]{3,2,1,0:T(8,128)}, u32[]{:S(2)}, u32[]{:S(2)}) %collective-permute-start) | collective-permute-done | bytes 786464 | tf_op jit(solution)/shard_map/ppermute | solution.py:22
  22.8 1.2 constant_dynamic-update-slice_fusion.1
  23.9 0.0 collective-permute-done.1
  24.0 1.2 constant_dynamic-update-slice_fusion.refs_2_.refs_3_.refs_4_.refs_5_.refs_6_.refs_7_.refs_8_.refs_9_.refs_10_.refs_11_.refs_12_
  25.2 1.4 copy-done.1
  26.6 5.3 %forward_planes_0.1 = f32[4,2,16,16,128]{4,3,2,1,0:T(8,128)} custom-call(s32[12]{0:T(128)} %get-tuple-element.8.refs_0_, s32[12]{0:T(128)} %get-tuple-element.7.refs_1_, f32[9,16,32,128]{3,2,1,0:T(8,128)} %copy-done.1, f32[9,16,32,128]{3,2,1,0:T(8,128)} %copy-done.1, f32[9,16,32,128]{3,2,1,0:T(8,128)} %copy-done.1, f32[9,16,32,128]{3,2,1,0:T(8,128)} %copy-done.1, ...), custom_call_target="tpu_custom_call" | custom-call | tf_op jit(solution)/shard_map/forward_planes_0/pallas_call | solution.py:120
  31.9 3.5 %all-to-all-start.4 = ((f32[4,2,16,16,128]{4,3,2,1,0:T(8,128)}), f32[4,2,16,16,128]{4,3,2,1,0:T(8,128)S(1)}, u32[]{:S(2)}, u32[]{:S(2)}) async-start(f32[4,2,16,16,128]{4,3,2,1,0:T(8,128)} %forward_planes_0.1), calls=%async_computation.4 | async-start | bytes 2097152 | tf_op jit(solution)/shard_map/all_to_all | solution.py:269
  35.4 5.3 %forward_planes_1.1 = f32[4,2,16,16,128]{4,3,2,1,0:T(8,128)} custom-call(s32[12]{0:T(128)} %get-tuple-element.8.refs_0_, s32[12]{0:T(128)} %get-tuple-element.7.refs_1_, f32[9,16,32,128]{3,2,1,0:T(8,128)} %copy-done.1, f32[9,16,32,128]{3,2,1,0:T(8,128)} %copy-done.1, f32[9,16,32,128]{3,2,1,0:T(8,128)} %copy-done.1, f32[9,16,32,128]{3,2,1,0:T(8,128)} %copy-done.1, ...), custom_call_target="tpu_custom_call" | custom-call | tf_op jit(solution)/shard_map/forward_planes_1/pallas_call | solution.py:120
  40.7 9.1 %all-to-all-done.4.data = f32[4,2,16,16,128]{4,3,2,1,0:T(8,128)S(1)} async-done(((f32[4,2,16,16,128]{4,3,2,1,0:T(8,128)}), f32[4,2,16,16,128]{4,3,2,1,0:T(8,128)S(1)}, u32[]{:S(2)}, u32[]{:S(2)}) %all-to-all-start.4) | async-done | bytes 1048608 | tf_op jit(solution)/shard_map/all_to_all | solution.py:269
  49.8 3.5 %all-to-all-start.2 = ((f32[4,2,16,16,128]{4,3,2,1,0:T(8,128)}), f32[4,2,16,16,128]{4,3,2,1,0:T(8,128)S(1)}, u32[]{:S(2)}, u32[]{:S(2)}) async-start(f32[4,2,16,16,128]{4,3,2,1,0:T(8,128)} %forward_planes_1.1), calls=%async_computation.2 | async-start | bytes 2097152 | tf_op jit(solution)/shard_map/all_to_all | solution.py:269
  53.3 5.3 %forward_planes_2.1 = f32[4,2,16,16,128]{4,3,2,1,0:T(8,128)} custom-call(s32[12]{0:T(128)} %get-tuple-element.8.refs_0_, s32[12]{0:T(128)} %get-tuple-element.7.refs_1_, f32[9,16,32,128]{3,2,1,0:T(8,128)} %copy-done.1, f32[9,16,32,128]{3,2,1,0:T(8,128)} %copy-done.1, f32[9,16,32,128]{3,2,1,0:T(8,128)} %copy-done.1, f32[9,16,32,128]{3,2,1,0:T(8,128)} %copy-done.1, ...), custom_call_target="tpu_custom_call" | custom-call | tf_op jit(solution)/shard_map/forward_planes_2/pallas_call | solution.py:120
  58.6 0.0 copy-done.6
  58.6 9.1 %all-to-all-done.2.data = f32[4,2,16,16,128]{4,3,2,1,0:T(8,128)S(1)} async-done(((f32[4,2,16,16,128]{4,3,2,1,0:T(8,128)}), f32[4,2,16,16,128]{4,3,2,1,0:T(8,128)S(1)}, u32[]{:S(2)}, u32[]{:S(2)}) %all-to-all-start.2) | async-done | bytes 1048608 | tf_op jit(solution)/shard_map/all_to_all | solution.py:269
  67.7 3.5 %all-to-all-start = ((f32[4,2,16,16,128]{4,3,2,1,0:T(8,128)}), f32[4,2,16,16,128]{4,3,2,1,0:T(8,128)S(1)}, u32[]{:S(2)}, u32[]{:S(2)}) async-start(f32[4,2,16,16,128]{4,3,2,1,0:T(8,128)} %forward_planes_2.1), calls=%async_computation | async-start | bytes 2097152 | tf_op jit(solution)/shard_map/all_to_all | solution.py:269
  71.3 0.1 broadcast_add_fusion
  71.3 1.0 fusion.4.kern
  72.3 3.3 %solve_columns_0.1 = f32[4,2,16,16,128]{4,3,2,1,0:T(8,128)} custom-call(f32[4,2,16,16,128]{4,3,2,1,0:T(8,128)} %copy-done.6, f32[16,64,128]{2,1,0:T(8,128)} %fusion.4.kern, bf16[128,128]{1,0:T(8,128)(2,1)} %constant.109.clone.fh, bf16[128,128]{1,0:T(8,128)(2,1)} %constant.110.clone.fl, bf16[128,128]{1,0:T(8,128)(2,1)} %constant.111.clone.ih, ...), custom_call_target="tpu_custom_call" | custom-call | tf_op jit(solution)/shard_map/solve_columns_0/pallas_call | solution.py:155
  75.7 10.0 %all-to-all-done.data = f32[4,2,16,16,128]{4,3,2,1,0:T(8,128)S(1)} async-done(((f32[4,2,16,16,128]{4,3,2,1,0:T(8,128)}), f32[4,2,16,16,128]{4,3,2,1,0:T(8,128)S(1)}, u32[]{:S(2)}, u32[]{:S(2)}) %all-to-all-start) | async-done | bytes 1048608 | tf_op jit(solution)/shard_map/all_to_all | solution.py:269
  85.6 3.5 %all-to-all-start.5 = ((f32[4,2,16,16,128]{4,3,2,1,0:T(8,128)}), f32[4,2,16,16,128]{4,3,2,1,0:T(8,128)S(1)}, u32[]{:S(2)}, u32[]{:S(2)}) async-start(f32[4,2,16,16,128]{4,3,2,1,0:T(8,128)} %solve_columns_0.1), calls=%async_computation.5 | async-start | bytes 2097152 | tf_op jit(solution)/shard_map/all_to_all | solution.py:269
  89.1 3.3 %solve_columns_1.1 = f32[4,2,16,16,128]{4,3,2,1,0:T(8,128)} custom-call(f32[4,2,16,16,128]{4,3,2,1,0:T(8,128)} %copy-done.5, f32[16,64,128]{2,1,0:T(8,128)} %fusion.4.kern, bf16[128,128]{1,0:T(8,128)(2,1)} %constant.109.clone.fh, bf16[128,128]{1,0:T(8,128)(2,1)} %constant.110.clone.fl, bf16[128,128]{1,0:T(8,128)(2,1)} %constant.111.clone.ih, ...), custom_call_target="tpu_custom_call" | custom-call | tf_op jit(solution)/shard_map/solve_columns_1/pallas_call | solution.py:155
  92.5 11.1 %all-to-all-done.5.refs_4_ = f32[4,2,16,16,128]{4,3,2,1,0:T(8,128)S(1)} async-done(((f32[4,2,16,16,128]{4,3,2,1,0:T(8,128)}), f32[4,2,16,16,128]{4,3,2,1,0:T(8,128)S(1)}, u32[]{:S(2)}, u32[]{:S(2)}) %all-to-all-start.5) | async-done | bytes 1048608 | tf_op jit(solution)/shard_map/all_to_all | solution.py:269
  103.5 3.5 %all-to-all-start.3 = ((f32[4,2,16,16,128]{4,3,2,1,0:T(8,128)}), f32[4,2,16,16,128]{4,3,2,1,0:T(8,128)S(1)}, u32[]{:S(2)}, u32[]{:S(2)}) async-start(f32[4,2,16,16,128]{4,3,2,1,0:T(8,128)} %solve_columns_1.1), calls=%async_computation.3 | async-start | bytes 2097152 | tf_op jit(solution)/shard_map/all_to_all | solution.py:269
  107.1 3.3 %solve_columns_2.1 = f32[4,2,16,16,128]{4,3,2,1,0:T(8,128)} custom-call(f32[4,2,16,16,128]{4,3,2,1,0:T(8,128)} %copy-done.7, f32[16,64,128]{2,1,0:T(8,128)} %fusion.4.kern, bf16[128,128]{1,0:T(8,128)(2,1)} %constant.109.clone.fh, bf16[128,128]{1,0:T(8,128)(2,1)} %constant.110.clone.fl, bf16[128,128]{1,0:T(8,128)(2,1)} %constant.111.clone.ih, ...), custom_call_target="tpu_custom_call" | custom-call | tf_op jit(solution)/shard_map/solve_columns_2/pallas_call | solution.py:155
  110.4 11.1 %all-to-all-done.3.refs_4_ = f32[4,2,16,16,128]{4,3,2,1,0:T(8,128)S(1)} async-done(((f32[4,2,16,16,128]{4,3,2,1,0:T(8,128)}), f32[4,2,16,16,128]{4,3,2,1,0:T(8,128)S(1)}, u32[]{:S(2)}, u32[]{:S(2)}) %all-to-all-start.3) | async-done | bytes 1048608 | tf_op jit(solution)/shard_map/all_to_all | solution.py:269
  121.5 3.5 %all-to-all-start.1 = ((f32[4,2,16,16,128]{4,3,2,1,0:T(8,128)}), f32[4,2,16,16,128]{4,3,2,1,0:T(8,128)S(1)}, u32[]{:S(2)}, u32[]{:S(2)}) async-start(f32[4,2,16,16,128]{4,3,2,1,0:T(8,128)} %solve_columns_2.1), calls=%async_computation.1 | async-start | bytes 2097152 | tf_op jit(solution)/shard_map/all_to_all | solution.py:269
  125.0 0.5 convert_element_type.10.refs_2_
  125.5 0.5 convert_element_type.11.refs_3_
  126.0 6.2 %add_exchange_0.1.refs_17_ = f32[9,16,32,128]{3,2,1,0:T(8,128)} custom-call(s32[12]{0:T(128)} %get-tuple-element.8.refs_0_, s32[12]{0:T(128)} %get-tuple-element.7.refs_1_, f32[12]{0:T(128)} %convert_element_type.10.refs_2_, f32[12]{0:T(128)} %convert_element_type.11.refs_3_, f32[4,2,16,16,128]{4,3,2,1,0:T(8,128)} %copy-done.2, ...), custom_call_target="tpu_custom_call" | custom-call | tf_op jit(solution)/shard_map/add_exchange_0/pallas_call | solution.py:209
  132.2 6.4 %add_exchange_1.1.refs_17_ = f32[9,16,32,128]{3,2,1,0:T(8,128)} custom-call(s32[12]{0:T(128)} %get-tuple-element.8.refs_0_, s32[12]{0:T(128)} %get-tuple-element.7.refs_1_, f32[12]{0:T(128)} %convert_element_type.10.refs_2_, f32[12]{0:T(128)} %convert_element_type.11.refs_3_, f32[4,2,16,16,128]{4,3,2,1,0:T(8,128)} %copy-done.3, ...), custom_call_target="tpu_custom_call", output_to_operand_aliasing={{}: (17, {})} | custom-call | tf_op jit(solution)/shard_map/add_exchange_1/pallas_call | solution.py:209
  138.6 0.8 all-to-all-done.1.refs_4_
  139.4 1.0 copy-done.4
  140.4 6.4 %add_exchange_2.1 = f32[9,16,32,128]{3,2,1,0:T(8,128)} custom-call(s32[12]{0:T(128)} %get-tuple-element.8.refs_0_, s32[12]{0:T(128)} %get-tuple-element.7.refs_1_, f32[12]{0:T(128)} %convert_element_type.10.refs_2_, f32[12]{0:T(128)} %convert_element_type.11.refs_3_, f32[4,2,16,16,128]{4,3,2,1,0:T(8,128)} %copy-done.4, ...), custom_call_target="tpu_custom_call", output_to_operand_aliasing={{}: (17, {})} | custom-call | tf_op jit(solution)/shard_map/add_exchange_2/pallas_call | solution.py:209
  146.8 1.5 fusion.19
  148.3 16.4 %collective-permute-start.2 = (f32[3,16,32,128]{3,2,1,0:T(8,128)S(1)}, f32[3,16,32,128]{3,2,1,0:T(8,128)S(1)}, u32[]{:S(2)}, u32[]{:S(2)}) collective-permute-start(f32[3,16,32,128]{3,2,1,0:T(8,128)S(1)} %get-tuple-element.9), channel_id=1, source_target_pairs={{28,0},{0,4},{4,8},{8,12},{12,16},{16,20},{20,24},{24,28},{29,1},{... | collective-permute-start | bytes 2359304 | tf_op jit(solution)/shard_map/ppermute | solution.py:22
  164.6 1.4 collective-permute-start.3
  166.0 16.6 %collective-permute-done.2 = f32[3,16,32,128]{3,2,1,0:T(8,128)S(1)} collective-permute-done((f32[3,16,32,128]{3,2,1,0:T(8,128)S(1)}, f32[3,16,32,128]{3,2,1,0:T(8,128)S(1)}, u32[]{:S(2)}, u32[]{:S(2)}) %collective-permute-start.2) | collective-permute-done | bytes 786464 | tf_op jit(solution)/shard_map/ppermute | solution.py:22
  182.6 19.5 %collective-permute-done.3 = f32[3,16,32,128]{3,2,1,0:T(8,128)S(1)} collective-permute-done((f32[3,16,32,128]{3,2,1,0:T(8,128)S(1)}, f32[3,16,32,128]{3,2,1,0:T(8,128)S(1)}, u32[]{:S(2)}, u32[]{:S(2)}) %collective-permute-start.3) | collective-permute-done | bytes 786464 | tf_op jit(solution)/shard_map/ppermute | solution.py:22
  202.1 1.4 fusion.1
  203.5 1.0 reshape.74
  (15 shorter events, 0.0 us)
Async XLA Ops:
  0.0 6.2 %copy-start = (s32[24,24]{1,0:T(8,128)S(1)}, s32[24,24]{1,0:T(8,128)}, u32[]{:S(2)}) copy-start(s32[24,24]{1,0:T(8,128)} %param.22) | copy-start | bytes 6916
  1.3 21.5 %collective-permute-start = (f32[3,16,32,128]{3,2,1,0:T(8,128)S(1)}, f32[3,16,32,128]{3,2,1,0:T(8,128)}, u32[]{:S(2)}, u32[]{:S(2)}) collective-permute-start(f32[3,16,32,128]{3,2,1,0:T(8,128)S(1)} %bitcast.8), channel_id=1, source_target_pairs={{4,0},{8,4},{12,8},{16,12},{20,16},{24,20},{28,24},{0,28},{5,1},{9... | collective-permute-start | bytes 2359304 | tf_op jit(solution)/shard_map/ppermute | solution.py:22
  1.4 22.6 %collective-permute-start.1 = (f32[3,16,32,128]{3,2,1,0:T(8,128)S(1)}, f32[3,16,32,128]{3,2,1,0:T(8,128)}, u32[]{:S(2)}, u32[]{:S(2)}) collective-permute-start(f32[3,16,32,128]{3,2,1,0:T(8,128)S(1)} %bitcast.9), channel_id=1, source_target_pairs={{8,0},{12,4},{16,8},{20,12},{24,16},{28,20},{0,24},{4,28},{9,1},{1... | collective-permute-start | bytes 2359304 | tf_op jit(solution)/shard_map/ppermute | solution.py:22
  25.1 1.4 copy-start.1
  31.9 17.9 %all-to-all-start.4 = ((f32[4,2,16,16,128]{4,3,2,1,0:T(8,128)}), f32[4,2,16,16,128]{4,3,2,1,0:T(8,128)S(1)}, u32[]{:S(2)}, u32[]{:S(2)}) async-start(f32[4,2,16,16,128]{4,3,2,1,0:T(8,128)} %forward_planes_0.1), calls=%async_computation.4 | async-start | bytes 2097152 | tf_op jit(solution)/shard_map/all_to_all | solution.py:269
  49.8 8.8 %copy-start.6 = (f32[4,2,16,16,128]{4,3,2,1,0:T(8,128)}, f32[4,2,16,16,128]{4,3,2,1,0:T(8,128)S(1)}, u32[]{:S(2)}) copy-start(f32[4,2,16,16,128]{4,3,2,1,0:T(8,128)S(1)} %all-to-all-done.4.data) | copy-start | bytes 3145732
  49.8 17.9 %all-to-all-start.2 = ((f32[4,2,16,16,128]{4,3,2,1,0:T(8,128)}), f32[4,2,16,16,128]{4,3,2,1,0:T(8,128)S(1)}, u32[]{:S(2)}, u32[]{:S(2)}) async-start(f32[4,2,16,16,128]{4,3,2,1,0:T(8,128)} %forward_planes_1.1), calls=%async_computation.2 | async-start | bytes 2097152 | tf_op jit(solution)/shard_map/all_to_all | solution.py:269
  67.7 8.0 %copy-start.5 = (f32[4,2,16,16,128]{4,3,2,1,0:T(8,128)}, f32[4,2,16,16,128]{4,3,2,1,0:T(8,128)S(1)}, u32[]{:S(2)}) copy-start(f32[4,2,16,16,128]{4,3,2,1,0:T(8,128)S(1)} %all-to-all-done.2.data) | copy-start | bytes 3145732
  67.7 17.9 %all-to-all-start = ((f32[4,2,16,16,128]{4,3,2,1,0:T(8,128)}), f32[4,2,16,16,128]{4,3,2,1,0:T(8,128)S(1)}, u32[]{:S(2)}, u32[]{:S(2)}) async-start(f32[4,2,16,16,128]{4,3,2,1,0:T(8,128)} %forward_planes_2.1), calls=%async_computation | async-start | bytes 2097152 | tf_op jit(solution)/shard_map/all_to_all | solution.py:269
  85.6 6.9 %copy-start.7 = (f32[4,2,16,16,128]{4,3,2,1,0:T(8,128)}, f32[4,2,16,16,128]{4,3,2,1,0:T(8,128)S(1)}, u32[]{:S(2)}) copy-start(f32[4,2,16,16,128]{4,3,2,1,0:T(8,128)S(1)} %all-to-all-done.data) | copy-start | bytes 3145732
  85.6 17.9 %all-to-all-start.5 = ((f32[4,2,16,16,128]{4,3,2,1,0:T(8,128)}), f32[4,2,16,16,128]{4,3,2,1,0:T(8,128)S(1)}, u32[]{:S(2)}, u32[]{:S(2)}) async-start(f32[4,2,16,16,128]{4,3,2,1,0:T(8,128)} %solve_columns_0.1), calls=%async_computation.5 | async-start | bytes 2097152 | tf_op jit(solution)/shard_map/all_to_all | solution.py:269
  103.5 6.9 %copy-start.2 = (f32[4,2,16,16,128]{4,3,2,1,0:T(8,128)}, f32[4,2,16,16,128]{4,3,2,1,0:T(8,128)S(1)}, u32[]{:S(2)}) copy-start(f32[4,2,16,16,128]{4,3,2,1,0:T(8,128)S(1)} %all-to-all-done.5.refs_4_) | copy-start | bytes 3145732
  103.5 17.9 %all-to-all-start.3 = ((f32[4,2,16,16,128]{4,3,2,1,0:T(8,128)}), f32[4,2,16,16,128]{4,3,2,1,0:T(8,128)S(1)}, u32[]{:S(2)}, u32[]{:S(2)}) async-start(f32[4,2,16,16,128]{4,3,2,1,0:T(8,128)} %solve_columns_1.1), calls=%async_computation.3 | async-start | bytes 2097152 | tf_op jit(solution)/shard_map/all_to_all | solution.py:269
  121.5 10.7 %copy-start.3 = (f32[4,2,16,16,128]{4,3,2,1,0:T(8,128)}, f32[4,2,16,16,128]{4,3,2,1,0:T(8,128)S(1)}, u32[]{:S(2)}) copy-start(f32[4,2,16,16,128]{4,3,2,1,0:T(8,128)S(1)} %all-to-all-done.3.refs_4_) | copy-start | bytes 3145732
  121.5 17.9 %all-to-all-start.1 = ((f32[4,2,16,16,128]{4,3,2,1,0:T(8,128)}), f32[4,2,16,16,128]{4,3,2,1,0:T(8,128)S(1)}, u32[]{:S(2)}, u32[]{:S(2)}) async-start(f32[4,2,16,16,128]{4,3,2,1,0:T(8,128)} %solve_columns_2.1), calls=%async_computation.1 | async-start | bytes 2097152 | tf_op jit(solution)/shard_map/all_to_all | solution.py:269
  139.4 1.0 copy-start.4
  148.3 34.3 %collective-permute-start.2 = (f32[3,16,32,128]{3,2,1,0:T(8,128)S(1)}, f32[3,16,32,128]{3,2,1,0:T(8,128)S(1)}, u32[]{:S(2)}, u32[]{:S(2)}) collective-permute-start(f32[3,16,32,128]{3,2,1,0:T(8,128)S(1)} %get-tuple-element.9), channel_id=1, source_target_pairs={{28,0},{0,4},{4,8},{8,12},{12,16},{16,20},{20,24},{24,28},{29,1},{... | collective-permute-start | bytes 2359304 | tf_op jit(solution)/shard_map/ppermute | solution.py:22
  164.6 37.4 %collective-permute-start.3 = (f32[3,16,32,128]{3,2,1,0:T(8,128)S(1)}, f32[3,16,32,128]{3,2,1,0:T(8,128)S(1)}, u32[]{:S(2)}, u32[]{:S(2)}) collective-permute-start(f32[3,16,32,128]{3,2,1,0:T(8,128)S(1)} %get-tuple-element.10), channel_id=1, source_target_pairs={{24,0},{28,4},{0,8},{4,12},{8,16},{12,20},{16,24},{20,28},{25,1},{... | collective-permute-start | bytes 2359304 | tf_op jit(solution)/shard_map/ppermute | solution.py:22

commit v2 on v1

--- a/solution.py
+++ b/solution.py
@@ -38,7 +38,21 @@
     return jnp.asarray(high), jnp.asarray(low)
 
 
-def dft_tables(n):
+def peer_order(parts):
+    power = parts & (parts - 1) == 0
+    return [[m ^ s if power else (m + s) % parts for s in range(parts)] for m in range(parts)]
+
+
+def block_order(table, parts, side):
+    n = table.shape[0] // 2
+    stacked = []
+    for order in peer_order(parts):
+        index = np.arange(2 * n).reshape(2, parts, n // parts)[:, order].reshape(-1)
+        stacked.append(table[index] if side == 0 else table[:, index])
+    return np.stack(stacked)
+
+
+def dft_tables(n, parts):
     k = np.arange(n)
     angles = (k[:, None] * k[None, :] % n) * (2.0 * math.pi / n)
     c, s = np.cos(angles), np.sin(angles)
@@ -46,14 +60,17 @@
     inverse = np.array([[c, s], [-s, c]])
     e = np.eye(2)
     z_forward = np.einsum("cdzk,qr,yw->cqyzdwrk", forward, e, e).reshape(8 * n, 8 * n)
-    z_inverse = np.einsum("cdkz,qr,yw->cyqkdrwz", inverse, e, e).reshape(8 * n, 8 * n)
     f4 = forward.reshape(2, 2, n // 2, 2, n)
     y_forward = f4.transpose(1, 4, 0, 3, 2).reshape(2 * n, 2 * n)
     i4 = inverse.reshape(2, 2, n, n // 2, 2)
     y_inverse = i4.transpose(1, 4, 3, 0, 2).reshape(2 * n, 2 * n)
     x_forward = forward.transpose(1, 3, 0, 2).reshape(2 * n, 2 * n)
     x_inverse = inverse.transpose(1, 3, 0, 2).reshape(2 * n, 2 * n)
-    named = (z_forward, y_forward, x_forward, x_inverse, y_inverse, z_inverse)
+    y_forward = block_order(y_forward, parts, 0)
+    x_forward = block_order(x_forward, parts, 1)
+    x_inverse = block_order(x_inverse, parts, 0)
+    y_inverse = block_order(y_inverse, parts, 1)
+    named = (z_forward, y_forward, x_forward, x_inverse, y_inverse)
     return [split_table(t) for t in named]
 
 
@@ -76,14 +93,24 @@
     return dot(xh, th[...]) + (dot(xh, tl[...]) + dot(xl, th[...]))
 
 
-def whole_spec(table):
-    return pl.BlockSpec(table.shape, lambda *_: (0,) * table.ndim)
+def right_transposed(x, th, tl):
+    def dot_t(a, b):
+        return lax.dot_general(a, b, (((1,), (1,)), ((), ())), preferred_element_type=jnp.float32)
+
+    xh, xl = halves(x)
+    return dot_t(xh, th[...]) + (dot_t(xh, tl[...]) + dot_t(xl, th[...]))
+
+
+def table_spec(table):
+    if table.ndim == 2:
+        return pl.BlockSpec(table.shape, lambda *_: (0, 0))
+    return pl.BlockSpec((pl.squeezed, *table.shape[1:]), lambda i, me, *_: (me[0], 0, 0))
 
 
 def orbital_specs(group, bx, rows, lanes):
     def spec(which, p):
         return pl.BlockSpec(
-            (1, bx, rows, lanes), lambda i, *s: (s[which][group * GROUP + p], i, 0, 0)
+            (1, bx, rows, lanes), lambda i, *s: (s[which + 1][group * GROUP + p], i, 0, 0)
         )
 
     return [spec(0, p) for p in range(GROUP)] + [spec(1, p) for p in range(GROUP)]
@@ -98,7 +125,8 @@
     def body(*refs):
         refs = refs[len(scalars):]
         leads, seconds = refs[:GROUP], refs[GROUP : 2 * GROUP]
-        zh, zl, yh, yl, out = refs[2 * GROUP :]
+        zh, zl, yh, yl = refs[2 * GROUP : 2 * GROUP + 4]
+        outs = refs[2 * GROUP + 4 :]
         rho = [(a[0] * b[0]).reshape(bx * rows, lanes) for a, b in zip(leads, seconds)]
         z = right(jnp.concatenate(rho, axis=1), zh, zl)
         cols = [
@@ -114,7 +142,7 @@
         for d in range(parts):
             for c in range(2):
                 start = c * n + d * width
-                out[d, c] = turned[start : start + width]
+                outs[d][c] = turned[start : start + width]
 
     ops = [*tables[0], *tables[1]]
     return pl.pallas_call(
@@ -122,23 +150,26 @@
         grid_spec=pltpu.PrefetchScalarGridSpec(
             num_scalar_prefetch=len(scalars),
             grid=(planes // bx,),
-            in_specs=orbital_specs(group, bx, rows, lanes) + [whole_spec(t) for t in ops],
-            out_specs=pl.BlockSpec((parts, 2, width, bx, lanes), lambda i, *_: (0, 0, 0, i, 0)),
+            in_specs=orbital_specs(group, bx, rows, lanes) + [table_spec(t) for t in ops],
+            out_specs=[pl.BlockSpec((2, width, bx, lanes), lambda i, *_: (0, 0, i, 0))] * parts,
         ),
-        out_shape=jax.ShapeDtypeStruct((parts, 2, width, planes, lanes), jnp.float32),
+        out_shape=[jax.ShapeDtypeStruct((2, width, planes, lanes), jnp.float32)] * parts,
         name=f"forward_planes_{group}",
     )(*scalars, *([flat] * (2 * GROUP)), *ops)
 
 
-def solve_columns(group, columns, kernel, tables):
-    parts, _, width, planes, lanes = columns.shape
+def solve_columns(group, me, columns, kernel, tables):
+    parts = len(columns)
+    _, width, planes, lanes = columns[0].shape
     n = parts * planes
     bk = BLOCK_PLANES
 
-    def body(data, kern, fh, fl, ih, il, out):
+    def body(_, *refs):
+        data, outs = refs[:parts], refs[parts + 5 :]
+        kern, fh, fl, ih, il = refs[parts : parts + 5]
         cols = []
         for k in range(bk):
-            pieces = [data[d, c, k] for c in range(2) for d in range(parts)]
+            pieces = [data[d][c, k] for c in range(2) for d in range(parts)]
             cols.append(jnp.concatenate(pieces, axis=0))
         spectrum = left(fh, fl, jnp.concatenate(cols, axis=1))
         weights = jnp.concatenate([kern[k] for k in range(bk)], axis=1)
@@ -148,34 +179,39 @@
             for c in range(2):
                 for d in range(parts):
                     start = c * n + d * planes
-                    out[d, c, k] = back[start : start + planes, k * lanes : (k + 1) * lanes]
+                    outs[d][c, k] = back[start : start + planes, k * lanes : (k + 1) * lanes]
 
     ops = [*tables[2], *tables[3]]
-    block = pl.BlockSpec((parts, 2, bk, planes, lanes), lambda i: (0, 0, i, 0, 0))
+    block = pl.BlockSpec((2, bk, planes, lanes), lambda i, *_: (0, i, 0, 0))
     return pl.pallas_call(
         body,
-        grid=(width // bk,),
-        in_specs=[block, pl.BlockSpec((bk, n, lanes), lambda i: (i, 0, 0))]
-        + [whole_spec(t) for t in ops],
-        out_specs=block,
-        out_shape=jax.ShapeDtypeStruct(columns.shape, jnp.float32),
+        grid_spec=pltpu.PrefetchScalarGridSpec(
+            num_scalar_prefetch=1,
+            grid=(width // bk,),
+            in_specs=[block] * parts
+            + [pl.BlockSpec((bk, n, lanes), lambda i, *_: (i, 0, 0))]
+            + [table_spec(t) for t in ops],
+            out_specs=[block] * parts,
+        ),
+        out_shape=[jax.ShapeDtypeStruct(columns[0].shape, jnp.float32)] * parts,
         name=f"solve_columns_{group}",
-    )(columns, kernel, *ops)
+    )(me, *columns, kernel, *ops)
 
 
 def add_exchange(group, scalars, returned, flat, totals, tables):
     slots, planes, rows, lanes = flat.shape
-    parts, _, width, _, _ = returned.shape
+    parts = len(returned)
+    width = returned[0].shape[1]
     bx = BLOCK_PLANES
 
     def body(*refs):
-        first, slot, weight, cross = refs[: len(scalars)]
+        _, first, slot, weight, cross = refs[: len(scalars)]
         refs = refs[len(scalars):]
-        data = refs[0]
-        leads, seconds = refs[1 : 1 + GROUP], refs[1 + GROUP : 1 + 2 * GROUP]
-        yh, yl, zh, zl = refs[1 + 2 * GROUP : 5 + 2 * GROUP]
+        data, refs = refs[:parts], refs[parts:]
+        leads, seconds = refs[:GROUP], refs[GROUP : 2 * GROUP]
+        yh, yl, zh, zl = refs[2 * GROUP : 2 * GROUP + 4]
         out = refs[-1]
-        pieces = [data[d, c] for c in range(2) for d in range(parts)]
+        pieces = [data[d][c] for c in range(2) for d in range(parts)]
         turned = jnp.swapaxes(jnp.concatenate(pieces, axis=0), 0, 1)
         y = left(yh, yl, jnp.concatenate([turned[x] for x in range(bx)], axis=1))
         lines = [
@@ -185,7 +221,7 @@
             )
             for x in range(bx)
         ]
-        v = right(jnp.concatenate(lines, axis=0), zh, zl)
+        v = right_transposed(jnp.concatenate(lines, axis=0), zh, zl)
         if totals is None:
             out[...] = jnp.zeros_like(out)
         else:
@@ -196,11 +232,11 @@
             out[first[at]] += weight[at] * potential * seconds[p][0]
             out[slot[at]] += cross[at] * potential * leads[p][0]
 
-    ops = [*tables[4], *tables[5]]
+    ops = [*tables[4], *tables[0]]
     total_spec = pl.BlockSpec((slots, bx, rows, lanes), lambda i, *_: (0, i, 0, 0))
-    in_specs = [pl.BlockSpec((parts, 2, width, bx, lanes), lambda i, *_: (0, 0, 0, i, 0))]
-    in_specs += orbital_specs(group, bx, rows, lanes) + [whole_spec(t) for t in ops]
-    args = [*scalars, returned, *([flat] * (2 * GROUP)), *ops]
+    in_specs = [pl.BlockSpec((2, width, bx, lanes), lambda i, *_: (0, 0, i, 0))] * parts
+    in_specs += orbital_specs(group, bx, rows, lanes) + [table_spec(t) for t in ops]
+    args = [*scalars, *returned, *([flat] * (2 * GROUP)), *ops]
     aliases = {}
     if totals is not None:
         in_specs.append(total_spec)
@@ -258,20 +294,28 @@
     orb_count, planes, cells = orbitals.shape
     n = math.isqrt(cells)
     parts = lax.axis_size("grid")
-    tables = dft_tables(n)
+    tables = dft_tables(n, parts)
     own = orbitals.reshape(orb_count, planes, n // 2, 2 * n)
     visits = [own] + [shifted(own, "band", -d) for d in range(1, REACH + 1)]
     flat = jnp.concatenate(visits, axis=0)
-    scalars = live_pairs(pair_mask)
+    me = lax.axis_index("grid").astype(jnp.int32).reshape(1)
+    scalars = (me, *live_pairs(pair_mask))
     kernel = green_kernel(n, n // parts)
 
-    def exchange(block):
-        return lax.all_to_all(block, "grid", split_axis=0, concat_axis=0, tiled=True)
+    order = peer_order(parts)
+
+    def exchange(blocks):
+        moved = [blocks[0]]
+        for s in range(1, parts):
+            back = order[order[0][s]].index(0)
+            route = [(order[m][s], m) for m in range(parts)]
+            moved.append(lax.ppermute(blocks[back], "grid", route))
+        return moved
 
     turns = range(-(-CAP // GROUP))
-    spectra = [forward_planes(g, scalars[:2], flat, tables, parts) for g in turns]
+    spectra = [forward_planes(g, scalars[:3], flat, tables, parts) for g in turns]
     columns = [exchange(s) for s in spectra]
-    solved = [solve_columns(g, columns[g], kernel, tables) for g in turns]
+    solved = [solve_columns(g, me, columns[g], kernel, tables) for g in turns]
     returned = [exchange(s) for s in solved]
     totals = None
     for g in turns:

time: 206 us -> 170 us (0.83)
  waiting for transfers between devices: 101 us -> 70.7 us
  starting transfers between devices: 43 us -> 35.9 us
    all_to_all x6 -> x0, waiting for transfers between devices: 51 us -> none  [exchange(): lax.all_to_all(block, 'grid', split_axis=0, concat_axis=0, tiled=True)]
    all_to_all x6 -> x0, starting transfers between devices: 21.1 us -> none  [exchange(): lax.all_to_all(block, 'grid', split_axis=0, concat_axis=0, tiled=True)]
    ppermute x0 -> x18, waiting for transfers between devices: none -> 20.7 us  [exchange(): moved.append(lax.ppermute(blocks[back], 'grid', route))]
    ppermute x0 -> x18, starting transfers between devices: none -> 14 us  [exchange(): moved.append(lax.ppermute(blocks[back], 'grid', route))]
    unnamed x19 -> x51, local copies, waits for them, and re-layouts: 4.94 us -> 5.39 us
  transfers between devices with their start and end apart: 10 -> 22, of which waited for: 9 -> 10; matrix products, arithmetic and copies ran while one was open for 3% -> 4% of each run, Pallas kernels for 16% -> 20%
where the time goes in v2:
time: 170 us
  waiting for transfers between devices  70.7 us (42%)
  Pallas kernels  46.8 us (28%)
  starting transfers between devices  35.9 us (21%)
  local copies, waits for them, and re-layouts  9.88 us (6%)
  other arithmetic  6.47 us (4%)
    ppermute x4, waiting for transfers between devices, shifted(): lax.ppermute(block, axis, [((i - distance) % count, i) for i in range(cou...  50 us
    ppermute x4, starting transfers between devices, shifted(): lax.ppermute(block, axis, [((i - distance) % count, i) for i in range(cou...  21.9 us
    ppermute x18, waiting for transfers between devices, exchange(): moved.append(lax.ppermute(blocks[back], 'grid', route))  20.7 us
    pallas_call x3, Pallas kernels, add_exchange(): pl.pallas_call(body, grid_spec=pltpu.PrefetchScalarGridSpec(num_scalar_pr...  19.7 us
    pallas_call x3, Pallas kernels, forward_planes(): pl.pallas_call(body, grid_spec=pltpu.PrefetchScalarGridSpec(num_scalar_pr...  16.6 us
    ppermute x18, starting transfers between devices, exchange(): moved.append(lax.ppermute(blocks[back], 'grid', route))  14 us
    pallas_call x3, Pallas kernels, solve_columns(): pl.pallas_call(body, grid_spec=pltpu.PrefetchScalarGridSpec(num_scalar_pr...  10.5 us
    unnamed x51, local copies, waits for them, and re-layouts  5.39 us
  transfers between devices with their start and end apart: 22, of which 10 were waited for; matrix products, arithmetic and copies ran while one was open for 4% of the time, Pallas kernels for 20%

profile of v2, /device:TPU:4, one launch (start us, length us, event | category | flops | bytes accessed | tf_op | source)
XLA Modules:
  0.0 170.0 jit_solution(2125284167929951883)
XLA Ops:
  0.0 1.3 copy.22
  1.4 4.1 %collective-permute-start.1 = (f32[3,16,32,128]{3,2,1,0:T(8,128)S(1)}, f32[3,16,32,128]{3,2,1,0:T(8,128)}, u32[]{:S(2)}, u32[]{:S(2)}) collective-permute-start(f32[3,16,32,128]{3,2,1,0:T(8,128)S(1)} %bitcast.10), channel_id=1, source_target_pairs={{8,0},{12,4},{16,8},{20,12},{24,16},{28,20},{0,24},{4,28},{9,1},{1... | collective-permute-start | bytes 2359304 | tf_op jit(solution)/shard_map/ppermute | solution.py:22
  5.5 0.7 fusion.13
  6.2 0.8 gather_fusion
  7.0 0.8 multiply_reduce_fusion
  7.8 1.4 fusion.7
  9.2 13.5 %collective-permute-done = f32[3,16,32,128]{3,2,1,0:T(8,128)} collective-permute-done((f32[3,16,32,128]{3,2,1,0:T(8,128)S(1)}, f32[3,16,32,128]{3,2,1,0:T(8,128)}, u32[]{:S(2)}, u32[]{:S(2)}) %collective-permute-start) | collective-permute-done | bytes 786464 | tf_op jit(solution)/shard_map/ppermute | solution.py:22
  22.8 1.2 constant_dynamic-update-slice_fusion.1
  24.0 1.2 constant_dynamic-update-slice_fusion.refs_3_.refs_4_.refs_5_.refs_6_.refs_7_.refs_8_.refs_9_.refs_10_.refs_11_.refs_12_.refs_13_.refs_14_.refs_15_.refs_16_
  25.2 1.4 copy-done.1
  26.6 5.3 %forward_planes_0.1 = (f32[2,16,16,128]{3,2,1,0:T(8,128)}, f32[2,16,16,128]{3,2,1,0:T(8,128)}, f32[2,16,16,128]{3,2,1,0:T(8,128)}, f32[2,16,16,128]{3,2,1,0:T(8,128)}) custom-call(s32[1]{0:T(128)} %bitcast.refs_0_._, s32[12]{0:T(128)} %get-tuple-element.56.refs_1_, s32[12]{0:T(128)} %get-tuple-element.55.refs_2_, f32[9,16,32,128]{3,2,1,0:T(8,128)} %copy-done.1, ...), custom_call_target="tpu_custom_call" | custom-call | tf_op jit(solution)/shard_map/forward_planes_0/pallas_call | solution.py:148
  32.0 1.5 collective-permute-start.15
  33.9 5.3 %forward_planes_1.1 = (f32[2,16,16,128]{3,2,1,0:T(8,128)}, f32[2,16,16,128]{3,2,1,0:T(8,128)}, f32[2,16,16,128]{3,2,1,0:T(8,128)}, f32[2,16,16,128]{3,2,1,0:T(8,128)}) custom-call(s32[1]{0:T(128)} %bitcast.refs_0_._, s32[12]{0:T(128)} %get-tuple-element.56.refs_1_, s32[12]{0:T(128)} %get-tuple-element.55.refs_2_, f32[9,16,32,128]{3,2,1,0:T(8,128)} %copy-done.1, ...), custom_call_target="tpu_custom_call" | custom-call | tf_op jit(solution)/shard_map/forward_planes_1/pallas_call | solution.py:148
  39.2 6.1 %forward_planes_2.1 = (f32[2,16,16,128]{3,2,1,0:T(8,128)}, f32[2,16,16,128]{3,2,1,0:T(8,128)}, f32[2,16,16,128]{3,2,1,0:T(8,128)}, f32[2,16,16,128]{3,2,1,0:T(8,128)}) custom-call(s32[1]{0:T(128)} %bitcast.refs_0_._, s32[12]{0:T(128)} %get-tuple-element.56.refs_1_, s32[12]{0:T(128)} %get-tuple-element.55.refs_2_, f32[9,16,32,128]{3,2,1,0:T(8,128)} %copy-done.1, ...), custom_call_target="tpu_custom_call" | custom-call | tf_op jit(solution)/shard_map/forward_planes_2/pallas_call | solution.py:148
  45.3 1.5 collective-permute-start.10
  46.9 0.6 collective-permute-start.9
  47.6 1.5 collective-permute-start.3
  49.1 1.0 fusion.4.refs_4_
  50.1 3.5 %solve_columns_0.1 = (f32[2,16,16,128]{3,2,1,0:T(8,128)}, f32[2,16,16,128]{3,2,1,0:T(8,128)}, f32[2,16,16,128]{3,2,1,0:T(8,128)}, f32[2,16,16,128]{3,2,1,0:T(8,128)}) custom-call(s32[1]{0:T(128)} %bitcast.refs_0_._, f32[2,16,16,128]{3,2,1,0:T(8,128)} %get-tuple-element.45.refs_0_, f32[2,16,16,128]{3,2,1,0:T(8,128)} %copy-done.15, ...), custom_call_target="tpu_custom_call" | custom-call | tf_op jit(solution)/shard_map/solve_columns_0/pallas_call | solution.py:186
  53.7 1.7 %collective-permute-start.4 = (f32[2,16,16,128]{3,2,1,0:T(8,128)S(1)}, f32[2,16,16,128]{3,2,1,0:T(8,128)S(1)}, u32[]{:S(2)}, u32[]{:S(2)}) collective-permute-start(f32[2,16,16,128]{3,2,1,0:T(8,128)S(1)} %copy-done.20), channel_id=1, source_target_pairs={{3,0},{2,1},{1,2},{0,3},{7,4},{6,5},{5,6},{4,7},{11,8},{10,9},{9,1... | collective-permute-start | bytes 786440 | tf_op jit(solution)/shard_map/ppermute | solution.py:312
  55.4 4.7 %collective-permute-done.9.refs_2_ = f32[2,16,16,128]{3,2,1,0:T(8,128)S(1)} collective-permute-done((f32[2,16,16,128]{3,2,1,0:T(8,128)S(1)}, f32[2,16,16,128]{3,2,1,0:T(8,128)S(1)}, u32[]{:S(2)}, u32[]{:S(2)}) %collective-permute-start.9) | collective-permute-done | bytes 262176 | tf_op jit(solution)/shard_map/ppermute | solution.py:312
  60.1 1.5 collective-permute-start.18
  61.6 3.5 %solve_columns_1.1 = (f32[2,16,16,128]{3,2,1,0:T(8,128)}, f32[2,16,16,128]{3,2,1,0:T(8,128)}, f32[2,16,16,128]{3,2,1,0:T(8,128)}, f32[2,16,16,128]{3,2,1,0:T(8,128)}) custom-call(s32[1]{0:T(128)} %bitcast.refs_0_._, f32[2,16,16,128]{3,2,1,0:T(8,128)} %get-tuple-element.37.refs_0_, f32[2,16,16,128]{3,2,1,0:T(8,128)} %copy-done.14, ...), custom_call_target="tpu_custom_call" | custom-call | tf_op jit(solution)/shard_map/solve_columns_1/pallas_call | solution.py:186
  65.2 0.5 collective-permute-done.3.refs_2_
  66.0 4.4 %collective-permute-done.4.refs_3_ = f32[2,16,16,128]{3,2,1,0:T(8,128)S(1)} collective-permute-done((f32[2,16,16,128]{3,2,1,0:T(8,128)S(1)}, f32[2,16,16,128]{3,2,1,0:T(8,128)S(1)}, u32[]{:S(2)}, u32[]{:S(2)}) %collective-permute-start.4) | collective-permute-done | bytes 262176 | tf_op jit(solution)/shard_map/ppermute | solution.py:312
  70.3 1.4 collective-permute-start.12
  71.7 3.5 %solve_columns_2.1 = (f32[2,16,16,128]{3,2,1,0:T(8,128)}, f32[2,16,16,128]{3,2,1,0:T(8,128)}, f32[2,16,16,128]{3,2,1,0:T(8,128)}, f32[2,16,16,128]{3,2,1,0:T(8,128)}) custom-call(s32[1]{0:T(128)} %bitcast.refs_0_._, f32[2,16,16,128]{3,2,1,0:T(8,128)} %get-tuple-element.29.refs_0_, f32[2,16,16,128]{3,2,1,0:T(8,128)} %copy-done.11, ...), custom_call_target="tpu_custom_call" | custom-call | tf_op jit(solution)/shard_map/solve_columns_2/pallas_call | solution.py:186
  75.3 1.3 collective-permute-start.13
  76.5 0.4 collective-permute-done.18.refs_7_
  77.0 4.7 %collective-permute-done.19.refs_8_ = f32[2,16,16,128]{3,2,1,0:T(8,128)S(1)} collective-permute-done((f32[2,16,16,128]{3,2,1,0:T(8,128)}, f32[2,16,16,128]{3,2,1,0:T(8,128)S(1)}, u32[]{:S(2)}, u32[]{:S(2)}) %collective-permute-start.19) | collective-permute-done | bytes 262176 | tf_op jit(solution)/shard_map/ppermute | solution.py:312
  81.7 1.3 collective-permute-start.6
  83.0 0.8 collective-permute-start.7
  83.7 0.5 convert_element_type.10.refs_3_
  84.3 0.5 convert_element_type.11.refs_4_
  84.8 6.1 %add_exchange_0.1.refs_21_ = f32[9,16,32,128]{3,2,1,0:T(8,128)} custom-call(s32[1]{0:T(128)} %bitcast.refs_0_._, s32[12]{0:T(128)} %get-tuple-element.56.refs_1_, s32[12]{0:T(128)} %get-tuple-element.55.refs_2_, f32[12]{0:T(128)} %convert_element_type.10.refs_3_, f32[12]{0:T(128)} %convert_element_type.11.refs_4_, ...), custom_call_target="tpu_custom_call" | custom-call | tf_op jit(solution)/shard_map/add_exchange_0/pallas_call | solution.py:245
  90.9 2.0 %collective-permute-done.13.refs_8_ = f32[2,16,16,128]{3,2,1,0:T(8,128)S(1)} collective-permute-done((f32[2,16,16,128]{3,2,1,0:T(8,128)}, f32[2,16,16,128]{3,2,1,0:T(8,128)S(1)}, u32[]{:S(2)}, u32[]{:S(2)}) %collective-permute-start.13) | collective-permute-done | bytes 262176 | tf_op jit(solution)/shard_map/ppermute | solution.py:312
  92.9 0.7 copy-done.10
  93.6 6.4 %add_exchange_1.1.refs_21_ = f32[9,16,32,128]{3,2,1,0:T(8,128)} custom-call(s32[1]{0:T(128)} %bitcast.refs_0_._, s32[12]{0:T(128)} %get-tuple-element.56.refs_1_, s32[12]{0:T(128)} %get-tuple-element.55.refs_2_, f32[12]{0:T(128)} %convert_element_type.10.refs_3_, f32[12]{0:T(128)} %convert_element_type.11.refs_4_, ...), custom_call_target="tpu_custom_call", output_to_operand_aliasing={{}: (21, {})} | custom-call | tf_op jit(solution)/shard_map/add_exchange_1/pallas_call | solution.py:245
  100.1 3.9 %collective-permute-done.7.refs_8_ = f32[2,16,16,128]{3,2,1,0:T(8,128)S(1)} collective-permute-done((f32[2,16,16,128]{3,2,1,0:T(8,128)}, f32[2,16,16,128]{3,2,1,0:T(8,128)S(1)}, u32[]{:S(2)}, u32[]{:S(2)}) %collective-permute-start.7) | collective-permute-done | bytes 262176 | tf_op jit(solution)/shard_map/ppermute | solution.py:312
  104.0 0.7 copy-done.9
  104.7 7.2 %add_exchange_2.1 = f32[9,16,32,128]{3,2,1,0:T(8,128)} custom-call(s32[1]{0:T(128)} %bitcast.refs_0_._, s32[12]{0:T(128)} %get-tuple-element.56.refs_1_, s32[12]{0:T(128)} %get-tuple-element.55.refs_2_, f32[12]{0:T(128)} %convert_element_type.10.refs_3_, f32[12]{0:T(128)} %convert_element_type.11.refs_4_, ...), custom_call_target="tpu_custom_call", output_to_operand_aliasing={{}: (21, {})} | custom-call | tf_op jit(solution)/shard_map/add_exchange_2/pallas_call | solution.py:245
  111.9 1.5 fusion.19
  113.4 16.2 %collective-permute-start.20 = (f32[3,16,32,128]{3,2,1,0:T(8,128)S(1)}, f32[3,16,32,128]{3,2,1,0:T(8,128)S(1)}, u32[]{:S(2)}, u32[]{:S(2)}) collective-permute-start(f32[3,16,32,128]{3,2,1,0:T(8,128)S(1)} %get-tuple-element.57), channel_id=1, source_target_pairs={{28,0},{0,4},{4,8},{8,12},{12,16},{16,20},{20,24},{24,28},{29,1},{... | collective-permute-start | bytes 2359304 | tf_op jit(solution)/shard_map/ppermute | solution.py:22
  129.5 1.6 collective-permute-start.21
  131.1 16.7 %collective-permute-done.20 = f32[3,16,32,128]{3,2,1,0:T(8,128)S(1)} collective-permute-done((f32[3,16,32,128]{3,2,1,0:T(8,128)S(1)}, f32[3,16,32,128]{3,2,1,0:T(8,128)S(1)}, u32[]{:S(2)}, u32[]{:S(2)}) %collective-permute-start.20) | collective-permute-done | bytes 786464 | tf_op jit(solution)/shard_map/ppermute | solution.py:22
  147.8 19.8 %collective-permute-done.21 = f32[3,16,32,128]{3,2,1,0:T(8,128)S(1)} collective-permute-done((f32[3,16,32,128]{3,2,1,0:T(8,128)S(1)}, f32[3,16,32,128]{3,2,1,0:T(8,128)S(1)}, u32[]{:S(2)}, u32[]{:S(2)}) %collective-permute-start.21) | collective-permute-done | bytes 786464 | tf_op jit(solution)/shard_map/ppermute | solution.py:22
  167.6 1.4 fusion.1
  169.0 1.0 reshape.78
  (71 shorter events, 1.3 us)
Async XLA Ops:
  0.0 6.2 %copy-start = (s32[24,24]{1,0:T(8,128)S(1)}, s32[24,24]{1,0:T(8,128)}, u32[]{:S(2)}) copy-start(s32[24,24]{1,0:T(8,128)} %param.20) | copy-start | bytes 6916
  1.3 21.5 %collective-permute-start = (f32[3,16,32,128]{3,2,1,0:T(8,128)S(1)}, f32[3,16,32,128]{3,2,1,0:T(8,128)}, u32[]{:S(2)}, u32[]{:S(2)}) collective-permute-start(f32[3,16,32,128]{3,2,1,0:T(8,128)S(1)} %bitcast.9), channel_id=1, source_target_pairs={{4,0},{8,4},{12,8},{16,12},{20,16},{24,20},{28,24},{0,28},{5,1},{9... | collective-permute-start | bytes 2359304 | tf_op jit(solution)/shard_map/ppermute | solution.py:22
  1.4 22.6 %collective-permute-start.1 = (f32[3,16,32,128]{3,2,1,0:T(8,128)S(1)}, f32[3,16,32,128]{3,2,1,0:T(8,128)}, u32[]{:S(2)}, u32[]{:S(2)}) collective-permute-start(f32[3,16,32,128]{3,2,1,0:T(8,128)S(1)} %bitcast.10), channel_id=1, source_target_pairs={{8,0},{12,4},{16,8},{20,12},{24,16},{28,20},{0,24},{4,28},{9,1},{1... | collective-permute-start | bytes 2359304 | tf_op jit(solution)/shard_map/ppermute | solution.py:22
  25.1 1.4 copy-start.1
  31.9 15.1 %collective-permute-start.14 = (f32[2,16,16,128]{3,2,1,0:T(8,128)}, f32[2,16,16,128]{3,2,1,0:T(8,128)S(1)}, u32[]{:S(2)}, u32[]{:S(2)}) collective-permute-start(f32[2,16,16,128]{3,2,1,0:T(8,128)} %get-tuple-element.46), channel_id=1, source_target_pairs={{1,0},{0,1},{3,2},{2,3},{5,4},{4,5},{7,6},{6,7},{9,8},{8,9},{11,10... | collective-permute-start | bytes 786440 | tf_op jit(solution)/shard_map/ppermute | solution.py:312
  32.0 15.6 %collective-permute-start.15 = (f32[2,16,16,128]{3,2,1,0:T(8,128)}, f32[2,16,16,128]{3,2,1,0:T(8,128)S(1)}, u32[]{:S(2)}, u32[]{:S(2)}) collective-permute-start(f32[2,16,16,128]{3,2,1,0:T(8,128)} %get-tuple-element.47), channel_id=1, source_target_pairs={{2,0},{3,1},{0,2},{1,3},{6,4},{7,5},{4,6},{5,7},{10,8},{11,9},{8,1... | collective-permute-start | bytes 786440 | tf_op jit(solution)/shard_map/ppermute | solution.py:312
  33.5 14.1 %collective-permute-start.16 = (f32[2,16,16,128]{3,2,1,0:T(8,128)}, f32[2,16,16,128]{3,2,1,0:T(8,128)S(1)}, u32[]{:S(2)}, u32[]{:S(2)}) collective-permute-start(f32[2,16,16,128]{3,2,1,0:T(8,128)} %get-tuple-element.48), channel_id=1, source_target_pairs={{3,0},{2,1},{1,2},{0,3},{7,4},{6,5},{5,6},{4,7},{11,8},{10,9},{9,1... | collective-permute-start | bytes 786440 | tf_op jit(solution)/shard_map/ppermute | solution.py:312
  39.2 6.1 %copy-start.23 = (f32[2,16,16,128]{3,2,1,0:T(8,128)S(1)}, f32[2,16,16,128]{3,2,1,0:T(8,128)}, u32[]{:S(2)}) copy-start(f32[2,16,16,128]{3,2,1,0:T(8,128)} %get-tuple-element.40) | copy-start | bytes 786436
  39.2 7.6 %copy-start.22 = (f32[2,16,16,128]{3,2,1,0:T(8,128)S(1)}, f32[2,16,16,128]{3,2,1,0:T(8,128)}, u32[]{:S(2)}) copy-start(f32[2,16,16,128]{3,2,1,0:T(8,128)} %get-tuple-element.38) | copy-start | bytes 786436
  39.2 7.8 %copy-start.21 = (f32[2,16,16,128]{3,2,1,0:T(8,128)S(1)}, f32[2,16,16,128]{3,2,1,0:T(8,128)}, u32[]{:S(2)}) copy-start(f32[2,16,16,128]{3,2,1,0:T(8,128)} %get-tuple-element.39) | copy-start | bytes 786436
  45.2 8.4 %copy-start.20 = (f32[2,16,16,128]{3,2,1,0:T(8,128)S(1)}, f32[2,16,16,128]{3,2,1,0:T(8,128)}, u32[]{:S(2)}) copy-start(f32[2,16,16,128]{3,2,1,0:T(8,128)} %get-tuple-element.32) | copy-start | bytes 786436
  45.3 8.4 %collective-permute-start.10 = (f32[2,16,16,128]{3,2,1,0:T(8,128)S(1)}, f32[2,16,16,128]{3,2,1,0:T(8,128)S(1)}, u32[]{:S(2)}, u32[]{:S(2)}) collective-permute-start(f32[2,16,16,128]{3,2,1,0:T(8,128)S(1)} %copy-done.23), channel_id=1, source_target_pairs={{3,0},{2,1},{1,2},{0,3},{7,4},{6,5},{5,6},{4,7},{11,8},{10,9},{9,1... | collective-permute-start | bytes 786440 | tf_op jit(solution)/shard_map/ppermute | solution.py:312
  46.8 8.6 %collective-permute-start.8 = (f32[2,16,16,128]{3,2,1,0:T(8,128)S(1)}, f32[2,16,16,128]{3,2,1,0:T(8,128)S(1)}, u32[]{:S(2)}, u32[]{:S(2)}) collective-permute-start(f32[2,16,16,128]{3,2,1,0:T(8,128)S(1)} %copy-done.22), channel_id=1, source_target_pairs={{1,0},{0,1},{3,2},{2,3},{5,4},{4,5},{7,6},{6,7},{9,8},{8,9},{11,10... | collective-permute-start | bytes 786440 | tf_op jit(solution)/shard_map/ppermute | solution.py:312
  46.9 3.2 %copy-start.15 = (f32[2,16,16,128]{3,2,1,0:T(8,128)}, f32[2,16,16,128]{3,2,1,0:T(8,128)S(1)}, u32[]{:S(2)}) copy-start(f32[2,16,16,128]{3,2,1,0:T(8,128)S(1)} %collective-permute-done.14.refs_1_) | copy-start | bytes 786436
  46.9 13.2 %collective-permute-start.9 = (f32[2,16,16,128]{3,2,1,0:T(8,128)S(1)}, f32[2,16,16,128]{3,2,1,0:T(8,128)S(1)}, u32[]{:S(2)}, u32[]{:S(2)}) collective-permute-start(f32[2,16,16,128]{3,2,1,0:T(8,128)S(1)} %copy-done.21), channel_id=1, source_target_pairs={{2,0},{3,1},{0,2},{1,3},{6,4},{7,5},{4,6},{5,7},{10,8},{11,9},{8,1... | collective-permute-start | bytes 786440 | tf_op jit(solution)/shard_map/ppermute | solution.py:312
  47.6 2.6 %copy-start.16 = (f32[2,16,16,128]{3,2,1,0:T(8,128)}, f32[2,16,16,128]{3,2,1,0:T(8,128)S(1)}, u32[]{:S(2)}) copy-start(f32[2,16,16,128]{3,2,1,0:T(8,128)S(1)} %collective-permute-done.15.refs_2_) | copy-start | bytes 786436
  47.6 17.5 %collective-permute-start.2 = (f32[2,16,16,128]{3,2,1,0:T(8,128)}, f32[2,16,16,128]{3,2,1,0:T(8,128)S(1)}, u32[]{:S(2)}, u32[]{:S(2)}) collective-permute-start(f32[2,16,16,128]{3,2,1,0:T(8,128)} %get-tuple-element.30), channel_id=1, source_target_pairs={{1,0},{0,1},{3,2},{2,3},{5,4},{4,5},{7,6},{6,7},{9,8},{8,9},{11,10... | collective-permute-start | bytes 786440 | tf_op jit(solution)/shard_map/ppermute | solution.py:312
  47.6 2.5 %copy-start.19 = (f32[2,16,16,128]{3,2,1,0:T(8,128)}, f32[2,16,16,128]{3,2,1,0:T(8,128)S(1)}, u32[]{:S(2)}) copy-start(f32[2,16,16,128]{3,2,1,0:T(8,128)S(1)} %collective-permute-done.16.refs_3_) | copy-start | bytes 786436
  47.6 18.1 %collective-permute-start.3 = (f32[2,16,16,128]{3,2,1,0:T(8,128)}, f32[2,16,16,128]{3,2,1,0:T(8,128)S(1)}, u32[]{:S(2)}, u32[]{:S(2)}) collective-permute-start(f32[2,16,16,128]{3,2,1,0:T(8,128)} %get-tuple-element.31), channel_id=1, source_target_pairs={{2,0},{3,1},{0,2},{1,3},{6,4},{7,5},{4,6},{5,7},{10,8},{11,9},{8,1... | collective-permute-start | bytes 786440 | tf_op jit(solution)/shard_map/ppermute | solution.py:312
  53.6 7.9 %copy-start.13 = (f32[2,16,16,128]{3,2,1,0:T(8,128)}, f32[2,16,16,128]{3,2,1,0:T(8,128)S(1)}, u32[]{:S(2)}) copy-start(f32[2,16,16,128]{3,2,1,0:T(8,128)S(1)} %collective-permute-done.10.refs_3_) | copy-start | bytes 786436
  53.7 16.7 %collective-permute-start.4 = (f32[2,16,16,128]{3,2,1,0:T(8,128)S(1)}, f32[2,16,16,128]{3,2,1,0:T(8,128)S(1)}, u32[]{:S(2)}, u32[]{:S(2)}) collective-permute-start(f32[2,16,16,128]{3,2,1,0:T(8,128)S(1)} %copy-done.20), channel_id=1, source_target_pairs={{3,0},{2,1},{1,2},{0,3},{7,4},{6,5},{5,6},{4,7},{11,8},{10,9},{9,1... | collective-permute-start | bytes 786440 | tf_op jit(solution)/shard_map/ppermute | solution.py:312
  55.4 6.2 %copy-start.14 = (f32[2,16,16,128]{3,2,1,0:T(8,128)}, f32[2,16,16,128]{3,2,1,0:T(8,128)S(1)}, u32[]{:S(2)}) copy-start(f32[2,16,16,128]{3,2,1,0:T(8,128)S(1)} %collective-permute-done.8.refs_1_) | copy-start | bytes 786436
  55.4 19.9 %collective-permute-start.17 = (f32[2,16,16,128]{3,2,1,0:T(8,128)}, f32[2,16,16,128]{3,2,1,0:T(8,128)S(1)}, u32[]{:S(2)}, u32[]{:S(2)}) collective-permute-start(f32[2,16,16,128]{3,2,1,0:T(8,128)} %get-tuple-element.50), channel_id=1, source_target_pairs={{1,0},{0,1},{3,2},{2,3},{5,4},{4,5},{7,6},{6,7},{9,8},{8,9},{11,10... | collective-permute-start | bytes 786440 | tf_op jit(solution)/shard_map/ppermute | solution.py:312
  60.1 1.5 copy-start.18
  60.1 16.9 %collective-permute-start.18 = (f32[2,16,16,128]{3,2,1,0:T(8,128)}, f32[2,16,16,128]{3,2,1,0:T(8,128)S(1)}, u32[]{:S(2)}, u32[]{:S(2)}) collective-permute-start(f32[2,16,16,128]{3,2,1,0:T(8,128)} %get-tuple-element.51), channel_id=1, source_target_pairs={{2,0},{3,1},{0,2},{1,3},{6,4},{7,5},{4,6},{5,7},{10,8},{11,9},{8,1... | collective-permute-start | bytes 786440 | tf_op jit(solution)/shard_map/ppermute | solution.py:312
  65.1 6.7 %copy-start.11 = (f32[2,16,16,128]{3,2,1,0:T(8,128)}, f32[2,16,16,128]{3,2,1,0:T(8,128)S(1)}, u32[]{:S(2)}) copy-start(f32[2,16,16,128]{3,2,1,0:T(8,128)S(1)} %collective-permute-done.2.refs_1_) | copy-start | bytes 786436
  65.1 16.6 %collective-permute-start.19 = (f32[2,16,16,128]{3,2,1,0:T(8,128)}, f32[2,16,16,128]{3,2,1,0:T(8,128)S(1)}, u32[]{:S(2)}, u32[]{:S(2)}) collective-permute-start(f32[2,16,16,128]{3,2,1,0:T(8,128)} %get-tuple-element.52), channel_id=1, source_target_pairs={{3,0},{2,1},{1,2},{0,3},{7,4},{6,5},{5,6},{4,7},{11,8},{10,9},{9,1... | collective-permute-start | bytes 786440 | tf_op jit(solution)/shard_map/ppermute | solution.py:312
  65.7 6.0 %copy-start.12 = (f32[2,16,16,128]{3,2,1,0:T(8,128)}, f32[2,16,16,128]{3,2,1,0:T(8,128)S(1)}, u32[]{:S(2)}) copy-start(f32[2,16,16,128]{3,2,1,0:T(8,128)S(1)} %collective-permute-done.3.refs_2_) | copy-start | bytes 786436
  65.7 17.3 %collective-permute-start.11 = (f32[2,16,16,128]{3,2,1,0:T(8,128)}, f32[2,16,16,128]{3,2,1,0:T(8,128)S(1)}, u32[]{:S(2)}, u32[]{:S(2)}) collective-permute-start(f32[2,16,16,128]{3,2,1,0:T(8,128)} %get-tuple-element.42), channel_id=1, source_target_pairs={{1,0},{0,1},{3,2},{2,3},{5,4},{4,5},{7,6},{6,7},{9,8},{8,9},{11,10... | collective-permute-start | bytes 786440 | tf_op jit(solution)/shard_map/ppermute | solution.py:312
  70.3 1.4 copy-start.17
  70.3 20.6 %collective-permute-start.12 = (f32[2,16,16,128]{3,2,1,0:T(8,128)}, f32[2,16,16,128]{3,2,1,0:T(8,128)S(1)}, u32[]{:S(2)}, u32[]{:S(2)}) collective-permute-start(f32[2,16,16,128]{3,2,1,0:T(8,128)} %get-tuple-element.43), channel_id=1, source_target_pairs={{2,0},{3,1},{0,2},{1,3},{6,4},{7,5},{4,6},{5,7},{10,8},{11,9},{8,1... | collective-permute-start | bytes 786440 | tf_op jit(solution)/shard_map/ppermute | solution.py:312
  75.2 9.6 %copy-start.2 = (f32[2,16,16,128]{3,2,1,0:T(8,128)}, f32[2,16,16,128]{3,2,1,0:T(8,128)S(1)}, u32[]{:S(2)}) copy-start(f32[2,16,16,128]{3,2,1,0:T(8,128)S(1)} %collective-permute-done.17.refs_6_) | copy-start | bytes 786436
  75.3 17.6 %collective-permute-start.13 = (f32[2,16,16,128]{3,2,1,0:T(8,128)}, f32[2,16,16,128]{3,2,1,0:T(8,128)S(1)}, u32[]{:S(2)}, u32[]{:S(2)}) collective-permute-start(f32[2,16,16,128]{3,2,1,0:T(8,128)} %get-tuple-element.44), channel_id=1, source_target_pairs={{3,0},{2,1},{1,2},{0,3},{7,4},{6,5},{5,6},{4,7},{11,8},{10,9},{9,1... | collective-permute-start | bytes 786440 | tf_op jit(solution)/shard_map/ppermute | solution.py:312
  77.0 7.9 %copy-start.3 = (f32[2,16,16,128]{3,2,1,0:T(8,128)}, f32[2,16,16,128]{3,2,1,0:T(8,128)S(1)}, u32[]{:S(2)}) copy-start(f32[2,16,16,128]{3,2,1,0:T(8,128)S(1)} %collective-permute-done.18.refs_7_) | copy-start | bytes 786436
  77.0 23.1 %collective-permute-start.5 = (f32[2,16,16,128]{3,2,1,0:T(8,128)}, f32[2,16,16,128]{3,2,1,0:T(8,128)S(1)}, u32[]{:S(2)}, u32[]{:S(2)}) collective-permute-start(f32[2,16,16,128]{3,2,1,0:T(8,128)} %get-tuple-element.34), channel_id=1, source_target_pairs={{1,0},{0,1},{3,2},{2,3},{5,4},{4,5},{7,6},{6,7},{9,8},{8,9},{11,10... | collective-permute-start | bytes 786440 | tf_op jit(solution)/shard_map/ppermute | solution.py:312
  81.7 3.1 %copy-start.5 = (f32[2,16,16,128]{3,2,1,0:T(8,128)}, f32[2,16,16,128]{3,2,1,0:T(8,128)S(1)}, u32[]{:S(2)}) copy-start(f32[2,16,16,128]{3,2,1,0:T(8,128)S(1)} %collective-permute-done.19.refs_8_) | copy-start | bytes 786436
  81.7 18.4 %collective-permute-start.6 = (f32[2,16,16,128]{3,2,1,0:T(8,128)}, f32[2,16,16,128]{3,2,1,0:T(8,128)S(1)}, u32[]{:S(2)}, u32[]{:S(2)}) collective-permute-start(f32[2,16,16,128]{3,2,1,0:T(8,128)} %get-tuple-element.35), channel_id=1, source_target_pairs={{2,0},{3,1},{0,2},{1,3},{6,4},{7,5},{4,6},{5,7},{10,8},{11,9},{8,1... | collective-permute-start | bytes 786440 | tf_op jit(solution)/shard_map/ppermute | solution.py:312
  83.0 7.9 %copy-start.4 = (f32[2,16,16,128]{3,2,1,0:T(8,128)}, f32[2,16,16,128]{3,2,1,0:T(8,128)S(1)}, u32[]{:S(2)}) copy-start(f32[2,16,16,128]{3,2,1,0:T(8,128)S(1)} %collective-permute-done.11.refs_6_) | copy-start | bytes 786436
  83.0 21.0 %collective-permute-start.7 = (f32[2,16,16,128]{3,2,1,0:T(8,128)}, f32[2,16,16,128]{3,2,1,0:T(8,128)S(1)}, u32[]{:S(2)}, u32[]{:S(2)}) collective-permute-start(f32[2,16,16,128]{3,2,1,0:T(8,128)} %get-tuple-element.36), channel_id=1, source_target_pairs={{3,0},{2,1},{1,2},{0,3},{7,4},{6,5},{5,6},{4,7},{11,8},{10,9},{9,1... | collective-permute-start | bytes 786440 | tf_op jit(solution)/shard_map/ppermute | solution.py:312
  90.9 2.0 %copy-start.6 = (f32[2,16,16,128]{3,2,1,0:T(8,128)}, f32[2,16,16,128]{3,2,1,0:T(8,128)S(1)}, u32[]{:S(2)}) copy-start(f32[2,16,16,128]{3,2,1,0:T(8,128)S(1)} %collective-permute-done.12.refs_7_) | copy-start | bytes 786436
  92.9 0.7 copy-start.10
  100.0 3.9 %copy-start.7 = (f32[2,16,16,128]{3,2,1,0:T(8,128)}, f32[2,16,16,128]{3,2,1,0:T(8,128)S(1)}, u32[]{:S(2)}) copy-start(f32[2,16,16,128]{3,2,1,0:T(8,128)S(1)} %collective-permute-done.5.refs_6_) | copy-start | bytes 786436
  100.1 3.9 %copy-start.8 = (f32[2,16,16,128]{3,2,1,0:T(8,128)}, f32[2,16,16,128]{3,2,1,0:T(8,128)S(1)}, u32[]{:S(2)}) copy-start(f32[2,16,16,128]{3,2,1,0:T(8,128)S(1)} %collective-permute-done.6.refs_7_) | copy-start | bytes 786436
  104.0 0.7 copy-start.9
  113.4 34.4 %collective-permute-start.20 = (f32[3,16,32,128]{3,2,1,0:T(8,128)S(1)}, f32[3,16,32,128]{3,2,1,0:T(8,128)S(1)}, u32[]{:S(2)}, u32[]{:S(2)}) collective-permute-start(f32[3,16,32,128]{3,2,1,0:T(8,128)S(1)} %get-tuple-element.57), channel_id=1, source_target_pairs={{28,0},{0,4},{4,8},{8,12},{12,16},{16,20},{20,24},{24,28},{29,1},{... | collective-permute-start | bytes 2359304 | tf_op jit(solution)/shard_map/ppermute | solution.py:22
  129.5 38.1 %collective-permute-start.21 = (f32[3,16,32,128]{3,2,1,0:T(8,128)S(1)}, f32[3,16,32,128]{3,2,1,0:T(8,128)S(1)}, u32[]{:S(2)}, u32[]{:S(2)}) collective-permute-start(f32[3,16,32,128]{3,2,1,0:T(8,128)S(1)} %get-tuple-element.58), channel_id=1, source_target_pairs={{24,0},{28,4},{0,8},{4,12},{8,16},{12,20},{16,24},{20,28},{25,1},{... | collective-permute-start | bytes 2359304 | tf_op jit(solution)/shard_map/ppermute | solution.py:22

commit v3 on v2

--- a/solution.py
+++ b/solution.py
@@ -116,7 +116,7 @@
     return [spec(0, p) for p in range(GROUP)] + [spec(1, p) for p in range(GROUP)]
 
 
-def forward_planes(group, scalars, flat, tables, parts):
+def forward_planes(group, half, scalars, flat, tables, parts):
     _, planes, rows, lanes = flat.shape
     n = lanes // 2
     width = n // parts
@@ -154,22 +154,26 @@
             out_specs=[pl.BlockSpec((2, width, bx, lanes), lambda i, *_: (0, 0, i, 0))] * parts,
         ),
         out_shape=[jax.ShapeDtypeStruct((2, width, planes, lanes), jnp.float32)] * parts,
-        name=f"forward_planes_{group}",
+        name=f"forward_planes_{group}_{half}",
     )(*scalars, *([flat] * (2 * GROUP)), *ops)
 
 
 def solve_columns(group, me, columns, kernel, tables):
+    pieces_each = len(columns[0])
     parts = len(columns)
-    _, width, planes, lanes = columns[0].shape
+    inputs = [piece for peer in columns for piece in peer]
+    count = len(inputs)
+    _, width, bx, lanes = inputs[0].shape
+    planes = pieces_each * bx
     n = parts * planes
     bk = BLOCK_PLANES
 
     def body(_, *refs):
-        data, outs = refs[:parts], refs[parts + 5 :]
-        kern, fh, fl, ih, il = refs[parts : parts + 5]
+        data, outs = refs[:count], refs[count + 5 :]
+        kern, fh, fl, ih, il = refs[count : count + 5]
         cols = []
         for k in range(bk):
-            pieces = [data[d][c, k] for c in range(2) for d in range(parts)]
+            pieces = [data[d][c, k] for c in range(2) for d in range(count)]
             cols.append(jnp.concatenate(pieces, axis=0))
         spectrum = left(fh, fl, jnp.concatenate(cols, axis=1))
         weights = jnp.concatenate([kern[k] for k in range(bk)], axis=1)
@@ -188,17 +192,17 @@
         grid_spec=pltpu.PrefetchScalarGridSpec(
             num_scalar_prefetch=1,
             grid=(width // bk,),
-            in_specs=[block] * parts
+            in_specs=[pl.BlockSpec((2, bk, bx, lanes), lambda i, *_: (0, i, 0, 0))] * count
             + [pl.BlockSpec((bk, n, lanes), lambda i, *_: (i, 0, 0))]
             + [table_spec(t) for t in ops],
             out_specs=[block] * parts,
         ),
-        out_shape=[jax.ShapeDtypeStruct(columns[0].shape, jnp.float32)] * parts,
+        out_shape=[jax.ShapeDtypeStruct((2, width, planes, lanes), jnp.float32)] * parts,
         name=f"solve_columns_{group}",
-    )(me, *columns, kernel, *ops)
-
-
-def add_exchange(group, scalars, returned, flat, totals, tables):
+    )(me, *inputs, kernel, *ops)
+
+
+def add_exchange(group, half, scalars, returned, flat, totals, tables):
     slots, planes, rows, lanes = flat.shape
     parts = len(returned)
     width = returned[0].shape[1]
@@ -234,7 +238,7 @@
 
     ops = [*tables[4], *tables[0]]
     total_spec = pl.BlockSpec((slots, bx, rows, lanes), lambda i, *_: (0, i, 0, 0))
-    in_specs = [pl.BlockSpec((2, width, bx, lanes), lambda i, *_: (0, 0, i, 0))] * parts
+    in_specs = [pl.BlockSpec((2, width, bx, lanes), lambda i, *_: (0, 0, half, 0))] * parts
     in_specs += orbital_specs(group, bx, rows, lanes) + [table_spec(t) for t in ops]
     args = [*scalars, *returned, *([flat] * (2 * GROUP)), *ops]
     aliases = {}
@@ -252,7 +256,7 @@
         ),
         out_shape=jax.ShapeDtypeStruct(flat.shape, jnp.float32),
         input_output_aliases=aliases,
-        name=f"add_exchange_{group}",
+        name=f"add_exchange_{group}_{half}",
     )(*args)
 
 
@@ -290,14 +294,42 @@
     return jnp.where(squared > 0, scale / safe, 0.0)
 
 
+def pair_swap(block):
+    return lax.ppermute(block, "band", [(i, i ^ 1) for i in range(lax.axis_size("band"))])
+
+
+def visiting(own):
+    if REACH != 2 or lax.axis_size("band") % 2:
+        return [shifted(own, "band", -d) for d in range(1, REACH + 1)]
+    even = lax.axis_index("band") % 2 == 0
+    second = shifted(own, "band", -2)
+    return [pair_swap(jnp.where(even, second, own)), second]
+
+
+def collected(totals, count):
+    pieces = [totals[d * count : (d + 1) * count] for d in range(REACH + 1)]
+    if REACH != 2 or lax.axis_size("band") % 2:
+        owned = pieces[0]
+        for d in range(1, REACH + 1):
+            owned = owned + shifted(pieces[d], "band", d)
+        return owned
+    even = lax.axis_index("band") % 2 == 0
+    swapped = pair_swap(pieces[1])
+    ahead = shifted(pieces[2] + jnp.where(even, swapped, 0.0), "band", 2)
+    return pieces[0] + jnp.where(even, 0.0, swapped) + ahead
+
+
 def local(orbitals, pair_mask):
     orb_count, planes, cells = orbitals.shape
     n = math.isqrt(cells)
     parts = lax.axis_size("grid")
     tables = dft_tables(n, parts)
     own = orbitals.reshape(orb_count, planes, n // 2, 2 * n)
-    visits = [own] + [shifted(own, "band", -d) for d in range(1, REACH + 1)]
-    flat = jnp.concatenate(visits, axis=0)
+    halves_of = range(planes // BLOCK_PLANES)
+    flats = []
+    for h in halves_of:
+        mine = own[:, h * BLOCK_PLANES : (h + 1) * BLOCK_PLANES]
+        flats.append(jnp.concatenate([mine, *visiting(mine)], axis=0))
     me = lax.axis_index("grid").astype(jnp.int32).reshape(1)
     scalars = (me, *live_pairs(pair_mask))
     kernel = green_kernel(n, n // parts)
@@ -313,17 +345,22 @@
         return moved
 
     turns = range(-(-CAP // GROUP))
-    spectra = [forward_planes(g, scalars[:3], flat, tables, parts) for g in turns]
-    columns = [exchange(s) for s in spectra]
-    solved = [solve_columns(g, me, columns[g], kernel, tables) for g in turns]
-    returned = [exchange(s) for s in solved]
-    totals = None
+    moved = [
+        [exchange(forward_planes(g, h, scalars[:3], flats[h], tables, parts)) for g in turns]
+        for h in halves_of
+    ]
+    returned = []
     for g in turns:
-        totals = add_exchange(g, scalars, returned[g], flat, totals, tables)
-    owned = totals[:orb_count]
-    for d in range(1, REACH + 1):
-        owned = owned + shifted(totals[d * orb_count : (d + 1) * orb_count], "band", d)
-    return (-MIXING * owned).reshape(orb_count, planes, cells)
+        columns = [[moved[h][g][s] for h in halves_of] for s in range(parts)]
+        returned.append(exchange(solve_columns(g, me, columns, kernel, tables)))
+    owned = []
+    for h in halves_of:
+        totals = None
+        for g in turns:
+            totals = add_exchange(g, h, scalars, returned[g], flats[h], totals, tables)
+        owned.append(collected(totals, orb_count))
+    total = jnp.concatenate(owned, axis=1)
+    return (-MIXING * total).reshape(orb_count, planes, cells)
 
 
 def solution(mesh):

time: 170 us -> 180 us (1.059); the launches traced: 170 us -> 177 us
  Pallas kernels: 46.8 us -> 64.9 us
  starting transfers between devices: 35.9 us -> 30.3 us
  waiting for transfers between devices: 70.7 us -> 66.1 us
  local copies, waits for them, and re-layouts: 9.88 us -> 5.97 us
  other arithmetic: 6.47 us -> 9.25 us
    ppermute x4, waiting for transfers between devices: 50 us -> 26.6 us  [shifted(): lax.ppermute(block, axis, [((i - distance) % count, i) for i in range(cou...]
    ppermute x4, starting transfers between devices: 21.9 us -> 8.05 us  [shifted(): lax.ppermute(block, axis, [((i - distance) % count, i) for i in range(cou...]
    ppermute x0 -> x4, waiting for transfers between devices: none -> 13.2 us  [pair_swap(): lax.ppermute(block, 'band', [(i, i ^ 1) for i in range(lax.axis_size('ban...]
    pallas_call x3 -> x6, Pallas kernels: 19.7 us -> 29.5 us  [add_exchange(): pl.pallas_call(body, grid_spec=pltpu.PrefetchScalarGridSpec(num_scalar_pr...]
    pallas_call x3 -> x6, Pallas kernels: 16.6 us -> 24.6 us  [forward_planes(): pl.pallas_call(body, grid_spec=pltpu.PrefetchScalarGridSpec(num_scalar_pr...]
    ppermute x18 -> x27, waiting for transfers between devices: 20.7 us -> 26.3 us  [exchange(): moved.append(lax.ppermute(blocks[back], 'grid', route))]
    ppermute x18 -> x27, starting transfers between devices: 14 us -> 19 us  [exchange(): moved.append(lax.ppermute(blocks[back], 'grid', route))]
    ppermute x0 -> x4, starting transfers between devices: none -> 3.25 us  [pair_swap(): lax.ppermute(block, 'band', [(i, i ^ 1) for i in range(lax.axis_size('ban...]
  transfers between devices with their start and end apart: 22 -> 35, of which waited for: 10 -> 11; matrix products, arithmetic and copies ran while one was open for 4% -> 5% of each run, Pallas kernels for 20% -> 34%
where the time goes in v3:
time: 180 us; the launch traced here: 177 us
  waiting for transfers between devices  66.1 us (37%)
  Pallas kernels  64.9 us (36%)
  starting transfers between devices  30.3 us (17%)
  other arithmetic  9.25 us (5%)
  local copies, waits for them, and re-layouts  5.97 us (3%)
    pallas_call x6, Pallas kernels, add_exchange(): pl.pallas_call(body, grid_spec=pltpu.PrefetchScalarGridSpec(num_scalar_pr...  29.5 us
    ppermute x4, waiting for transfers between devices, shifted(): lax.ppermute(block, axis, [((i - distance) % count, i) for i in range(cou...  26.6 us
    ppermute x27, waiting for transfers between devices, exchange(): moved.append(lax.ppermute(blocks[back], 'grid', route))  26.3 us
    pallas_call x6, Pallas kernels, forward_planes(): pl.pallas_call(body, grid_spec=pltpu.PrefetchScalarGridSpec(num_scalar_pr...  24.6 us
    ppermute x27, starting transfers between devices, exchange(): moved.append(lax.ppermute(blocks[back], 'grid', route))  19 us
    ppermute x4, waiting for transfers between devices, pair_swap(): lax.ppermute(block, 'band', [(i, i ^ 1) for i in range(lax.axis_size('ban...  13.2 us
    pallas_call x3, Pallas kernels, solve_columns(): pl.pallas_call(body, grid_spec=pltpu.PrefetchScalarGridSpec(num_scalar_pr...  10.8 us
    ppermute x4, starting transfers between devices, shifted(): lax.ppermute(block, axis, [((i - distance) % count, i) for i in range(cou...  8.05 us
  transfers between devices with their start and end apart: 35, of which 11 were waited for; matrix products, arithmetic and copies ran while one was open for 5% of the time, Pallas kernels for 34%

profile of v3, /device:TPU:4, one launch (start us, length us, event | category | flops | bytes accessed | tf_op | source)
XLA Modules:
  0.0 177.1 jit_solution(9825498596767092963)
XLA Ops:
  0.0 1.3 copy.24
  1.4 3.7 %collective-permute-start.2 = (f32[3,8,32,128]{3,2,1,0:T(8,128)S(1)}, f32[3,8,32,128]{3,2,1,0:T(8,128)S(1)}, u32[]{:S(2)}, u32[]{:S(2)}) collective-permute-start(f32[3,8,32,128]{3,2,1,0:T(8,128)S(1)} %slice.35), channel_id=1, source_target_pairs={{8,0},{12,4},{16,8},{20,12},{24,16},{28,20},{0,24},{4,28},{9,1},{1... | collective-permute-start | bytes 1179656 | tf_op jit(solution)/shard_map/ppermute | solution.py:22
  5.0 8.4 %collective-permute-done.2 = f32[3,8,32,128]{3,2,1,0:T(8,128)S(1)} collective-permute-done((f32[3,8,32,128]{3,2,1,0:T(8,128)S(1)}, f32[3,8,32,128]{3,2,1,0:T(8,128)S(1)}, u32[]{:S(2)}, u32[]{:S(2)}) %collective-permute-start.2) | collective-permute-done | bytes 393248 | tf_op jit(solution)/shard_map/ppermute | solution.py:22
  13.5 4.3 %collective-permute-start = (f32[3,8,32,128]{3,2,1,0:T(8,128)S(1)}, f32[3,8,32,128]{3,2,1,0:T(8,128)S(1)}, u32[]{:S(2)}, u32[]{:S(2)}) collective-permute-start(f32[3,8,32,128]{3,2,1,0:T(8,128)S(1)} %get-tuple-element.82), channel_id=1, source_target_pairs={{8,0},{12,4},{16,8},{20,12},{24,16},{28,20},{0,24},{4,28},{9,1},{1... | collective-permute-start | bytes 1179656 | tf_op jit(solution)/shard_map/ppermute | solution.py:22
  19.3 6.0 %collective-permute-done = f32[3,8,32,128]{3,2,1,0:T(8,128)S(1)} collective-permute-done((f32[3,8,32,128]{3,2,1,0:T(8,128)S(1)}, f32[3,8,32,128]{3,2,1,0:T(8,128)S(1)}, u32[]{:S(2)}, u32[]{:S(2)}) %collective-permute-start) | collective-permute-done | bytes 393248 | tf_op jit(solution)/shard_map/ppermute | solution.py:22
  26.0 1.4 fusion.7
  27.4 3.3 %collective-permute-done.3 = f32[3,8,32,128]{3,2,1,0:T(8,128)S(1)} collective-permute-done((f32[3,8,32,128]{3,2,1,0:T(8,128)S(1)}, f32[3,8,32,128]{3,2,1,0:T(8,128)S(1)}, u32[]{:S(2)}, u32[]{:S(2)}) %collective-permute-start.3) | collective-permute-done | bytes 393248 | tf_op jit(solution)/shard_map/ppermute | solution.py:298
  30.6 1.2 pad_maximum_fusion.1.refs_3_.refs_4_.refs_5_.refs_6_.refs_7_.refs_8_.refs_9_.refs_10_.refs_11_.refs_12_.refs_13_.refs_14_.refs_15_.refs_16_
  31.8 4.0 %forward_planes_0_1.1 = (f32[2,16,8,128]{3,2,1,0:T(8,128)}, f32[2,16,8,128]{3,2,1,0:T(8,128)}, f32[2,16,8,128]{3,2,1,0:T(8,128)}, f32[2,16,8,128]{3,2,1,0:T(8,128)}) custom-call(s32[1]{0:T(128)} %bitcast.refs_0_._, s32[12]{0:T(128)} %get-tuple-element.80.refs_1_, s32[12]{0:T(128)} %get-tuple-element.79.refs_2_, ...), custom_call_target="tpu_custom_call" | custom-call | tf_op jit(solution)/shard_map/forward_planes_0_1/pallas_call | solution.py:148
  35.8 4.2 %forward_planes_1_1.1 = (f32[2,16,8,128]{3,2,1,0:T(8,128)}, f32[2,16,8,128]{3,2,1,0:T(8,128)}, f32[2,16,8,128]{3,2,1,0:T(8,128)}, f32[2,16,8,128]{3,2,1,0:T(8,128)}) custom-call(s32[1]{0:T(128)} %bitcast.refs_0_._, s32[12]{0:T(128)} %get-tuple-element.80.refs_1_, s32[12]{0:T(128)} %get-tuple-element.79.refs_2_, ...), custom_call_target="tpu_custom_call" | custom-call | tf_op jit(solution)/shard_map/forward_planes_1_1/pallas_call | solution.py:148
  40.0 1.5 collective-permute-start.25
  42.2 1.5 collective-permute-start.16
  43.8 1.2 pad_maximum_fusion.refs_3_.refs_4_.refs_5_.refs_6_.refs_7_.refs_8_.refs_9_.refs_10_.refs_11_.refs_12_.refs_13_.refs_14_.refs_15_.refs_16_
  44.9 4.1 %forward_planes_0_0.1 = (f32[2,16,8,128]{3,2,1,0:T(8,128)}, f32[2,16,8,128]{3,2,1,0:T(8,128)}, f32[2,16,8,128]{3,2,1,0:T(8,128)}, f32[2,16,8,128]{3,2,1,0:T(8,128)}) custom-call(s32[1]{0:T(128)} %bitcast.refs_0_._, s32[12]{0:T(128)} %get-tuple-element.80.refs_1_, s32[12]{0:T(128)} %get-tuple-element.79.refs_2_, ...), custom_call_target="tpu_custom_call" | custom-call | tf_op jit(solution)/shard_map/forward_planes_0_0/pallas_call | solution.py:148
  49.0 4.2 %forward_planes_1_0.1 = (f32[2,16,8,128]{3,2,1,0:T(8,128)}, f32[2,16,8,128]{3,2,1,0:T(8,128)}, f32[2,16,8,128]{3,2,1,0:T(8,128)}, f32[2,16,8,128]{3,2,1,0:T(8,128)}) custom-call(s32[1]{0:T(128)} %bitcast.refs_0_._, s32[12]{0:T(128)} %get-tuple-element.80.refs_1_, s32[12]{0:T(128)} %get-tuple-element.79.refs_2_, ...), custom_call_target="tpu_custom_call" | custom-call | tf_op jit(solution)/shard_map/forward_planes_1_0/pallas_call | solution.py:148
  53.9 1.6 collective-permute-start.24
  56.2 1.5 collective-permute-start.15
  57.7 4.0 %forward_planes_2_1.1 = (f32[2,16,8,128]{3,2,1,0:T(8,128)}, f32[2,16,8,128]{3,2,1,0:T(8,128)}, f32[2,16,8,128]{3,2,1,0:T(8,128)}, f32[2,16,8,128]{3,2,1,0:T(8,128)}) custom-call(s32[1]{0:T(128)} %bitcast.refs_0_._, s32[12]{0:T(128)} %get-tuple-element.80.refs_1_, s32[12]{0:T(128)} %get-tuple-element.79.refs_2_, ...), custom_call_target="tpu_custom_call" | custom-call | tf_op jit(solution)/shard_map/forward_planes_2_1/pallas_call | solution.py:148
  61.8 4.1 %forward_planes_2_0.1 = (f32[2,16,8,128]{3,2,1,0:T(8,128)}, f32[2,16,8,128]{3,2,1,0:T(8,128)}, f32[2,16,8,128]{3,2,1,0:T(8,128)}, f32[2,16,8,128]{3,2,1,0:T(8,128)}) custom-call(s32[1]{0:T(128)} %bitcast.refs_0_._, s32[12]{0:T(128)} %get-tuple-element.80.refs_1_, s32[12]{0:T(128)} %get-tuple-element.79.refs_2_, ...), custom_call_target="tpu_custom_call" | custom-call | tf_op jit(solution)/shard_map/forward_planes_2_0/pallas_call | solution.py:148
  66.7 1.3 collective-permute-start.9
  68.8 1.0 fusion.2.refs_8_
  69.8 7.4 %collective-permute-done.17.refs_6_ = f32[2,16,8,128]{3,2,1,0:T(8,128)S(1)} collective-permute-done((f32[2,16,8,128]{3,2,1,0:T(8,128)S(1)}, f32[2,16,8,128]{3,2,1,0:T(8,128)S(1)}, u32[]{:S(2)}, u32[]{:S(2)}) %collective-permute-start.17) | collective-permute-done | bytes 131104 | tf_op jit(solution)/shard_map/ppermute | solution.py:344
  77.7 3.7 %solve_columns_0.1 = (f32[2,16,16,128]{3,2,1,0:T(8,128)}, f32[2,16,16,128]{3,2,1,0:T(8,128)}, f32[2,16,16,128]{3,2,1,0:T(8,128)}, f32[2,16,16,128]{3,2,1,0:T(8,128)}) custom-call(s32[1]{0:T(128)} %bitcast.refs_0_._, f32[2,16,8,128]{3,2,1,0:T(8,128)} %get-tuple-element.65.refs_0_, f32[2,16,8,128]{3,2,1,0:T(8,128)} %get-tuple-element.66.refs_1_, ...), custom_call_target="tpu_custom_call" | custom-call | tf_op jit(solution)/shard_map/solve_columns_0/pallas_call | solution.py:190
  81.5 3.5 %solve_columns_1.1 = (f32[2,16,16,128]{3,2,1,0:T(8,128)}, f32[2,16,16,128]{3,2,1,0:T(8,128)}, f32[2,16,16,128]{3,2,1,0:T(8,128)}, f32[2,16,16,128]{3,2,1,0:T(8,128)}) custom-call(s32[1]{0:T(128)} %bitcast.refs_0_._, f32[2,16,8,128]{3,2,1,0:T(8,128)} %get-tuple-element.53.refs_0_, f32[2,16,8,128]{3,2,1,0:T(8,128)} %get-tuple-element.54.refs_1_, ...), custom_call_target="tpu_custom_call" | custom-call | tf_op jit(solution)/shard_map/solve_columns_1/pallas_call | solution.py:190
  85.2 1.5 collective-permute-start.29
  87.5 1.3 collective-permute-start.8
  88.8 13.0 %collective-permute-done.8.refs_6_ = f32[2,16,8,128]{3,2,1,0:T(8,128)S(1)} collective-permute-done((f32[2,16,8,128]{3,2,1,0:T(8,128)S(1)}, f32[2,16,8,128]{3,2,1,0:T(8,128)S(1)}, u32[]{:S(2)}, u32[]{:S(2)}) %collective-permute-start.8) | collective-permute-done | bytes 131104 | tf_op jit(solution)/shard_map/ppermute | solution.py:344
  101.9 1.5 collective-permute-start.20
  103.4 3.5 %solve_columns_2.1 = (f32[2,16,16,128]{3,2,1,0:T(8,128)}, f32[2,16,16,128]{3,2,1,0:T(8,128)}, f32[2,16,16,128]{3,2,1,0:T(8,128)}, f32[2,16,16,128]{3,2,1,0:T(8,128)}) custom-call(s32[1]{0:T(128)} %bitcast.refs_0_._, f32[2,16,8,128]{3,2,1,0:T(8,128)} %get-tuple-element.41.refs_0_, f32[2,16,8,128]{3,2,1,0:T(8,128)} %get-tuple-element.42.refs_1_, ...), custom_call_target="tpu_custom_call" | custom-call | tf_op jit(solution)/shard_map/solve_columns_2/pallas_call | solution.py:190
  107.7 1.4 collective-permute-start.11
  110.6 4.7 %add_exchange_0_1.1.refs_21_ = f32[9,8,32,128]{3,2,1,0:T(8,128)} custom-call(s32[1]{0:T(128)} %bitcast.refs_0_._, s32[12]{0:T(128)} %get-tuple-element.80.refs_1_, s32[12]{0:T(128)} %get-tuple-element.79.refs_2_, f32[12]{0:T(128)} %convert_element_type.10.refs_3_, f32[12]{0:T(128)} %convert_element_type.11.refs_4_, ...), custom_call_target="tpu_custom_call" | custom-call | tf_op jit(solution)/shard_map/add_exchange_0_1/pallas_call | solution.py:249
  116.6 5.0 %add_exchange_1_1.1.refs_21_ = f32[9,8,32,128]{3,2,1,0:T(8,128)} custom-call(s32[1]{0:T(128)} %bitcast.refs_0_._, s32[12]{0:T(128)} %get-tuple-element.80.refs_1_, s32[12]{0:T(128)} %get-tuple-element.79.refs_2_, f32[12]{0:T(128)} %convert_element_type.10.refs_3_, f32[12]{0:T(128)} %convert_element_type.11.refs_4_, ...), custom_call_target="tpu_custom_call", output_to_operand_aliasing={{}: (21, {})} | custom-call | tf_op jit(solution)/shard_map/add_exchange_1_1/pallas_call | solution.py:249
  121.6 0.8 collective-permute-done.11.refs_7_
  122.5 4.4 %collective-permute-done.12.refs_8_ = f32[2,16,16,128]{3,2,1,0:T(8,128)S(1)} collective-permute-done((f32[2,16,16,128]{3,2,1,0:T(8,128)}, f32[2,16,16,128]{3,2,1,0:T(8,128)S(1)}, u32[]{:S(2)}, u32[]{:S(2)}) %collective-permute-start.12) | collective-permute-done | bytes 262176 | tf_op jit(solution)/shard_map/ppermute | solution.py:344
  127.6 5.0 %add_exchange_2_1.1 = f32[9,8,32,128]{3,2,1,0:T(8,128)} custom-call(s32[1]{0:T(128)} %bitcast.refs_0_._, s32[12]{0:T(128)} %get-tuple-element.80.refs_1_, s32[12]{0:T(128)} %get-tuple-element.79.refs_2_, f32[12]{0:T(128)} %convert_element_type.10.refs_3_, f32[12]{0:T(128)} %convert_element_type.11.refs_4_, ...), custom_call_target="tpu_custom_call", output_to_operand_aliasing={{}: (21, {})} | custom-call | tf_op jit(solution)/shard_map/add_exchange_2_1/pallas_call | solution.py:249
  132.6 1.0 slice.40
  133.6 1.0 collective-permute-start.33
  134.6 4.7 %add_exchange_0_0.1.refs_21_ = f32[9,8,32,128]{3,2,1,0:T(8,128)} custom-call(s32[1]{0:T(128)} %bitcast.refs_0_._, s32[12]{0:T(128)} %get-tuple-element.80.refs_1_, s32[12]{0:T(128)} %get-tuple-element.79.refs_2_, f32[12]{0:T(128)} %convert_element_type.10.refs_3_, f32[12]{0:T(128)} %convert_element_type.11.refs_4_, ...), custom_call_target="tpu_custom_call" | custom-call | tf_op jit(solution)/shard_map/add_exchange_0_0/pallas_call | solution.py:249
  139.3 5.0 %add_exchange_1_0.1.refs_21_ = f32[9,8,32,128]{3,2,1,0:T(8,128)} custom-call(s32[1]{0:T(128)} %bitcast.refs_0_._, s32[12]{0:T(128)} %get-tuple-element.80.refs_1_, s32[12]{0:T(128)} %get-tuple-element.79.refs_2_, f32[12]{0:T(128)} %convert_element_type.10.refs_3_, f32[12]{0:T(128)} %convert_element_type.11.refs_4_, ...), custom_call_target="tpu_custom_call", output_to_operand_aliasing={{}: (21, {})} | custom-call | tf_op jit(solution)/shard_map/add_exchange_1_0/pallas_call | solution.py:249
  144.3 5.1 %add_exchange_2_0.1 = f32[9,8,32,128]{3,2,1,0:T(8,128)} custom-call(s32[1]{0:T(128)} %bitcast.refs_0_._, s32[12]{0:T(128)} %get-tuple-element.80.refs_1_, s32[12]{0:T(128)} %get-tuple-element.79.refs_2_, f32[12]{0:T(128)} %convert_element_type.10.refs_3_, f32[12]{0:T(128)} %convert_element_type.11.refs_4_, ...), custom_call_target="tpu_custom_call", output_to_operand_aliasing={{}: (21, {})} | custom-call | tf_op jit(solution)/shard_map/add_exchange_2_0/pallas_call | solution.py:249
  149.4 1.1 slice.37
  150.5 1.2 collective-permute-start.31
  151.8 9.9 %collective-permute-done.31 = f32[3,8,32,128]{3,2,1,0:T(8,128)S(1)} collective-permute-done((f32[3,8,32,128]{3,2,1,0:T(8,128)S(1)}, f32[3,8,32,128]{3,2,1,0:T(8,128)S(1)}, u32[]{:S(2)}, u32[]{:S(2)}) %collective-permute-start.31) | collective-permute-done | bytes 393248 | tf_op jit(solution)/shard_map/ppermute | solution.py:298
  161.7 0.8 slice_add_fusion.2
  162.5 1.9 %collective-permute-done.34 = f32[3,8,32,128]{3,2,1,0:T(8,128)S(1)} collective-permute-done((f32[3,8,32,128]{3,2,1,0:T(8,128)S(1)}, f32[3,8,32,128]{3,2,1,0:T(8,128)S(1)}, u32[]{:S(2)}, u32[]{:S(2)}) %collective-permute-start.34) | collective-permute-done | bytes 393248 | tf_op jit(solution)/shard_map/ppermute | solution.py:22
  164.7 10.3 %collective-permute-done.32 = f32[3,8,32,128]{3,2,1,0:T(8,128)} collective-permute-done((f32[3,8,32,128]{3,2,1,0:T(8,128)}, f32[3,8,32,128]{3,2,1,0:T(8,128)}, u32[]{:S(2)}, u32[]{:S(2)}) %collective-permute-start.32) | collective-permute-done | bytes 393248 | tf_op jit(solution)/shard_map/ppermute | solution.py:22
  174.9 1.1 fusion.4
  176.2 0.9 maximum_multiply_fusion
  (163 shorter events, 11.9 us)
Async XLA Ops:
  0.0 17.9 %copy-start = (s32[24,24]{1,0:T(8,128)S(1)}, s32[24,24]{1,0:T(8,128)}, u32[]{:S(2)}) copy-start(s32[24,24]{1,0:T(8,128)} %param.20) | copy-start | bytes 6916
  1.3 16.5 %copy-start.31 = (s32[24]{0:T(128)S(1)}, s32[24]{0:T(128)}, u32[]{:S(2)}) copy-start(s32[24]{0:T(128)} %constant.128.clone) | copy-start | bytes 292
  1.3 16.5 %copy-start.34 = (s32[24]{0:T(128)S(1)}, s32[24]{0:T(128)}, u32[]{:S(2)}) copy-start(s32[24]{0:T(128)} %constant.130.clone) | copy-start | bytes 292
  1.4 16.5 %copy-start.35 = (s32[24]{0:T(128)S(1)}, s32[24]{0:T(128)}, u32[]{:S(2)}) copy-start(s32[24]{0:T(128)} %constant.129.clone) | copy-start | bytes 292
  1.4 12.0 %collective-permute-start.2 = (f32[3,8,32,128]{3,2,1,0:T(8,128)S(1)}, f32[3,8,32,128]{3,2,1,0:T(8,128)S(1)}, u32[]{:S(2)}, u32[]{:S(2)}) collective-permute-start(f32[3,8,32,128]{3,2,1,0:T(8,128)S(1)} %slice.35), channel_id=1, source_target_pairs={{8,0},{12,4},{16,8},{20,12},{24,16},{28,20},{0,24},{4,28},{9,1},{1... | collective-permute-start | bytes 1179656 | tf_op jit(solution)/shard_map/ppermute | solution.py:22
  5.0 14.2 %copy-start.30 = (s32[24,24]{1,0:T(8,128)S(1)}, s32[24,24]{1,0:T(8,128)}, u32[]{:S(2)}) copy-start(s32[24,24]{1,0:T(8,128)} %constant.131.clone) | copy-start | bytes 6916
  13.5 11.9 %collective-permute-start = (f32[3,8,32,128]{3,2,1,0:T(8,128)S(1)}, f32[3,8,32,128]{3,2,1,0:T(8,128)S(1)}, u32[]{:S(2)}, u32[]{:S(2)}) collective-permute-start(f32[3,8,32,128]{3,2,1,0:T(8,128)S(1)} %get-tuple-element.82), channel_id=1, source_target_pairs={{8,0},{12,4},{16,8},{20,12},{24,16},{28,20},{0,24},{4,28},{9,1},{1... | collective-permute-start | bytes 1179656 | tf_op jit(solution)/shard_map/ppermute | solution.py:22
  18.7 12.0 %collective-permute-start.3 = (f32[3,8,32,128]{3,2,1,0:T(8,128)S(1)}, f32[3,8,32,128]{3,2,1,0:T(8,128)S(1)}, u32[]{:S(2)}, u32[]{:S(2)}) collective-permute-start(f32[3,8,32,128]{3,2,1,0:T(8,128)S(1)} %get-tuple-element.81), channel_id=1, source_target_pairs={{0,4},{4,0},{8,12},{12,8},{16,20},{20,16},{24,28},{28,24},{1,5},{5... | collective-permute-start | bytes 1179656 | tf_op jit(solution)/shard_map/ppermute | solution.py:298
  25.4 18.3 %collective-permute-start.1 = (f32[3,8,32,128]{3,2,1,0:T(8,128)S(1)}, f32[3,8,32,128]{3,2,1,0:T(8,128)S(1)}, u32[]{:S(2)}, u32[]{:S(2)}) collective-permute-start(f32[3,8,32,128]{3,2,1,0:T(8,128)S(1)} %broadcast_select_fusion.1), channel_id=1, source_target_pairs={{0,4},{4,0},{8,12},{12,8},{16,20},{20,16},{24,28},{28,24},{1,5},{5... | collective-permute-start | bytes 1179656 | tf_op jit(solution)/shard_map/ppermute | solution.py:298
  35.8 6.4 %collective-permute-start.23 = (f32[2,16,8,128]{3,2,1,0:T(8,128)}, f32[2,16,8,128]{3,2,1,0:T(8,128)S(1)}, u32[]{:S(2)}, u32[]{:S(2)}) collective-permute-start(f32[2,16,8,128]{3,2,1,0:T(8,128)} %get-tuple-element.68), channel_id=1, source_target_pairs={{1,0},{0,1},{3,2},{2,3},{5,4},{4,5},{7,6},{6,7},{9,8},{8,9},{11,10... | collective-permute-start | bytes 393224 | tf_op jit(solution)/shard_map/ppermute | solution.py:344
  40.0 13.2 %collective-permute-start.25 = (f32[2,16,8,128]{3,2,1,0:T(8,128)S(1)}, f32[2,16,8,128]{3,2,1,0:T(8,128)S(1)}, u32[]{:S(2)}, u32[]{:S(2)}) collective-permute-start(f32[2,16,8,128]{3,2,1,0:T(8,128)S(1)} %copy-done.49), channel_id=1, source_target_pairs={{2,0},{3,1},{0,2},{1,3},{6,4},{7,5},{4,6},{5,7},{10,8},{11,9},{8,1... | collective-permute-start | bytes 393224 | tf_op jit(solution)/shard_map/ppermute | solution.py:344
  41.5 12.3 %collective-permute-start.27 = (f32[2,16,8,128]{3,2,1,0:T(8,128)S(1)}, f32[2,16,8,128]{3,2,1,0:T(8,128)S(1)}, u32[]{:S(2)}, u32[]{:S(2)}) collective-permute-start(f32[2,16,8,128]{3,2,1,0:T(8,128)S(1)} %copy-done.47), channel_id=1, source_target_pairs={{3,0},{2,1},{1,2},{0,3},{7,4},{6,5},{5,6},{4,7},{11,8},{10,9},{9,1... | collective-permute-start | bytes 393224 | tf_op jit(solution)/shard_map/ppermute | solution.py:344
  41.9 13.5 %collective-permute-start.14 = (f32[2,16,8,128]{3,2,1,0:T(8,128)}, f32[2,16,8,128]{3,2,1,0:T(8,128)S(1)}, u32[]{:S(2)}, u32[]{:S(2)}) collective-permute-start(f32[2,16,8,128]{3,2,1,0:T(8,128)} %get-tuple-element.56), channel_id=1, source_target_pairs={{1,0},{0,1},{3,2},{2,3},{5,4},{4,5},{7,6},{6,7},{9,8},{8,9},{11,10... | collective-permute-start | bytes 393224 | tf_op jit(solution)/shard_map/ppermute | solution.py:344
  42.2 13.3 %collective-permute-start.16 = (f32[2,16,8,128]{3,2,1,0:T(8,128)}, f32[2,16,8,128]{3,2,1,0:T(8,128)S(1)}, u32[]{:S(2)}, u32[]{:S(2)}) collective-permute-start(f32[2,16,8,128]{3,2,1,0:T(8,128)} %get-tuple-element.58), channel_id=1, source_target_pairs={{2,0},{3,1},{0,2},{1,3},{6,4},{7,5},{4,6},{5,7},{10,8},{11,9},{8,1... | collective-permute-start | bytes 393224 | tf_op jit(solution)/shard_map/ppermute | solution.py:344
  43.7 12.5 %collective-permute-start.18 = (f32[2,16,8,128]{3,2,1,0:T(8,128)}, f32[2,16,8,128]{3,2,1,0:T(8,128)S(1)}, u32[]{:S(2)}, u32[]{:S(2)}) collective-permute-start(f32[2,16,8,128]{3,2,1,0:T(8,128)} %get-tuple-element.60), channel_id=1, source_target_pairs={{3,0},{2,1},{1,2},{0,3},{7,4},{6,5},{5,6},{4,7},{11,8},{10,9},{9,1... | collective-permute-start | bytes 393224 | tf_op jit(solution)/shard_map/ppermute | solution.py:344
  53.2 12.7 %collective-permute-start.22 = (f32[2,16,8,128]{3,2,1,0:T(8,128)S(1)}, f32[2,16,8,128]{3,2,1,0:T(8,128)S(1)}, u32[]{:S(2)}, u32[]{:S(2)}) collective-permute-start(f32[2,16,8,128]{3,2,1,0:T(8,128)S(1)} %copy-done.48), channel_id=1, source_target_pairs={{1,0},{0,1},{3,2},{2,3},{5,4},{4,5},{7,6},{6,7},{9,8},{8,9},{11,10... | collective-permute-start | bytes 393224 | tf_op jit(solution)/shard_map/ppermute | solution.py:344
  53.9 12.2 %collective-permute-start.24 = (f32[2,16,8,128]{3,2,1,0:T(8,128)S(1)}, f32[2,16,8,128]{3,2,1,0:T(8,128)S(1)}, u32[]{:S(2)}, u32[]{:S(2)}) collective-permute-start(f32[2,16,8,128]{3,2,1,0:T(8,128)S(1)} %copy-done.46), channel_id=1, source_target_pairs={{2,0},{3,1},{0,2},{1,3},{6,4},{7,5},{4,6},{5,7},{10,8},{11,9},{8,1... | collective-permute-start | bytes 393224 | tf_op jit(solution)/shard_map/ppermute | solution.py:344
  55.4 11.3 %collective-permute-start.26 = (f32[2,16,8,128]{3,2,1,0:T(8,128)S(1)}, f32[2,16,8,128]{3,2,1,0:T(8,128)S(1)}, u32[]{:S(2)}, u32[]{:S(2)}) collective-permute-start(f32[2,16,8,128]{3,2,1,0:T(8,128)S(1)} %copy-done.45), channel_id=1, source_target_pairs={{3,0},{2,1},{1,2},{0,3},{7,4},{6,5},{5,6},{4,7},{11,8},{10,9},{9,1... | collective-permute-start | bytes 393224 | tf_op jit(solution)/shard_map/ppermute | solution.py:344
  55.5 12.5 %collective-permute-start.13 = (f32[2,16,8,128]{3,2,1,0:T(8,128)}, f32[2,16,8,128]{3,2,1,0:T(8,128)S(1)}, u32[]{:S(2)}, u32[]{:S(2)}) collective-permute-start(f32[2,16,8,128]{3,2,1,0:T(8,128)} %get-tuple-element.55), channel_id=1, source_target_pairs={{1,0},{0,1},{3,2},{2,3},{5,4},{4,5},{7,6},{6,7},{9,8},{8,9},{11,10... | collective-permute-start | bytes 393224 | tf_op jit(solution)/shard_map/ppermute | solution.py:344
  56.2 12.4 %collective-permute-start.15 = (f32[2,16,8,128]{3,2,1,0:T(8,128)}, f32[2,16,8,128]{3,2,1,0:T(8,128)S(1)}, u32[]{:S(2)}, u32[]{:S(2)}) collective-permute-start(f32[2,16,8,128]{3,2,1,0:T(8,128)} %get-tuple-element.57), channel_id=1, source_target_pairs={{2,0},{3,1},{0,2},{1,3},{6,4},{7,5},{4,6},{5,7},{10,8},{11,9},{8,1... | collective-permute-start | bytes 393224 | tf_op jit(solution)/shard_map/ppermute | solution.py:344
  66.0 19.1 %collective-permute-start.5 = (f32[2,16,8,128]{3,2,1,0:T(8,128)S(1)}, f32[2,16,8,128]{3,2,1,0:T(8,128)S(1)}, u32[]{:S(2)}, u32[]{:S(2)}) collective-permute-start(f32[2,16,8,128]{3,2,1,0:T(8,128)S(1)} %copy-done.44), channel_id=1, source_target_pairs={{1,0},{0,1},{3,2},{2,3},{5,4},{4,5},{7,6},{6,7},{9,8},{8,9},{11,10... | collective-permute-start | bytes 393224 | tf_op jit(solution)/shard_map/ppermute | solution.py:344
  66.1 19.1 %collective-permute-start.7 = (f32[2,16,8,128]{3,2,1,0:T(8,128)S(1)}, f32[2,16,8,128]{3,2,1,0:T(8,128)S(1)}, u32[]{:S(2)}, u32[]{:S(2)}) collective-permute-start(f32[2,16,8,128]{3,2,1,0:T(8,128)S(1)} %copy-done.43), channel_id=1, source_target_pairs={{2,0},{3,1},{0,2},{1,3},{6,4},{7,5},{4,6},{5,7},{10,8},{11,9},{8,1... | collective-permute-start | bytes 393224 | tf_op jit(solution)/shard_map/ppermute | solution.py:344
  66.7 20.1 %collective-permute-start.9 = (f32[2,16,8,128]{3,2,1,0:T(8,128)S(1)}, f32[2,16,8,128]{3,2,1,0:T(8,128)S(1)}, u32[]{:S(2)}, u32[]{:S(2)}) collective-permute-start(f32[2,16,8,128]{3,2,1,0:T(8,128)S(1)} %copy-done.41), channel_id=1, source_target_pairs={{3,0},{2,1},{1,2},{0,3},{7,4},{6,5},{5,6},{4,7},{11,8},{10,9},{9,1... | collective-permute-start | bytes 393224 | tf_op jit(solution)/shard_map/ppermute | solution.py:344
  68.0 9.1 %collective-permute-start.17 = (f32[2,16,8,128]{3,2,1,0:T(8,128)S(1)}, f32[2,16,8,128]{3,2,1,0:T(8,128)S(1)}, u32[]{:S(2)}, u32[]{:S(2)}) collective-permute-start(f32[2,16,8,128]{3,2,1,0:T(8,128)S(1)} %copy-done.42), channel_id=1, source_target_pairs={{3,0},{2,1},{1,2},{0,3},{7,4},{6,5},{5,6},{4,7},{11,8},{10,9},{9,1... | collective-permute-start | bytes 393224 | tf_op jit(solution)/shard_map/ppermute | solution.py:344
  68.6 18.6 %collective-permute-start.4 = (f32[2,16,8,128]{3,2,1,0:T(8,128)}, f32[2,16,8,128]{3,2,1,0:T(8,128)S(1)}, u32[]{:S(2)}, u32[]{:S(2)}) collective-permute-start(f32[2,16,8,128]{3,2,1,0:T(8,128)} %get-tuple-element.43), channel_id=1, source_target_pairs={{1,0},{0,1},{3,2},{2,3},{5,4},{4,5},{7,6},{6,7},{9,8},{8,9},{11,10... | collective-permute-start | bytes 393224 | tf_op jit(solution)/shard_map/ppermute | solution.py:344
  77.1 10.4 %collective-permute-start.6 = (f32[2,16,8,128]{3,2,1,0:T(8,128)}, f32[2,16,8,128]{3,2,1,0:T(8,128)S(1)}, u32[]{:S(2)}, u32[]{:S(2)}) collective-permute-start(f32[2,16,8,128]{3,2,1,0:T(8,128)} %get-tuple-element.45), channel_id=1, source_target_pairs={{2,0},{3,1},{0,2},{1,3},{6,4},{7,5},{4,6},{5,7},{10,8},{11,9},{8,1... | collective-permute-start | bytes 393224 | tf_op jit(solution)/shard_map/ppermute | solution.py:344
  85.0 21.9 %copy-start.36 = (f32[2,16,16,128]{3,2,1,0:T(8,128)S(1)}, f32[2,16,16,128]{3,2,1,0:T(8,128)}, u32[]{:S(2)}) copy-start(f32[2,16,16,128]{3,2,1,0:T(8,128)} %get-tuple-element.64) | copy-start | bytes 786436
  85.1 24.4 %copy-start.33 = (s32[12]{0:T(128)S(1)}, s32[12]{0:T(128)}, u32[]{:S(2)}) copy-start(s32[12]{0:T(128)} %get-tuple-element.77) | copy-start | bytes 148
  85.1 24.9 %copy-start.32 = (s32[12]{0:T(128)S(1)}, s32[12]{0:T(128)}, u32[]{:S(2)}) copy-start(s32[12]{0:T(128)} %get-tuple-element.78) | copy-start | bytes 148
  85.1 18.3 %copy-start.18 = (f32[2,16,8,128]{3,2,1,0:T(8,128)}, f32[2,16,8,128]{3,2,1,0:T(8,128)S(1)}, u32[]{:S(2)}) copy-start(f32[2,16,8,128]{3,2,1,0:T(8,128)S(1)} %collective-permute-done.5.refs_3_) | copy-start | bytes 393220
  85.1 21.8 %collective-permute-start.28 = (f32[2,16,16,128]{3,2,1,0:T(8,128)S(1)}, f32[2,16,16,128]{3,2,1,0:T(8,128)S(1)}, u32[]{:S(2)}, u32[]{:S(2)}) collective-permute-start(f32[2,16,16,128]{3,2,1,0:T(8,128)S(1)} %copy-done.39), channel_id=1, source_target_pairs={{1,0},{0,1},{3,2},{2,3},{5,4},{4,5},{7,6},{6,7},{9,8},{8,9},{11,10... | collective-permute-start | bytes 786440 | tf_op jit(solution)/shard_map/ppermute | solution.py:344
  85.2 18.2 %copy-start.19 = (f32[2,16,8,128]{3,2,1,0:T(8,128)}, f32[2,16,8,128]{3,2,1,0:T(8,128)S(1)}, u32[]{:S(2)}) copy-start(f32[2,16,8,128]{3,2,1,0:T(8,128)S(1)} %collective-permute-done.7.refs_5_) | copy-start | bytes 393220
  85.2 22.3 %collective-permute-start.29 = (f32[2,16,16,128]{3,2,1,0:T(8,128)S(1)}, f32[2,16,16,128]{3,2,1,0:T(8,128)S(1)}, u32[]{:S(2)}, u32[]{:S(2)}) collective-permute-start(f32[2,16,16,128]{3,2,1,0:T(8,128)S(1)} %copy-done.38), channel_id=1, source_target_pairs={{2,0},{3,1},{0,2},{1,3},{6,4},{7,5},{4,6},{5,7},{10,8},{11,9},{8,1... | collective-permute-start | bytes 786440 | tf_op jit(solution)/shard_map/ppermute | solution.py:344
  86.8 16.6 %copy-start.20 = (f32[2,16,8,128]{3,2,1,0:T(8,128)}, f32[2,16,8,128]{3,2,1,0:T(8,128)S(1)}, u32[]{:S(2)}) copy-start(f32[2,16,8,128]{3,2,1,0:T(8,128)S(1)} %collective-permute-done.9.refs_7_) | copy-start | bytes 393220
  86.8 21.0 %collective-permute-start.30 = (f32[2,16,16,128]{3,2,1,0:T(8,128)S(1)}, f32[2,16,16,128]{3,2,1,0:T(8,128)S(1)}, u32[]{:S(2)}, u32[]{:S(2)}) collective-permute-start(f32[2,16,16,128]{3,2,1,0:T(8,128)S(1)} %copy-done.37), channel_id=1, source_target_pairs={{3,0},{2,1},{1,2},{0,3},{7,4},{6,5},{5,6},{4,7},{11,8},{10,9},{9,1... | collective-permute-start | bytes 786440 | tf_op jit(solution)/shard_map/ppermute | solution.py:344
  87.2 16.2 %copy-start.22 = (f32[2,16,8,128]{3,2,1,0:T(8,128)}, f32[2,16,8,128]{3,2,1,0:T(8,128)S(1)}, u32[]{:S(2)}) copy-start(f32[2,16,8,128]{3,2,1,0:T(8,128)S(1)} %collective-permute-done.4.refs_2_) | copy-start | bytes 393220
  87.2 22.0 %collective-permute-start.19 = (f32[2,16,16,128]{3,2,1,0:T(8,128)}, f32[2,16,16,128]{3,2,1,0:T(8,128)S(1)}, u32[]{:S(2)}, u32[]{:S(2)}) collective-permute-start(f32[2,16,16,128]{3,2,1,0:T(8,128)} %get-tuple-element.62), channel_id=1, source_target_pairs={{1,0},{0,1},{3,2},{2,3},{5,4},{4,5},{7,6},{6,7},{9,8},{8,9},{11,10... | collective-permute-start | bytes 786440 | tf_op jit(solution)/shard_map/ppermute | solution.py:344
  87.5 15.9 %copy-start.26 = (f32[2,16,8,128]{3,2,1,0:T(8,128)}, f32[2,16,8,128]{3,2,1,0:T(8,128)S(1)}, u32[]{:S(2)}) copy-start(f32[2,16,8,128]{3,2,1,0:T(8,128)S(1)} %collective-permute-done.6.refs_4_) | copy-start | bytes 393220
  87.5 14.4 %collective-permute-start.8 = (f32[2,16,8,128]{3,2,1,0:T(8,128)S(1)}, f32[2,16,8,128]{3,2,1,0:T(8,128)S(1)}, u32[]{:S(2)}, u32[]{:S(2)}) collective-permute-start(f32[2,16,8,128]{3,2,1,0:T(8,128)S(1)} %copy-done.40), channel_id=1, source_target_pairs={{3,0},{2,1},{1,2},{0,3},{7,4},{6,5},{5,6},{4,7},{11,8},{10,9},{9,1... | collective-permute-start | bytes 393224 | tf_op jit(solution)/shard_map/ppermute | solution.py:344
  101.9 13.4 %collective-permute-start.20 = (f32[2,16,16,128]{3,2,1,0:T(8,128)}, f32[2,16,16,128]{3,2,1,0:T(8,128)S(1)}, u32[]{:S(2)}, u32[]{:S(2)}) collective-permute-start(f32[2,16,16,128]{3,2,1,0:T(8,128)} %get-tuple-element.63), channel_id=1, source_target_pairs={{2,0},{3,1},{0,2},{1,3},{6,4},{7,5},{4,6},{5,7},{10,8},{11,9},{8,1... | collective-permute-start | bytes 786440 | tf_op jit(solution)/shard_map/ppermute | solution.py:344
  107.0 8.9 %collective-permute-start.21 = (f32[2,16,16,128]{3,2,1,0:T(8,128)S(1)}, f32[2,16,16,128]{3,2,1,0:T(8,128)S(1)}, u32[]{:S(2)}, u32[]{:S(2)}) collective-permute-start(f32[2,16,16,128]{3,2,1,0:T(8,128)S(1)} %copy-done.36), channel_id=1, source_target_pairs={{3,0},{2,1},{1,2},{0,3},{7,4},{6,5},{5,6},{4,7},{11,8},{10,9},{9,1... | collective-permute-start | bytes 786440 | tf_op jit(solution)/shard_map/ppermute | solution.py:344
  107.6 14.0 %collective-permute-start.10 = (f32[2,16,16,128]{3,2,1,0:T(8,128)}, f32[2,16,16,128]{3,2,1,0:T(8,128)S(1)}, u32[]{:S(2)}, u32[]{:S(2)}) collective-permute-start(f32[2,16,16,128]{3,2,1,0:T(8,128)} %get-tuple-element.50), channel_id=1, source_target_pairs={{1,0},{0,1},{3,2},{2,3},{5,4},{4,5},{7,6},{6,7},{9,8},{8,9},{11,10... | collective-permute-start | bytes 786440 | tf_op jit(solution)/shard_map/ppermute | solution.py:344
  107.7 14.7 %collective-permute-start.11 = (f32[2,16,16,128]{3,2,1,0:T(8,128)}, f32[2,16,16,128]{3,2,1,0:T(8,128)S(1)}, u32[]{:S(2)}, u32[]{:S(2)}) collective-permute-start(f32[2,16,16,128]{3,2,1,0:T(8,128)} %get-tuple-element.51), channel_id=1, source_target_pairs={{2,0},{3,1},{0,2},{1,3},{6,4},{7,5},{4,6},{5,7},{10,8},{11,9},{8,1... | collective-permute-start | bytes 786440 | tf_op jit(solution)/shard_map/ppermute | solution.py:344
  109.2 17.7 %collective-permute-start.12 = (f32[2,16,16,128]{3,2,1,0:T(8,128)}, f32[2,16,16,128]{3,2,1,0:T(8,128)S(1)}, u32[]{:S(2)}, u32[]{:S(2)}) collective-permute-start(f32[2,16,16,128]{3,2,1,0:T(8,128)} %get-tuple-element.52), channel_id=1, source_target_pairs={{3,0},{2,1},{1,2},{0,3},{7,4},{6,5},{5,6},{4,7},{11,8},{10,9},{9,1... | collective-permute-start | bytes 786440 | tf_op jit(solution)/shard_map/ppermute | solution.py:344
  133.6 18.0 %collective-permute-start.33 = (f32[3,8,32,128]{3,2,1,0:T(8,128)S(1)}, f32[3,8,32,128]{3,2,1,0:T(8,128)S(1)}, u32[]{:S(2)}, u32[]{:S(2)}) collective-permute-start(f32[3,8,32,128]{3,2,1,0:T(8,128)S(1)} %slice.40), channel_id=1, source_target_pairs={{0,4},{4,0},{8,12},{12,8},{16,20},{20,16},{24,28},{28,24},{1,5},{5... | collective-permute-start | bytes 1179656 | tf_op jit(solution)/shard_map/ppermute | solution.py:298
  150.5 11.2 %collective-permute-start.31 = (f32[3,8,32,128]{3,2,1,0:T(8,128)S(1)}, f32[3,8,32,128]{3,2,1,0:T(8,128)S(1)}, u32[]{:S(2)}, u32[]{:S(2)}) collective-permute-start(f32[3,8,32,128]{3,2,1,0:T(8,128)S(1)} %slice.37), channel_id=1, source_target_pairs={{0,4},{4,0},{8,12},{12,8},{16,20},{20,16},{24,28},{28,24},{1,5},{5... | collective-permute-start | bytes 1179656 | tf_op jit(solution)/shard_map/ppermute | solution.py:298
  151.7 12.7 %collective-permute-start.34 = (f32[3,8,32,128]{3,2,1,0:T(8,128)S(1)}, f32[3,8,32,128]{3,2,1,0:T(8,128)S(1)}, u32[]{:S(2)}, u32[]{:S(2)}) collective-permute-start(f32[3,8,32,128]{3,2,1,0:T(8,128)S(1)} %slice_add_fusion), channel_id=1, source_target_pairs={{24,0},{28,4},{0,8},{4,12},{8,16},{12,20},{16,24},{20,28},{25,1},{... | collective-permute-start | bytes 1179656 | tf_op jit(solution)/shard_map/ppermute | solution.py:22
  162.5 12.4 %collective-permute-start.32 = (f32[3,8,32,128]{3,2,1,0:T(8,128)}, f32[3,8,32,128]{3,2,1,0:T(8,128)}, u32[]{:S(2)}, u32[]{:S(2)}) collective-permute-start(f32[3,8,32,128]{3,2,1,0:T(8,128)} %slice_add_fusion.2), channel_id=1, source_target_pairs={{24,0},{28,4},{0,8},{4,12},{8,16},{12,20},{16,24},{20,28},{25,1},{... | collective-permute-start | bytes 1179656 | tf_op jit(solution)/shard_map/ppermute | solution.py:22
  (37 other events, 214.5 us)

commit v4 on v2

--- a/solution.py
+++ b/solution.py
@@ -290,14 +290,39 @@
     return jnp.where(squared > 0, scale / safe, 0.0)
 
 
+def pair_swap(block):
+    return lax.ppermute(block, "band", [(i, i ^ 1) for i in range(lax.axis_size("band"))])
+
+
+def visiting(own):
+    if REACH != 2 or lax.axis_size("band") % 2:
+        return [shifted(own, "band", -d) for d in range(1, REACH + 1)]
+    even = lax.axis_index("band") % 2 == 0
+    second = shifted(own, "band", -2)
+    return [pair_swap(jnp.where(even, second, own)), second]
+
+
+def collected(totals, at):
+    pieces = [totals[d * ORB_DEV + at : d * ORB_DEV + at + 1] for d in range(REACH + 1)]
+    if REACH != 2 or lax.axis_size("band") % 2:
+        owned = pieces[0]
+        for d in range(1, REACH + 1):
+            owned = owned + shifted(pieces[d], "band", d)
+        return owned
+    even = lax.axis_index("band") % 2 == 0
+    swapped = pair_swap(pieces[1])
+    ahead = shifted(pieces[2] + jnp.where(even, swapped, 0.0), "band", 2)
+    return pieces[0] + jnp.where(even, 0.0, swapped) + ahead
+
+
 def local(orbitals, pair_mask):
     orb_count, planes, cells = orbitals.shape
     n = math.isqrt(cells)
     parts = lax.axis_size("grid")
     tables = dft_tables(n, parts)
     own = orbitals.reshape(orb_count, planes, n // 2, 2 * n)
-    visits = [own] + [shifted(own, "band", -d) for d in range(1, REACH + 1)]
-    flat = jnp.concatenate(visits, axis=0)
+    visits = [visiting(own[a : a + 1]) for a in range(orb_count)]
+    flat = jnp.concatenate([own] + [v[d] for d in range(REACH) for v in visits], axis=0)
     me = lax.axis_index("grid").astype(jnp.int32).reshape(1)
     scalars = (me, *live_pairs(pair_mask))
     kernel = green_kernel(n, n // parts)
@@ -320,9 +345,7 @@
     totals = None
     for g in turns:
         totals = add_exchange(g, scalars, returned[g], flat, totals, tables)
-    owned = totals[:orb_count]
-    for d in range(1, REACH + 1):
-        owned = owned + shifted(totals[d * orb_count : (d + 1) * orb_count], "band", d)
+    owned = jnp.concatenate([collected(totals, a) for a in range(orb_count)], axis=0)
     return (-MIXING * owned).reshape(orb_count, planes, cells)
 
 

time: 170 us -> 165 us (0.971); the launches traced: 170 us -> 162 us
  starting transfers between devices: 35.9 us -> 29 us
  waiting for transfers between devices: 70.7 us -> 64.9 us
  other arithmetic: 6.47 us -> 11.6 us
    ppermute x4 -> x6, waiting for transfers between devices: 50 us -> 26.9 us  [shifted(): lax.ppermute(block, axis, [((i - distance) % count, i) for i in range(cou...]
    ppermute x0 -> x6, waiting for transfers between devices: none -> 18.5 us  [pair_swap(): lax.ppermute(block, 'band', [(i, i ^ 1) for i in range(lax.axis_size('ban...]
    ppermute x4 -> x6, starting transfers between devices: 21.9 us -> 9.83 us  [shifted(): lax.ppermute(block, axis, [((i - distance) % count, i) for i in range(cou...]
    ppermute x0 -> x6, starting transfers between devices: none -> 4.43 us  [pair_swap(): lax.ppermute(block, 'band', [(i, i ^ 1) for i in range(lax.axis_size('ban...]
    select_n x0 -> x3, other arithmetic: none -> 4.17 us  [visiting(): return [pair_swap(jnp.where(even, second, own)), second]]
    add x0 -> x3, other arithmetic: none -> 3.51 us  [the longest x2 2.3 us: collected(): return pieces[0] + jnp.where(even, 0.0, swapped) + ahead]
    unnamed x51 -> x79, local copies, waits for them, and re-layouts: 5.39 us -> 8.67 us
  transfers between devices with their start and end apart: 22 -> 30, of which waited for: 10 -> 19; matrix products, arithmetic and copies ran while one was open for 4% -> 7% of each run, Pallas kernels for 20% -> 21%
where the time goes in v4:
time: 165 us; the launch traced here: 162 us
  waiting for transfers between devices  64.9 us (39%)
  Pallas kernels  45.9 us (28%)
  starting transfers between devices  29 us (18%)
  other arithmetic  11.6 us (7%)
  local copies, waits for them, and re-layouts  10.8 us (7%)
    ppermute x6, waiting for transfers between devices, shifted(): lax.ppermute(block, axis, [((i - distance) % count, i) for i in range(cou...  26.9 us
    ppermute x18, waiting for transfers between devices, exchange(): moved.append(lax.ppermute(blocks[back], 'grid', route))  19.5 us
    pallas_call x3, Pallas kernels, add_exchange(): pl.pallas_call(body, grid_spec=pltpu.PrefetchScalarGridSpec(num_scalar_pr...  19.2 us
    ppermute x6, waiting for transfers between devices, pair_swap(): lax.ppermute(block, 'band', [(i, i ^ 1) for i in range(lax.axis_size('ban...  18.5 us
    pallas_call x3, Pallas kernels, forward_planes(): pl.pallas_call(body, grid_spec=pltpu.PrefetchScalarGridSpec(num_scalar_pr...  16.1 us
    ppermute x18, starting transfers between devices, exchange(): moved.append(lax.ppermute(blocks[back], 'grid', route))  14.7 us
    pallas_call x3, Pallas kernels, solve_columns(): pl.pallas_call(body, grid_spec=pltpu.PrefetchScalarGridSpec(num_scalar_pr...  10.5 us
    ppermute x6, starting transfers between devices, shifted(): lax.ppermute(block, axis, [((i - distance) % count, i) for i in range(cou...  9.83 us
  transfers between devices with their start and end apart: 30, of which 19 were waited for; matrix products, arithmetic and copies ran while one was open for 7% of the time, Pallas kernels for 21%

profile of v4, /device:TPU:4, one launch (start us, length us, event | category | flops | bytes accessed | tf_op | source)
XLA Modules:
  0.0 162.5 jit_solution(17108254529464434305)
XLA Ops:
  0.0 1.2 slice_bitcast_fusion
  2.0 3.6 %collective-permute-start = (f32[1,16,32,128]{3,2,1,0:T(8,128)}, f32[1,16,32,128]{3,2,1,0:T(8,128)S(1)}, u32[]{:S(2)}, u32[]{:S(2)}) collective-permute-start(f32[1,16,32,128]{3,2,1,0:T(8,128)} %bitcast.8), channel_id=1, source_target_pairs={{8,0},{12,4},{16,8},{20,12},{24,16},{28,20},{0,24},{4,28},{9,1},{1... | collective-permute-start | bytes 786440 | tf_op jit(solution)/shard_map/ppermute | solution.py:22
  9.3 3.4 %collective-permute-done = f32[1,16,32,128]{3,2,1,0:T(8,128)S(1)} collective-permute-done((f32[1,16,32,128]{3,2,1,0:T(8,128)}, f32[1,16,32,128]{3,2,1,0:T(8,128)S(1)}, u32[]{:S(2)}, u32[]{:S(2)}) %collective-permute-start) | collective-permute-done | bytes 262176 | tf_op jit(solution)/shard_map/ppermute | solution.py:22
  12.7 1.7 %broadcast_select_fusion.2 = f32[1,16,32,128]{3,2,1,0:T(8,128)} fusion(f32[1,16,32,128]{3,2,1,0:T(8,128)S(1)} %collective-permute-done, pred[]{:T(512)S(6)} %eq.35, f32[1,16,32,128]{3,2,1,0:T(8,128)} %bitcast.33), kind=kLoop, calls=%fused_computation.22 | loop fusion | flops 65536 | bytes 786433 | tf_op jit(solution)/shard_map/jit(_where)/select_n | solution.py:302
  14.4 3.9 %collective-permute-done.2 = f32[1,16,32,128]{3,2,1,0:T(8,128)S(1)} collective-permute-done((f32[1,16,32,128]{3,2,1,0:T(8,128)}, f32[1,16,32,128]{3,2,1,0:T(8,128)S(1)}, u32[]{:S(2)}, u32[]{:S(2)}) %collective-permute-start.2) | collective-permute-done | bytes 262176 | tf_op jit(solution)/shard_map/ppermute | solution.py:22
  18.3 1.7 %broadcast_select_fusion.1 = f32[1,16,32,128]{3,2,1,0:T(8,128)} fusion(f32[1,16,32,128]{3,2,1,0:T(8,128)S(1)} %collective-permute-done.2, pred[]{:T(512)S(6)} %eq.35, f32[1,16,32,128]{3,2,1,0:T(8,128)} %bitcast.32), kind=kLoop, calls=%fused_computation.21 | loop fusion | flops 65536 | bytes 786433 | tf_op jit(solution)/shard_map/jit(_where)/select_n | solution.py:302
  20.0 2.7 %collective-permute-done.4 = f32[1,16,32,128]{3,2,1,0:T(8,128)S(1)} collective-permute-done((f32[1,16,32,128]{3,2,1,0:T(8,128)S(1)}, f32[1,16,32,128]{3,2,1,0:T(8,128)S(1)}, u32[]{:S(2)}, u32[]{:S(2)}) %collective-permute-start.4) | collective-permute-done | bytes 262176 | tf_op jit(solution)/shard_map/ppermute | solution.py:22
  23.9 1.0 constant_dynamic-update-slice_fusion.5
  24.9 3.2 %collective-permute-done.3 = f32[1,16,32,128]{3,2,1,0:T(8,128)} collective-permute-done((f32[1,16,32,128]{3,2,1,0:T(8,128)}, f32[1,16,32,128]{3,2,1,0:T(8,128)}, u32[]{:S(2)}, u32[]{:S(2)}) %collective-permute-start.3) | collective-permute-done | bytes 262176 | tf_op jit(solution)/shard_map/ppermute | solution.py:294
  28.1 1.0 constant_dynamic-update-slice_fusion.4
  29.0 3.2 %collective-permute-done.5 = f32[1,16,32,128]{3,2,1,0:T(8,128)S(1)} collective-permute-done((f32[1,16,32,128]{3,2,1,0:T(8,128)}, f32[1,16,32,128]{3,2,1,0:T(8,128)S(1)}, u32[]{:S(2)}, u32[]{:S(2)}) %collective-permute-start.5) | collective-permute-done | bytes 262176 | tf_op jit(solution)/shard_map/ppermute | solution.py:294
  32.3 1.4 copy-done.1
  33.7 5.3 %forward_planes_0.1 = (f32[2,16,16,128]{3,2,1,0:T(8,128)}, f32[2,16,16,128]{3,2,1,0:T(8,128)}, f32[2,16,16,128]{3,2,1,0:T(8,128)}, f32[2,16,16,128]{3,2,1,0:T(8,128)}) custom-call(s32[1]{0:T(128)} %bitcast.refs_0_._, s32[12]{0:T(128)} %get-tuple-element.56.refs_1_, s32[12]{0:T(128)} %get-tuple-element.55.refs_2_, f32[9,16,32,128]{3,2,1,0:T(8,128)} %copy-done.1, ...), custom_call_target="tpu_custom_call" | custom-call | tf_op jit(solution)/shard_map/forward_planes_0/pallas_call | solution.py:148
  39.1 1.6 collective-permute-start.19
  41.0 5.3 %forward_planes_1.1 = (f32[2,16,16,128]{3,2,1,0:T(8,128)}, f32[2,16,16,128]{3,2,1,0:T(8,128)}, f32[2,16,16,128]{3,2,1,0:T(8,128)}, f32[2,16,16,128]{3,2,1,0:T(8,128)}) custom-call(s32[1]{0:T(128)} %bitcast.refs_0_._, s32[12]{0:T(128)} %get-tuple-element.56.refs_1_, s32[12]{0:T(128)} %get-tuple-element.55.refs_2_, f32[9,16,32,128]{3,2,1,0:T(8,128)} %copy-done.1, ...), custom_call_target="tpu_custom_call" | custom-call | tf_op jit(solution)/shard_map/forward_planes_1/pallas_call | solution.py:148
  46.4 5.5 %forward_planes_2.1 = (f32[2,16,16,128]{3,2,1,0:T(8,128)}, f32[2,16,16,128]{3,2,1,0:T(8,128)}, f32[2,16,16,128]{3,2,1,0:T(8,128)}, f32[2,16,16,128]{3,2,1,0:T(8,128)}) custom-call(s32[1]{0:T(128)} %bitcast.refs_0_._, s32[12]{0:T(128)} %get-tuple-element.56.refs_1_, s32[12]{0:T(128)} %get-tuple-element.55.refs_2_, f32[9,16,32,128]{3,2,1,0:T(8,128)} %copy-done.1, ...), custom_call_target="tpu_custom_call" | custom-call | tf_op jit(solution)/shard_map/forward_planes_2/pallas_call | solution.py:148
  52.3 1.5 collective-permute-start.13
  54.5 1.5 collective-permute-start.7
  56.0 1.0 fusion.2.refs_4_
  57.0 3.5 %solve_columns_0.1 = (f32[2,16,16,128]{3,2,1,0:T(8,128)}, f32[2,16,16,128]{3,2,1,0:T(8,128)}, f32[2,16,16,128]{3,2,1,0:T(8,128)}, f32[2,16,16,128]{3,2,1,0:T(8,128)}) custom-call(s32[1]{0:T(128)} %bitcast.refs_0_._, f32[2,16,16,128]{3,2,1,0:T(8,128)} %get-tuple-element.45.refs_0_, f32[2,16,16,128]{3,2,1,0:T(8,128)} %copy-done.18, ...), custom_call_target="tpu_custom_call" | custom-call | tf_op jit(solution)/shard_map/solve_columns_0/pallas_call | solution.py:186
  61.5 4.6 %collective-permute-done.14.refs_3_ = f32[2,16,16,128]{3,2,1,0:T(8,128)S(1)} collective-permute-done((f32[2,16,16,128]{3,2,1,0:T(8,128)S(1)}, f32[2,16,16,128]{3,2,1,0:T(8,128)S(1)}, u32[]{:S(2)}, u32[]{:S(2)}) %collective-permute-start.14) | collective-permute-done | bytes 262176 | tf_op jit(solution)/shard_map/ppermute | solution.py:337
  66.9 3.5 %solve_columns_1.1 = (f32[2,16,16,128]{3,2,1,0:T(8,128)}, f32[2,16,16,128]{3,2,1,0:T(8,128)}, f32[2,16,16,128]{3,2,1,0:T(8,128)}, f32[2,16,16,128]{3,2,1,0:T(8,128)}) custom-call(s32[1]{0:T(128)} %bitcast.refs_0_._, f32[2,16,16,128]{3,2,1,0:T(8,128)} %get-tuple-element.37.refs_0_, f32[2,16,16,128]{3,2,1,0:T(8,128)} %copy-done.16, ...), custom_call_target="tpu_custom_call" | custom-call | tf_op jit(solution)/shard_map/solve_columns_1/pallas_call | solution.py:186
  70.5 1.8 %collective-permute-start.23 = (f32[2,16,16,128]{3,2,1,0:T(8,128)}, f32[2,16,16,128]{3,2,1,0:T(8,128)S(1)}, u32[]{:S(2)}, u32[]{:S(2)}) collective-permute-start(f32[2,16,16,128]{3,2,1,0:T(8,128)} %get-tuple-element.52), channel_id=1, source_target_pairs={{3,0},{2,1},{1,2},{0,3},{7,4},{6,5},{5,6},{4,7},{11,8},{10,9},{9,1... | collective-permute-start | bytes 786440 | tf_op jit(solution)/shard_map/ppermute | solution.py:337
  72.7 4.6 %collective-permute-done.8.refs_3_ = f32[2,16,16,128]{3,2,1,0:T(8,128)S(1)} collective-permute-done((f32[2,16,16,128]{3,2,1,0:T(8,128)S(1)}, f32[2,16,16,128]{3,2,1,0:T(8,128)S(1)}, u32[]{:S(2)}, u32[]{:S(2)}) %collective-permute-start.8) | collective-permute-done | bytes 262176 | tf_op jit(solution)/shard_map/ppermute | solution.py:337
  78.2 3.5 %solve_columns_2.1 = (f32[2,16,16,128]{3,2,1,0:T(8,128)}, f32[2,16,16,128]{3,2,1,0:T(8,128)}, f32[2,16,16,128]{3,2,1,0:T(8,128)}, f32[2,16,16,128]{3,2,1,0:T(8,128)}) custom-call(s32[1]{0:T(128)} %bitcast.refs_0_._, f32[2,16,16,128]{3,2,1,0:T(8,128)} %get-tuple-element.29.refs_0_, f32[2,16,16,128]{3,2,1,0:T(8,128)} %copy-done.14, ...), custom_call_target="tpu_custom_call" | custom-call | tf_op jit(solution)/shard_map/solve_columns_2/pallas_call | solution.py:186
  81.7 1.8 %collective-permute-start.17 = (f32[2,16,16,128]{3,2,1,0:T(8,128)}, f32[2,16,16,128]{3,2,1,0:T(8,128)S(1)}, u32[]{:S(2)}, u32[]{:S(2)}) collective-permute-start(f32[2,16,16,128]{3,2,1,0:T(8,128)} %get-tuple-element.44), channel_id=1, source_target_pairs={{3,0},{2,1},{1,2},{0,3},{7,4},{6,5},{5,6},{4,7},{11,8},{10,9},{9,1... | collective-permute-start | bytes 786440 | tf_op jit(solution)/shard_map/ppermute | solution.py:337
  83.9 1.5 collective-permute-start.10
  85.4 3.2 %collective-permute-done.23.refs_8_ = f32[2,16,16,128]{3,2,1,0:T(8,128)S(1)} collective-permute-done((f32[2,16,16,128]{3,2,1,0:T(8,128)}, f32[2,16,16,128]{3,2,1,0:T(8,128)S(1)}, u32[]{:S(2)}, u32[]{:S(2)}) %collective-permute-start.23) | collective-permute-done | bytes 262176 | tf_op jit(solution)/shard_map/ppermute | solution.py:337
  88.7 1.8 %collective-permute-start.11 = (f32[2,16,16,128]{3,2,1,0:T(8,128)}, f32[2,16,16,128]{3,2,1,0:T(8,128)S(1)}, u32[]{:S(2)}, u32[]{:S(2)}) collective-permute-start(f32[2,16,16,128]{3,2,1,0:T(8,128)} %get-tuple-element.36), channel_id=1, source_target_pairs={{3,0},{2,1},{1,2},{0,3},{7,4},{6,5},{5,6},{4,7},{11,8},{10,9},{9,1... | collective-permute-start | bytes 786440 | tf_op jit(solution)/shard_map/ppermute | solution.py:337
  91.6 6.2 %add_exchange_0.1.refs_21_ = f32[9,16,32,128]{3,2,1,0:T(8,128)} custom-call(s32[1]{0:T(128)} %bitcast.refs_0_._, s32[12]{0:T(128)} %get-tuple-element.56.refs_1_, s32[12]{0:T(128)} %get-tuple-element.55.refs_2_, f32[12]{0:T(128)} %convert_element_type.10.refs_3_, f32[12]{0:T(128)} %convert_element_type.11.refs_4_, ...), custom_call_target="tpu_custom_call" | custom-call | tf_op jit(solution)/shard_map/add_exchange_0/pallas_call | solution.py:245
  97.8 2.1 %collective-permute-done.17.refs_8_ = f32[2,16,16,128]{3,2,1,0:T(8,128)S(1)} collective-permute-done((f32[2,16,16,128]{3,2,1,0:T(8,128)}, f32[2,16,16,128]{3,2,1,0:T(8,128)S(1)}, u32[]{:S(2)}, u32[]{:S(2)}) %collective-permute-start.17) | collective-permute-done | bytes 262176 | tf_op jit(solution)/shard_map/ppermute | solution.py:337
  100.6 6.5 %add_exchange_1.1.refs_21_ = f32[9,16,32,128]{3,2,1,0:T(8,128)} custom-call(s32[1]{0:T(128)} %bitcast.refs_0_._, s32[12]{0:T(128)} %get-tuple-element.56.refs_1_, s32[12]{0:T(128)} %get-tuple-element.55.refs_2_, f32[12]{0:T(128)} %convert_element_type.10.refs_3_, f32[12]{0:T(128)} %convert_element_type.11.refs_4_, ...), custom_call_target="tpu_custom_call", output_to_operand_aliasing={{}: (21, {})} | custom-call | tf_op jit(solution)/shard_map/add_exchange_1/pallas_call | solution.py:245
  107.2 3.2 %collective-permute-done.11.refs_8_ = f32[2,16,16,128]{3,2,1,0:T(8,128)S(1)} collective-permute-done((f32[2,16,16,128]{3,2,1,0:T(8,128)}, f32[2,16,16,128]{3,2,1,0:T(8,128)S(1)}, u32[]{:S(2)}, u32[]{:S(2)}) %collective-permute-start.11) | collective-permute-done | bytes 262176 | tf_op jit(solution)/shard_map/ppermute | solution.py:337
  111.2 6.5 %add_exchange_2.1 = f32[9,16,32,128]{3,2,1,0:T(8,128)} custom-call(s32[1]{0:T(128)} %bitcast.refs_0_._, s32[12]{0:T(128)} %get-tuple-element.56.refs_1_, s32[12]{0:T(128)} %get-tuple-element.55.refs_2_, f32[12]{0:T(128)} %convert_element_type.10.refs_3_, f32[12]{0:T(128)} %convert_element_type.11.refs_4_, ...), custom_call_target="tpu_custom_call", output_to_operand_aliasing={{}: (21, {})} | custom-call | tf_op jit(solution)/shard_map/add_exchange_2/pallas_call | solution.py:245
  117.7 1.1 slice.63
  118.8 1.9 %collective-permute-start.24 = (f32[1,16,32,128]{3,2,1,0:T(8,128)S(1)}, f32[1,16,32,128]{3,2,1,0:T(8,128)S(1)}, u32[]{:S(2)}, u32[]{:S(2)}) collective-permute-start(f32[1,16,32,128]{3,2,1,0:T(8,128)S(1)} %slice.63), channel_id=1, source_target_pairs={{0,4},{4,0},{8,12},{12,8},{16,20},{20,16},{24,28},{28,24},{1,5},{5... | collective-permute-start | bytes 786440 | tf_op jit(solution)/shard_map/ppermute | solution.py:294
  120.7 7.1 %collective-permute-done.24 = f32[1,16,32,128]{3,2,1,0:T(8,128)S(1)} collective-permute-done((f32[1,16,32,128]{3,2,1,0:T(8,128)S(1)}, f32[1,16,32,128]{3,2,1,0:T(8,128)S(1)}, u32[]{:S(2)}, u32[]{:S(2)}) %collective-permute-start.24) | collective-permute-done | bytes 262176 | tf_op jit(solution)/shard_map/ppermute | solution.py:294
  127.8 1.2 slice_add_fusion.4
  129.1 2.1 %collective-permute-start.25 = (f32[1,16,32,128]{3,2,1,0:T(8,128)S(1)}, f32[1,16,32,128]{3,2,1,0:T(8,128)S(1)}, u32[]{:S(2)}, u32[]{:S(2)}) collective-permute-start(f32[1,16,32,128]{3,2,1,0:T(8,128)S(1)} %get-tuple-element.60), channel_id=1, source_target_pairs={{24,0},{28,4},{0,8},{4,12},{8,16},{12,20},{16,24},{20,28},{25,1},{... | collective-permute-start | bytes 786440 | tf_op jit(solution)/shard_map/ppermute | solution.py:22
  131.5 1.7 %collective-permute-start.28 = (f32[1,16,32,128]{3,2,1,0:T(8,128)S(1)}, f32[1,16,32,128]{3,2,1,0:T(8,128)S(1)}, u32[]{:S(2)}, u32[]{:S(2)}) collective-permute-start(f32[1,16,32,128]{3,2,1,0:T(8,128)S(1)} %get-tuple-element.61), channel_id=1, source_target_pairs={{0,4},{4,0},{8,12},{12,8},{16,20},{20,16},{24,28},{28,24},{1,5},{5... | collective-permute-start | bytes 786440 | tf_op jit(solution)/shard_map/ppermute | solution.py:294
  133.2 6.2 %collective-permute-done.25 = f32[1,16,32,128]{3,2,1,0:T(8,128)S(1)} collective-permute-done((f32[1,16,32,128]{3,2,1,0:T(8,128)S(1)}, f32[1,16,32,128]{3,2,1,0:T(8,128)S(1)}, u32[]{:S(2)}, u32[]{:S(2)}) %collective-permute-start.25) | collective-permute-done | bytes 262176 | tf_op jit(solution)/shard_map/ppermute | solution.py:22
  140.4 4.2 %collective-permute-done.28 = f32[1,16,32,128]{3,2,1,0:T(8,128)S(1)} collective-permute-done((f32[1,16,32,128]{3,2,1,0:T(8,128)S(1)}, f32[1,16,32,128]{3,2,1,0:T(8,128)S(1)}, u32[]{:S(2)}, u32[]{:S(2)}) %collective-permute-start.28) | collective-permute-done | bytes 262176 | tf_op jit(solution)/shard_map/ppermute | solution.py:294
  144.5 1.0 fusion.5
  145.9 2.8 %collective-permute-start.29 = (f32[1,16,32,128]{3,2,1,0:T(8,128)}, f32[1,16,32,128]{3,2,1,0:T(8,128)}, u32[]{:S(2)}, u32[]{:S(2)}) collective-permute-start(f32[1,16,32,128]{3,2,1,0:T(8,128)} %get-tuple-element.58), channel_id=1, source_target_pairs={{24,0},{28,4},{0,8},{4,12},{8,16},{12,20},{16,24},{20,28},{25,1},{... | collective-permute-start | bytes 786440 | tf_op jit(solution)/shard_map/ppermute | solution.py:22
  148.7 8.0 %collective-permute-done.27 = f32[1,16,32,128]{3,2,1,0:T(8,128)S(1)} collective-permute-done((f32[1,16,32,128]{3,2,1,0:T(8,128)}, f32[1,16,32,128]{3,2,1,0:T(8,128)S(1)}, u32[]{:S(2)}, u32[]{:S(2)}) %collective-permute-start.27) | collective-permute-done | bytes 262176 | tf_op jit(solution)/shard_map/ppermute | solution.py:22
  157.4 2.7 %collective-permute-done.29 = f32[1,16,32,128]{3,2,1,0:T(8,128)} collective-permute-done((f32[1,16,32,128]{3,2,1,0:T(8,128)}, f32[1,16,32,128]{3,2,1,0:T(8,128)}, u32[]{:S(2)}, u32[]{:S(2)}) %collective-permute-start.29) | collective-permute-done | bytes 262176 | tf_op jit(solution)/shard_map/ppermute | solution.py:22
  160.1 1.3 fusion.4
  161.6 0.9 maximum_multiply_fusion
  (123 shorter events, 15.8 us)
Async XLA Ops:
  0.0 7.4 %copy-start = (s32[24,24]{1,0:T(8,128)S(1)}, s32[24,24]{1,0:T(8,128)}, u32[]{:S(2)}) copy-start(s32[24,24]{1,0:T(8,128)} %param.20) | copy-start | bytes 6916
  0.0 7.4 %copy-start.25 = (s32[24]{0:T(128)S(1)}, s32[24]{0:T(128)}, u32[]{:S(2)}) copy-start(s32[24]{0:T(128)} %constant.132.clone) | copy-start | bytes 292
  0.0 7.4 %copy-start.28 = (s32[24]{0:T(128)S(1)}, s32[24]{0:T(128)}, u32[]{:S(2)}) copy-start(s32[24]{0:T(128)} %constant.133.clone) | copy-start | bytes 292
  0.0 7.4 %copy-start.29 = (s32[24]{0:T(128)S(1)}, s32[24]{0:T(128)}, u32[]{:S(2)}) copy-start(s32[24]{0:T(128)} %constant.134.clone) | copy-start | bytes 292
  0.0 8.2 %copy-start.24 = (s32[24,24]{1,0:T(8,128)S(1)}, s32[24,24]{1,0:T(8,128)}, u32[]{:S(2)}) copy-start(s32[24,24]{1,0:T(8,128)} %constant.135.clone) | copy-start | bytes 6916
  0.0 8.3 %copy-start.3 = (f32[3,16,4096]{2,1,0:T(8,128)S(1)}, f32[3,16,4096]{2,1,0:T(8,128)}, u32[]{:S(2)}) copy-start(f32[3,16,4096]{2,1,0:T(8,128)} %param.19) | copy-start | bytes 2359300
  2.0 10.6 %collective-permute-start = (f32[1,16,32,128]{3,2,1,0:T(8,128)}, f32[1,16,32,128]{3,2,1,0:T(8,128)S(1)}, u32[]{:S(2)}, u32[]{:S(2)}) collective-permute-start(f32[1,16,32,128]{3,2,1,0:T(8,128)} %bitcast.8), channel_id=1, source_target_pairs={{8,0},{12,4},{16,8},{20,12},{24,16},{28,20},{0,24},{4,28},{9,1},{1... | collective-permute-start | bytes 786440 | tf_op jit(solution)/shard_map/ppermute | solution.py:22
  6.4 11.9 %collective-permute-start.2 = (f32[1,16,32,128]{3,2,1,0:T(8,128)}, f32[1,16,32,128]{3,2,1,0:T(8,128)S(1)}, u32[]{:S(2)}, u32[]{:S(2)}) collective-permute-start(f32[1,16,32,128]{3,2,1,0:T(8,128)} %bitcast.12), channel_id=1, source_target_pairs={{8,0},{12,4},{16,8},{20,12},{24,16},{28,20},{0,24},{4,28},{9,1},{1... | collective-permute-start | bytes 786440 | tf_op jit(solution)/shard_map/ppermute | solution.py:22
  6.9 15.7 %collective-permute-start.4 = (f32[1,16,32,128]{3,2,1,0:T(8,128)S(1)}, f32[1,16,32,128]{3,2,1,0:T(8,128)S(1)}, u32[]{:S(2)}, u32[]{:S(2)}) collective-permute-start(f32[1,16,32,128]{3,2,1,0:T(8,128)S(1)} %bitcast.36), channel_id=1, source_target_pairs={{8,0},{12,4},{16,8},{20,12},{24,16},{28,20},{0,24},{4,28},{9,1},{1... | collective-permute-start | bytes 786440 | tf_op jit(solution)/shard_map/ppermute | solution.py:22
  14.4 9.6 %collective-permute-start.1 = (f32[1,16,32,128]{3,2,1,0:T(8,128)}, f32[1,16,32,128]{3,2,1,0:T(8,128)}, u32[]{:S(2)}, u32[]{:S(2)}) collective-permute-start(f32[1,16,32,128]{3,2,1,0:T(8,128)} %broadcast_select_fusion.2), channel_id=1, source_target_pairs={{0,4},{4,0},{8,12},{12,8},{16,20},{20,16},{24,28},{28,24},{1,5},{5... | collective-permute-start | bytes 786440 | tf_op jit(solution)/shard_map/ppermute | solution.py:294
  20.0 8.1 %collective-permute-start.3 = (f32[1,16,32,128]{3,2,1,0:T(8,128)}, f32[1,16,32,128]{3,2,1,0:T(8,128)}, u32[]{:S(2)}, u32[]{:S(2)}) collective-permute-start(f32[1,16,32,128]{3,2,1,0:T(8,128)} %broadcast_select_fusion.1), channel_id=1, source_target_pairs={{0,4},{4,0},{8,12},{12,8},{16,20},{20,16},{24,28},{28,24},{1,5},{5... | collective-permute-start | bytes 786440 | tf_op jit(solution)/shard_map/ppermute | solution.py:294
  23.4 8.8 %collective-permute-start.5 = (f32[1,16,32,128]{3,2,1,0:T(8,128)}, f32[1,16,32,128]{3,2,1,0:T(8,128)S(1)}, u32[]{:S(2)}, u32[]{:S(2)}) collective-permute-start(f32[1,16,32,128]{3,2,1,0:T(8,128)} %broadcast_select_fusion), channel_id=1, source_target_pairs={{0,4},{4,0},{8,12},{12,8},{16,20},{20,16},{24,28},{28,24},{1,5},{5... | collective-permute-start | bytes 786440 | tf_op jit(solution)/shard_map/ppermute | solution.py:294
  39.0 14.7 %collective-permute-start.18 = (f32[2,16,16,128]{3,2,1,0:T(8,128)}, f32[2,16,16,128]{3,2,1,0:T(8,128)S(1)}, u32[]{:S(2)}, u32[]{:S(2)}) collective-permute-start(f32[2,16,16,128]{3,2,1,0:T(8,128)} %get-tuple-element.46), channel_id=1, source_target_pairs={{1,0},{0,1},{3,2},{2,3},{5,4},{4,5},{7,6},{6,7},{9,8},{8,9},{11,10... | collective-permute-start | bytes 786440 | tf_op jit(solution)/shard_map/ppermute | solution.py:337
  39.1 14.8 %collective-permute-start.19 = (f32[2,16,16,128]{3,2,1,0:T(8,128)}, f32[2,16,16,128]{3,2,1,0:T(8,128)S(1)}, u32[]{:S(2)}, u32[]{:S(2)}) collective-permute-start(f32[2,16,16,128]{3,2,1,0:T(8,128)} %get-tuple-element.47), channel_id=1, source_target_pairs={{2,0},{3,1},{0,2},{1,3},{6,4},{7,5},{4,6},{5,7},{10,8},{11,9},{8,1... | collective-permute-start | bytes 786440 | tf_op jit(solution)/shard_map/ppermute | solution.py:337
  40.7 13.8 %collective-permute-start.20 = (f32[2,16,16,128]{3,2,1,0:T(8,128)}, f32[2,16,16,128]{3,2,1,0:T(8,128)S(1)}, u32[]{:S(2)}, u32[]{:S(2)}) collective-permute-start(f32[2,16,16,128]{3,2,1,0:T(8,128)} %get-tuple-element.48), channel_id=1, source_target_pairs={{3,0},{2,1},{1,2},{0,3},{7,4},{6,5},{5,6},{4,7},{11,8},{10,9},{9,1... | collective-permute-start | bytes 786440 | tf_op jit(solution)/shard_map/ppermute | solution.py:337
  46.3 5.5 %copy-start.33 = (f32[2,16,16,128]{3,2,1,0:T(8,128)S(1)}, f32[2,16,16,128]{3,2,1,0:T(8,128)}, u32[]{:S(2)}) copy-start(f32[2,16,16,128]{3,2,1,0:T(8,128)} %get-tuple-element.38) | copy-start | bytes 786436
  46.4 5.9 %copy-start.32 = (f32[2,16,16,128]{3,2,1,0:T(8,128)S(1)}, f32[2,16,16,128]{3,2,1,0:T(8,128)}, u32[]{:S(2)}) copy-start(f32[2,16,16,128]{3,2,1,0:T(8,128)} %get-tuple-element.39) | copy-start | bytes 786436
  46.4 7.4 %copy-start.31 = (f32[2,16,16,128]{3,2,1,0:T(8,128)S(1)}, f32[2,16,16,128]{3,2,1,0:T(8,128)}, u32[]{:S(2)}) copy-start(f32[2,16,16,128]{3,2,1,0:T(8,128)} %get-tuple-element.40) | copy-start | bytes 786436
  51.8 8.7 %copy-start.30 = (f32[2,16,16,128]{3,2,1,0:T(8,128)S(1)}, f32[2,16,16,128]{3,2,1,0:T(8,128)}, u32[]{:S(2)}) copy-start(f32[2,16,16,128]{3,2,1,0:T(8,128)} %get-tuple-element.32) | copy-start | bytes 786436
  51.9 8.7 %collective-permute-start.12 = (f32[2,16,16,128]{3,2,1,0:T(8,128)S(1)}, f32[2,16,16,128]{3,2,1,0:T(8,128)S(1)}, u32[]{:S(2)}, u32[]{:S(2)}) collective-permute-start(f32[2,16,16,128]{3,2,1,0:T(8,128)S(1)} %copy-done.33), channel_id=1, source_target_pairs={{1,0},{0,1},{3,2},{2,3},{5,4},{4,5},{7,6},{6,7},{9,8},{8,9},{11,10... | collective-permute-start | bytes 786440 | tf_op jit(solution)/shard_map/ppermute | solution.py:337
  52.3 9.2 %collective-permute-start.13 = (f32[2,16,16,128]{3,2,1,0:T(8,128)S(1)}, f32[2,16,16,128]{3,2,1,0:T(8,128)S(1)}, u32[]{:S(2)}, u32[]{:S(2)}) collective-permute-start(f32[2,16,16,128]{3,2,1,0:T(8,128)S(1)} %copy-done.32), channel_id=1, source_target_pairs={{2,0},{3,1},{0,2},{1,3},{6,4},{7,5},{4,6},{5,7},{10,8},{11,9},{8,1... | collective-permute-start | bytes 786440 | tf_op jit(solution)/shard_map/ppermute | solution.py:337
  53.8 12.3 %collective-permute-start.14 = (f32[2,16,16,128]{3,2,1,0:T(8,128)S(1)}, f32[2,16,16,128]{3,2,1,0:T(8,128)S(1)}, u32[]{:S(2)}, u32[]{:S(2)}) collective-permute-start(f32[2,16,16,128]{3,2,1,0:T(8,128)S(1)} %copy-done.31), channel_id=1, source_target_pairs={{3,0},{2,1},{1,2},{0,3},{7,4},{6,5},{5,6},{4,7},{11,8},{10,9},{9,1... | collective-permute-start | bytes 786440 | tf_op jit(solution)/shard_map/ppermute | solution.py:337
  53.9 16.6 %collective-permute-start.6 = (f32[2,16,16,128]{3,2,1,0:T(8,128)}, f32[2,16,16,128]{3,2,1,0:T(8,128)S(1)}, u32[]{:S(2)}, u32[]{:S(2)}) collective-permute-start(f32[2,16,16,128]{3,2,1,0:T(8,128)} %get-tuple-element.30), channel_id=1, source_target_pairs={{1,0},{0,1},{3,2},{2,3},{5,4},{4,5},{7,6},{6,7},{9,8},{8,9},{11,10... | collective-permute-start | bytes 786440 | tf_op jit(solution)/shard_map/ppermute | solution.py:337
  54.5 18.2 %collective-permute-start.7 = (f32[2,16,16,128]{3,2,1,0:T(8,128)}, f32[2,16,16,128]{3,2,1,0:T(8,128)S(1)}, u32[]{:S(2)}, u32[]{:S(2)}) collective-permute-start(f32[2,16,16,128]{3,2,1,0:T(8,128)} %get-tuple-element.31), channel_id=1, source_target_pairs={{2,0},{3,1},{0,2},{1,3},{6,4},{7,5},{4,6},{5,7},{10,8},{11,9},{8,1... | collective-permute-start | bytes 786440 | tf_op jit(solution)/shard_map/ppermute | solution.py:337
  60.5 6.4 %copy-start.16 = (f32[2,16,16,128]{3,2,1,0:T(8,128)}, f32[2,16,16,128]{3,2,1,0:T(8,128)S(1)}, u32[]{:S(2)}) copy-start(f32[2,16,16,128]{3,2,1,0:T(8,128)S(1)} %collective-permute-done.12.refs_1_) | copy-start | bytes 786436
  60.5 16.8 %collective-permute-start.8 = (f32[2,16,16,128]{3,2,1,0:T(8,128)S(1)}, f32[2,16,16,128]{3,2,1,0:T(8,128)S(1)}, u32[]{:S(2)}, u32[]{:S(2)}) collective-permute-start(f32[2,16,16,128]{3,2,1,0:T(8,128)S(1)} %copy-done.30), channel_id=1, source_target_pairs={{3,0},{2,1},{1,2},{0,3},{7,4},{6,5},{5,6},{4,7},{11,8},{10,9},{9,1... | collective-permute-start | bytes 786440 | tf_op jit(solution)/shard_map/ppermute | solution.py:337
  61.5 5.5 %copy-start.17 = (f32[2,16,16,128]{3,2,1,0:T(8,128)}, f32[2,16,16,128]{3,2,1,0:T(8,128)S(1)}, u32[]{:S(2)}) copy-start(f32[2,16,16,128]{3,2,1,0:T(8,128)S(1)} %collective-permute-done.13.refs_2_) | copy-start | bytes 786436
  61.5 20.2 %collective-permute-start.21 = (f32[2,16,16,128]{3,2,1,0:T(8,128)}, f32[2,16,16,128]{3,2,1,0:T(8,128)S(1)}, u32[]{:S(2)}, u32[]{:S(2)}) collective-permute-start(f32[2,16,16,128]{3,2,1,0:T(8,128)} %get-tuple-element.50), channel_id=1, source_target_pairs={{1,0},{0,1},{3,2},{2,3},{5,4},{4,5},{7,6},{6,7},{9,8},{8,9},{11,10... | collective-permute-start | bytes 786440 | tf_op jit(solution)/shard_map/ppermute | solution.py:337
  66.1 17.8 %collective-permute-start.22 = (f32[2,16,16,128]{3,2,1,0:T(8,128)}, f32[2,16,16,128]{3,2,1,0:T(8,128)S(1)}, u32[]{:S(2)}, u32[]{:S(2)}) collective-permute-start(f32[2,16,16,128]{3,2,1,0:T(8,128)} %get-tuple-element.51), channel_id=1, source_target_pairs={{2,0},{3,1},{0,2},{1,3},{6,4},{7,5},{4,6},{5,7},{10,8},{11,9},{8,1... | collective-permute-start | bytes 786440 | tf_op jit(solution)/shard_map/ppermute | solution.py:337
  70.4 7.7 %copy-start.14 = (f32[2,16,16,128]{3,2,1,0:T(8,128)}, f32[2,16,16,128]{3,2,1,0:T(8,128)S(1)}, u32[]{:S(2)}) copy-start(f32[2,16,16,128]{3,2,1,0:T(8,128)S(1)} %collective-permute-done.6.refs_1_) | copy-start | bytes 786436
  70.5 18.2 %collective-permute-start.23 = (f32[2,16,16,128]{3,2,1,0:T(8,128)}, f32[2,16,16,128]{3,2,1,0:T(8,128)S(1)}, u32[]{:S(2)}, u32[]{:S(2)}) collective-permute-start(f32[2,16,16,128]{3,2,1,0:T(8,128)} %get-tuple-element.52), channel_id=1, source_target_pairs={{3,0},{2,1},{1,2},{0,3},{7,4},{6,5},{5,6},{4,7},{11,8},{10,9},{9,1... | collective-permute-start | bytes 786440 | tf_op jit(solution)/shard_map/ppermute | solution.py:337
  72.7 5.5 %copy-start.15 = (f32[2,16,16,128]{3,2,1,0:T(8,128)}, f32[2,16,16,128]{3,2,1,0:T(8,128)S(1)}, u32[]{:S(2)}) copy-start(f32[2,16,16,128]{3,2,1,0:T(8,128)S(1)} %collective-permute-done.7.refs_2_) | copy-start | bytes 786436
  72.7 17.8 %collective-permute-start.15 = (f32[2,16,16,128]{3,2,1,0:T(8,128)}, f32[2,16,16,128]{3,2,1,0:T(8,128)S(1)}, u32[]{:S(2)}, u32[]{:S(2)}) collective-permute-start(f32[2,16,16,128]{3,2,1,0:T(8,128)} %get-tuple-element.42), channel_id=1, source_target_pairs={{1,0},{0,1},{3,2},{2,3},{5,4},{4,5},{7,6},{6,7},{9,8},{8,9},{11,10... | collective-permute-start | bytes 786440 | tf_op jit(solution)/shard_map/ppermute | solution.py:337
  77.3 20.4 %collective-permute-start.16 = (f32[2,16,16,128]{3,2,1,0:T(8,128)}, f32[2,16,16,128]{3,2,1,0:T(8,128)S(1)}, u32[]{:S(2)}, u32[]{:S(2)}) collective-permute-start(f32[2,16,16,128]{3,2,1,0:T(8,128)} %get-tuple-element.43), channel_id=1, source_target_pairs={{2,0},{3,1},{0,2},{1,3},{6,4},{7,5},{4,6},{5,7},{10,8},{11,9},{8,1... | collective-permute-start | bytes 786440 | tf_op jit(solution)/shard_map/ppermute | solution.py:337
  81.7 9.9 %copy-start.5 = (f32[2,16,16,128]{3,2,1,0:T(8,128)}, f32[2,16,16,128]{3,2,1,0:T(8,128)S(1)}, u32[]{:S(2)}) copy-start(f32[2,16,16,128]{3,2,1,0:T(8,128)S(1)} %collective-permute-done.21.refs_6_) | copy-start | bytes 786436
  81.7 18.2 %collective-permute-start.17 = (f32[2,16,16,128]{3,2,1,0:T(8,128)}, f32[2,16,16,128]{3,2,1,0:T(8,128)S(1)}, u32[]{:S(2)}, u32[]{:S(2)}) collective-permute-start(f32[2,16,16,128]{3,2,1,0:T(8,128)} %get-tuple-element.44), channel_id=1, source_target_pairs={{3,0},{2,1},{1,2},{0,3},{7,4},{6,5},{5,6},{4,7},{11,8},{10,9},{9,1... | collective-permute-start | bytes 786440 | tf_op jit(solution)/shard_map/ppermute | solution.py:337
  83.9 7.6 %copy-start.6 = (f32[2,16,16,128]{3,2,1,0:T(8,128)}, f32[2,16,16,128]{3,2,1,0:T(8,128)S(1)}, u32[]{:S(2)}) copy-start(f32[2,16,16,128]{3,2,1,0:T(8,128)S(1)} %collective-permute-done.22.refs_7_) | copy-start | bytes 786436
  83.9 23.2 %collective-permute-start.10 = (f32[2,16,16,128]{3,2,1,0:T(8,128)}, f32[2,16,16,128]{3,2,1,0:T(8,128)S(1)}, u32[]{:S(2)}, u32[]{:S(2)}) collective-permute-start(f32[2,16,16,128]{3,2,1,0:T(8,128)} %get-tuple-element.35), channel_id=1, source_target_pairs={{2,0},{3,1},{0,2},{1,3},{6,4},{7,5},{4,6},{5,7},{10,8},{11,9},{8,1... | collective-permute-start | bytes 786440 | tf_op jit(solution)/shard_map/ppermute | solution.py:337
  88.7 21.7 %collective-permute-start.11 = (f32[2,16,16,128]{3,2,1,0:T(8,128)}, f32[2,16,16,128]{3,2,1,0:T(8,128)S(1)}, u32[]{:S(2)}, u32[]{:S(2)}) collective-permute-start(f32[2,16,16,128]{3,2,1,0:T(8,128)} %get-tuple-element.36), channel_id=1, source_target_pairs={{3,0},{2,1},{1,2},{0,3},{7,4},{6,5},{5,6},{4,7},{11,8},{10,9},{9,1... | collective-permute-start | bytes 786440 | tf_op jit(solution)/shard_map/ppermute | solution.py:337
  90.5 7.3 %copy-start.7 = (f32[2,16,16,128]{3,2,1,0:T(8,128)}, f32[2,16,16,128]{3,2,1,0:T(8,128)S(1)}, u32[]{:S(2)}) copy-start(f32[2,16,16,128]{3,2,1,0:T(8,128)S(1)} %collective-permute-done.15.refs_6_) | copy-start | bytes 786436
  90.5 19.9 %collective-permute-start.9 = (f32[2,16,16,128]{3,2,1,0:T(8,128)}, f32[2,16,16,128]{3,2,1,0:T(8,128)S(1)}, u32[]{:S(2)}, u32[]{:S(2)}) collective-permute-start(f32[2,16,16,128]{3,2,1,0:T(8,128)} %get-tuple-element.34), channel_id=1, source_target_pairs={{1,0},{0,1},{3,2},{2,3},{5,4},{4,5},{7,6},{6,7},{9,8},{8,9},{11,10... | collective-permute-start | bytes 786440 | tf_op jit(solution)/shard_map/ppermute | solution.py:337
  117.7 26.8 %copy-start.2 = (f32[9,16,32,128]{3,2,1,0:T(8,128)S(1)}, f32[9,16,32,128]{3,2,1,0:T(8,128)}, u32[]{:S(2)}) copy-start(f32[9,16,32,128]{3,2,1,0:T(8,128)} %add_exchange_2.1) | copy-start | bytes 7077892
  118.8 9.0 %collective-permute-start.24 = (f32[1,16,32,128]{3,2,1,0:T(8,128)S(1)}, f32[1,16,32,128]{3,2,1,0:T(8,128)S(1)}, u32[]{:S(2)}, u32[]{:S(2)}) collective-permute-start(f32[1,16,32,128]{3,2,1,0:T(8,128)S(1)} %slice.63), channel_id=1, source_target_pairs={{0,4},{4,0},{8,12},{12,8},{16,20},{20,16},{24,28},{28,24},{1,5},{5... | collective-permute-start | bytes 786440 | tf_op jit(solution)/shard_map/ppermute | solution.py:294
  129.1 10.4 %collective-permute-start.25 = (f32[1,16,32,128]{3,2,1,0:T(8,128)S(1)}, f32[1,16,32,128]{3,2,1,0:T(8,128)S(1)}, u32[]{:S(2)}, u32[]{:S(2)}) collective-permute-start(f32[1,16,32,128]{3,2,1,0:T(8,128)S(1)} %get-tuple-element.60), channel_id=1, source_target_pairs={{24,0},{28,4},{0,8},{4,12},{8,16},{12,20},{16,24},{20,28},{25,1},{... | collective-permute-start | bytes 786440 | tf_op jit(solution)/shard_map/ppermute | solution.py:22
  131.2 9.2 %collective-permute-start.26 = (f32[1,16,32,128]{3,2,1,0:T(8,128)S(1)}, f32[1,16,32,128]{3,2,1,0:T(8,128)S(1)}, u32[]{:S(2)}, u32[]{:S(2)}) collective-permute-start(f32[1,16,32,128]{3,2,1,0:T(8,128)S(1)} %get-tuple-element.62), channel_id=1, source_target_pairs={{0,4},{4,0},{8,12},{12,8},{16,20},{20,16},{24,28},{28,24},{1,5},{5... | collective-permute-start | bytes 786440 | tf_op jit(solution)/shard_map/ppermute | solution.py:294
  131.5 13.0 %collective-permute-start.28 = (f32[1,16,32,128]{3,2,1,0:T(8,128)S(1)}, f32[1,16,32,128]{3,2,1,0:T(8,128)S(1)}, u32[]{:S(2)}, u32[]{:S(2)}) collective-permute-start(f32[1,16,32,128]{3,2,1,0:T(8,128)S(1)} %get-tuple-element.61), channel_id=1, source_target_pairs={{0,4},{4,0},{8,12},{12,8},{16,20},{20,16},{24,28},{28,24},{1,5},{5... | collective-permute-start | bytes 786440 | tf_op jit(solution)/shard_map/ppermute | solution.py:294
  145.5 11.2 %collective-permute-start.27 = (f32[1,16,32,128]{3,2,1,0:T(8,128)}, f32[1,16,32,128]{3,2,1,0:T(8,128)S(1)}, u32[]{:S(2)}, u32[]{:S(2)}) collective-permute-start(f32[1,16,32,128]{3,2,1,0:T(8,128)} %get-tuple-element.59), channel_id=1, source_target_pairs={{24,0},{28,4},{0,8},{4,12},{8,16},{12,20},{16,24},{20,28},{25,1},{... | collective-permute-start | bytes 786440 | tf_op jit(solution)/shard_map/ppermute | solution.py:22
  145.9 14.2 %collective-permute-start.29 = (f32[1,16,32,128]{3,2,1,0:T(8,128)}, f32[1,16,32,128]{3,2,1,0:T(8,128)}, u32[]{:S(2)}, u32[]{:S(2)}) collective-permute-start(f32[1,16,32,128]{3,2,1,0:T(8,128)} %get-tuple-element.58), channel_id=1, source_target_pairs={{24,0},{28,4},{0,8},{4,12},{8,16},{12,20},{16,24},{20,28},{25,1},{... | collective-permute-start | bytes 786440 | tf_op jit(solution)/shard_map/ppermute | solution.py:22
  (16 other events, 33.1 us)

commit v5 on v2

--- a/solution.py
+++ b/solution.py
@@ -290,14 +290,26 @@
     return jnp.where(squared > 0, scale / safe, 0.0)
 
 
+def pair_swap(block):
+    return lax.ppermute(block, "band", [(i, i ^ 1) for i in range(lax.axis_size("band"))])
+
+
+def visiting(own):
+    if REACH != 2 or lax.axis_size("band") % 2:
+        return [shifted(own, "band", -d) for d in range(1, REACH + 1)]
+    even = lax.axis_index("band") % 2 == 0
+    second = shifted(own, "band", -2)
+    return [pair_swap(jnp.where(even, second, own)), second]
+
+
 def local(orbitals, pair_mask):
     orb_count, planes, cells = orbitals.shape
     n = math.isqrt(cells)
     parts = lax.axis_size("grid")
     tables = dft_tables(n, parts)
     own = orbitals.reshape(orb_count, planes, n // 2, 2 * n)
-    visits = [own] + [shifted(own, "band", -d) for d in range(1, REACH + 1)]
-    flat = jnp.concatenate(visits, axis=0)
+    visits = [visiting(own[a : a + 1]) for a in range(orb_count)]
+    flat = jnp.concatenate([own] + [v[d] for d in range(REACH) for v in visits], axis=0)
     me = lax.axis_index("grid").astype(jnp.int32).reshape(1)
     scalars = (me, *live_pairs(pair_mask))
     kernel = green_kernel(n, n // parts)

time: 170 us -> 162 us (0.953)
  starting transfers between devices: 35.9 us -> 21.8 us
  other arithmetic: 6.47 us -> 8.62 us
  waiting for transfers between devices: 70.7 us -> 72.8 us
    ppermute x4 -> x5, starting transfers between devices: 21.9 us -> 6.58 us  [shifted(): lax.ppermute(block, axis, [((i - distance) % count, i) for i in range(cou...]
    ppermute x0 -> x3, waiting for transfers between devices: none -> 6.33 us  [pair_swap(): lax.ppermute(block, 'band', [(i, i ^ 1) for i in range(lax.axis_size('ban...]
    select_n x0 -> x3, other arithmetic: none -> 4.14 us  [visiting(): return [pair_swap(jnp.where(even, second, own)), second]]
    ppermute x4 -> x5, waiting for transfers between devices: 50 us -> 47 us  [shifted(): lax.ppermute(block, axis, [((i - distance) % count, i) for i in range(cou...]
    unnamed x51 -> x73, local copies, waits for them, and re-layouts: 5.39 us -> 8 us
  transfers between devices with their start and end apart: 22 -> 26, of which waited for: 10 -> 15; matrix products, arithmetic and copies ran while one was open for 4% -> 7% of each run, Pallas kernels for 20% -> 21%
where the time goes in v5:
time: 162 us
  waiting for transfers between devices  72.8 us (45%)
  Pallas kernels  47.2 us (29%)
  starting transfers between devices  21.8 us (13%)
  local copies, waits for them, and re-layouts  11.3 us (7%)
  other arithmetic  8.62 us (5%)
    ppermute x5, waiting for transfers between devices, shifted(): lax.ppermute(block, axis, [((i - distance) % count, i) for i in range(cou...  47 us
    pallas_call x3, Pallas kernels, add_exchange(): pl.pallas_call(body, grid_spec=pltpu.PrefetchScalarGridSpec(num_scalar_pr...  19.8 us
    ppermute x18, waiting for transfers between devices, exchange(): moved.append(lax.ppermute(blocks[back], 'grid', route))  19.5 us
    pallas_call x3, Pallas kernels, forward_planes(): pl.pallas_call(body, grid_spec=pltpu.PrefetchScalarGridSpec(num_scalar_pr...  16.9 us
    ppermute x18, starting transfers between devices, exchange(): moved.append(lax.ppermute(blocks[back], 'grid', route))  14.8 us
    pallas_call x3, Pallas kernels, solve_columns(): pl.pallas_call(body, grid_spec=pltpu.PrefetchScalarGridSpec(num_scalar_pr...  10.5 us
    unnamed x73, local copies, waits for them, and re-layouts  8 us
    ppermute x5, starting transfers between devices, shifted(): lax.ppermute(block, axis, [((i - distance) % count, i) for i in range(cou...  6.58 us
  transfers between devices with their start and end apart: 26, of which 15 were waited for; matrix products, arithmetic and copies ran while one was open for 7% of the time, Pallas kernels for 21%

profile of v5, /device:TPU:4, one launch (start us, length us, event | category | flops | bytes accessed | tf_op | source)
XLA Modules:
  0.0 162.2 jit_solution(12357179166070068394)
XLA Ops:
  0.0 1.2 slice_bitcast_fusion
  1.3 0.8 copy.23
  2.0 3.6 %collective-permute-start = (f32[1,16,32,128]{3,2,1,0:T(8,128)}, f32[1,16,32,128]{3,2,1,0:T(8,128)S(1)}, u32[]{:S(2)}, u32[]{:S(2)}) collective-permute-start(f32[1,16,32,128]{3,2,1,0:T(8,128)} %bitcast.8), channel_id=1, source_target_pairs={{8,0},{12,4},{16,8},{20,12},{24,16},{28,20},{0,24},{4,28},{9,1},{1... | collective-permute-start | bytes 786440 | tf_op jit(solution)/shard_map/ppermute | solution.py:22
  5.6 0.8 copy.24
  7.5 0.8 gather_fusion
  9.3 3.4 %collective-permute-done = f32[1,16,32,128]{3,2,1,0:T(8,128)S(1)} collective-permute-done((f32[1,16,32,128]{3,2,1,0:T(8,128)}, f32[1,16,32,128]{3,2,1,0:T(8,128)S(1)}, u32[]{:S(2)}, u32[]{:S(2)}) %collective-permute-start) | collective-permute-done | bytes 262176 | tf_op jit(solution)/shard_map/ppermute | solution.py:22
  12.7 1.7 %broadcast_select_fusion.2 = f32[1,16,32,128]{3,2,1,0:T(8,128)} fusion(f32[1,16,32,128]{3,2,1,0:T(8,128)S(1)} %collective-permute-done, pred[]{:T(512)S(6)} %eq.29, f32[1,16,32,128]{3,2,1,0:T(8,128)} %bitcast.29), kind=kLoop, calls=%fused_computation.15 | loop fusion | flops 65536 | bytes 786433 | tf_op jit(solution)/shard_map/jit(_where)/select_n | solution.py:302
  14.4 3.9 %collective-permute-done.2 = f32[1,16,32,128]{3,2,1,0:T(8,128)S(1)} collective-permute-done((f32[1,16,32,128]{3,2,1,0:T(8,128)}, f32[1,16,32,128]{3,2,1,0:T(8,128)S(1)}, u32[]{:S(2)}, u32[]{:S(2)}) %collective-permute-start.2) | collective-permute-done | bytes 262176 | tf_op jit(solution)/shard_map/ppermute | solution.py:22
  18.3 1.7 %broadcast_select_fusion.1 = f32[1,16,32,128]{3,2,1,0:T(8,128)} fusion(f32[1,16,32,128]{3,2,1,0:T(8,128)S(1)} %collective-permute-done.2, pred[]{:T(512)S(6)} %eq.29, f32[1,16,32,128]{3,2,1,0:T(8,128)} %bitcast.28), kind=kLoop, calls=%fused_computation.14 | loop fusion | flops 65536 | bytes 786433 | tf_op jit(solution)/shard_map/jit(_where)/select_n | solution.py:302
  20.0 2.7 %collective-permute-done.4 = f32[1,16,32,128]{3,2,1,0:T(8,128)S(1)} collective-permute-done((f32[1,16,32,128]{3,2,1,0:T(8,128)S(1)}, f32[1,16,32,128]{3,2,1,0:T(8,128)S(1)}, u32[]{:S(2)}, u32[]{:S(2)}) %collective-permute-start.4) | collective-permute-done | bytes 262176 | tf_op jit(solution)/shard_map/ppermute | solution.py:22
  22.7 0.7 broadcast_select_fusion
  23.9 1.0 constant_dynamic-update-slice_fusion.5
  24.9 3.2 %collective-permute-done.3 = f32[1,16,32,128]{3,2,1,0:T(8,128)} collective-permute-done((f32[1,16,32,128]{3,2,1,0:T(8,128)}, f32[1,16,32,128]{3,2,1,0:T(8,128)}, u32[]{:S(2)}, u32[]{:S(2)}) %collective-permute-start.3) | collective-permute-done | bytes 262176 | tf_op jit(solution)/shard_map/ppermute | solution.py:294
  28.0 1.0 constant_dynamic-update-slice_fusion.4
  29.0 3.2 %collective-permute-done.5 = f32[1,16,32,128]{3,2,1,0:T(8,128)S(1)} collective-permute-done((f32[1,16,32,128]{3,2,1,0:T(8,128)}, f32[1,16,32,128]{3,2,1,0:T(8,128)S(1)}, u32[]{:S(2)}, u32[]{:S(2)}) %collective-permute-start.5) | collective-permute-done | bytes 262176 | tf_op jit(solution)/shard_map/ppermute | solution.py:294
  32.3 1.4 copy-done.1
  33.7 5.3 %forward_planes_0.1 = (f32[2,16,16,128]{3,2,1,0:T(8,128)}, f32[2,16,16,128]{3,2,1,0:T(8,128)}, f32[2,16,16,128]{3,2,1,0:T(8,128)}, f32[2,16,16,128]{3,2,1,0:T(8,128)}) custom-call(s32[1]{0:T(128)} %bitcast.refs_0_._, s32[12]{0:T(128)} %get-tuple-element.56.refs_1_, s32[12]{0:T(128)} %get-tuple-element.55.refs_2_, f32[9,16,32,128]{3,2,1,0:T(8,128)} %copy-done.1, ...), custom_call_target="tpu_custom_call" | custom-call | tf_op jit(solution)/shard_map/forward_planes_0/pallas_call | solution.py:148
  39.1 1.6 collective-permute-start.19
  41.0 5.6 %forward_planes_1.1 = (f32[2,16,16,128]{3,2,1,0:T(8,128)}, f32[2,16,16,128]{3,2,1,0:T(8,128)}, f32[2,16,16,128]{3,2,1,0:T(8,128)}, f32[2,16,16,128]{3,2,1,0:T(8,128)}) custom-call(s32[1]{0:T(128)} %bitcast.refs_0_._, s32[12]{0:T(128)} %get-tuple-element.56.refs_1_, s32[12]{0:T(128)} %get-tuple-element.55.refs_2_, f32[9,16,32,128]{3,2,1,0:T(8,128)} %copy-done.1, ...), custom_call_target="tpu_custom_call" | custom-call | tf_op jit(solution)/shard_map/forward_planes_1/pallas_call | solution.py:148
  46.7 6.0 %forward_planes_2.1 = (f32[2,16,16,128]{3,2,1,0:T(8,128)}, f32[2,16,16,128]{3,2,1,0:T(8,128)}, f32[2,16,16,128]{3,2,1,0:T(8,128)}, f32[2,16,16,128]{3,2,1,0:T(8,128)}) custom-call(s32[1]{0:T(128)} %bitcast.refs_0_._, s32[12]{0:T(128)} %get-tuple-element.56.refs_1_, s32[12]{0:T(128)} %get-tuple-element.55.refs_2_, f32[9,16,32,128]{3,2,1,0:T(8,128)} %copy-done.1, ...), custom_call_target="tpu_custom_call" | custom-call | tf_op jit(solution)/shard_map/forward_planes_2/pallas_call | solution.py:148
  53.1 1.5 collective-permute-start.13
  55.3 1.5 collective-permute-start.7
  56.9 1.0 fusion.4.refs_4_
  57.9 3.5 %solve_columns_0.1 = (f32[2,16,16,128]{3,2,1,0:T(8,128)}, f32[2,16,16,128]{3,2,1,0:T(8,128)}, f32[2,16,16,128]{3,2,1,0:T(8,128)}, f32[2,16,16,128]{3,2,1,0:T(8,128)}) custom-call(s32[1]{0:T(128)} %bitcast.refs_0_._, f32[2,16,16,128]{3,2,1,0:T(8,128)} %get-tuple-element.45.refs_0_, f32[2,16,16,128]{3,2,1,0:T(8,128)} %copy-done.16, ...), custom_call_target="tpu_custom_call" | custom-call | tf_op jit(solution)/shard_map/solve_columns_0/pallas_call | solution.py:186
  61.5 0.8 collective-permute-done.13.refs_2_
  62.3 4.7 %collective-permute-done.14.refs_3_ = f32[2,16,16,128]{3,2,1,0:T(8,128)S(1)} collective-permute-done((f32[2,16,16,128]{3,2,1,0:T(8,128)S(1)}, f32[2,16,16,128]{3,2,1,0:T(8,128)S(1)}, u32[]{:S(2)}, u32[]{:S(2)}) %collective-permute-start.14) | collective-permute-done | bytes 262176 | tf_op jit(solution)/shard_map/ppermute | solution.py:324
  66.9 0.8 collective-permute-start.22
  67.7 3.5 %solve_columns_1.1 = (f32[2,16,16,128]{3,2,1,0:T(8,128)}, f32[2,16,16,128]{3,2,1,0:T(8,128)}, f32[2,16,16,128]{3,2,1,0:T(8,128)}, f32[2,16,16,128]{3,2,1,0:T(8,128)}) custom-call(s32[1]{0:T(128)} %bitcast.refs_0_._, f32[2,16,16,128]{3,2,1,0:T(8,128)} %get-tuple-element.37.refs_0_, f32[2,16,16,128]{3,2,1,0:T(8,128)} %copy-done.14, ...), custom_call_target="tpu_custom_call" | custom-call | tf_op jit(solution)/shard_map/solve_columns_1/pallas_call | solution.py:186
  71.2 1.9 %collective-permute-start.23 = (f32[2,16,16,128]{3,2,1,0:T(8,128)}, f32[2,16,16,128]{3,2,1,0:T(8,128)S(1)}, u32[]{:S(2)}, u32[]{:S(2)}) collective-permute-start(f32[2,16,16,128]{3,2,1,0:T(8,128)} %get-tuple-element.52), channel_id=1, source_target_pairs={{3,0},{2,1},{1,2},{0,3},{7,4},{6,5},{5,6},{4,7},{11,8},{10,9},{9,1... | collective-permute-start | bytes 786440 | tf_op jit(solution)/shard_map/ppermute | solution.py:324
  73.5 4.7 %collective-permute-done.8.refs_3_ = f32[2,16,16,128]{3,2,1,0:T(8,128)S(1)} collective-permute-done((f32[2,16,16,128]{3,2,1,0:T(8,128)S(1)}, f32[2,16,16,128]{3,2,1,0:T(8,128)S(1)}, u32[]{:S(2)}, u32[]{:S(2)}) %collective-permute-start.8) | collective-permute-done | bytes 262176 | tf_op jit(solution)/shard_map/ppermute | solution.py:324
  78.2 0.8 collective-permute-start.16
  79.0 3.5 %solve_columns_2.1 = (f32[2,16,16,128]{3,2,1,0:T(8,128)}, f32[2,16,16,128]{3,2,1,0:T(8,128)}, f32[2,16,16,128]{3,2,1,0:T(8,128)}, f32[2,16,16,128]{3,2,1,0:T(8,128)}) custom-call(s32[1]{0:T(128)} %bitcast.refs_0_._, f32[2,16,16,128]{3,2,1,0:T(8,128)} %get-tuple-element.29.refs_0_, f32[2,16,16,128]{3,2,1,0:T(8,128)} %copy-done.12, ...), custom_call_target="tpu_custom_call" | custom-call | tf_op jit(solution)/shard_map/solve_columns_2/pallas_call | solution.py:186
  82.5 1.9 %collective-permute-start.17 = (f32[2,16,16,128]{3,2,1,0:T(8,128)}, f32[2,16,16,128]{3,2,1,0:T(8,128)S(1)}, u32[]{:S(2)}, u32[]{:S(2)}) collective-permute-start(f32[2,16,16,128]{3,2,1,0:T(8,128)} %get-tuple-element.44), channel_id=1, source_target_pairs={{3,0},{2,1},{1,2},{0,3},{7,4},{6,5},{5,6},{4,7},{11,8},{10,9},{9,1... | collective-permute-start | bytes 786440 | tf_op jit(solution)/shard_map/ppermute | solution.py:324
  84.8 1.5 collective-permute-start.10
  86.3 3.2 %collective-permute-done.23.refs_8_ = f32[2,16,16,128]{3,2,1,0:T(8,128)S(1)} collective-permute-done((f32[2,16,16,128]{3,2,1,0:T(8,128)}, f32[2,16,16,128]{3,2,1,0:T(8,128)S(1)}, u32[]{:S(2)}, u32[]{:S(2)}) %collective-permute-start.23) | collective-permute-done | bytes 262176 | tf_op jit(solution)/shard_map/ppermute | solution.py:324
  89.5 1.8 %collective-permute-start.11 = (f32[2,16,16,128]{3,2,1,0:T(8,128)}, f32[2,16,16,128]{3,2,1,0:T(8,128)S(1)}, u32[]{:S(2)}, u32[]{:S(2)}) collective-permute-start(f32[2,16,16,128]{3,2,1,0:T(8,128)} %get-tuple-element.36), channel_id=1, source_target_pairs={{3,0},{2,1},{1,2},{0,3},{7,4},{6,5},{5,6},{4,7},{11,8},{10,9},{9,1... | collective-permute-start | bytes 786440 | tf_op jit(solution)/shard_map/ppermute | solution.py:324
  92.5 6.1 %add_exchange_0.1.refs_21_ = f32[9,16,32,128]{3,2,1,0:T(8,128)} custom-call(s32[1]{0:T(128)} %bitcast.refs_0_._, s32[12]{0:T(128)} %get-tuple-element.56.refs_1_, s32[12]{0:T(128)} %get-tuple-element.55.refs_2_, f32[12]{0:T(128)} %convert_element_type.10.refs_3_, f32[12]{0:T(128)} %convert_element_type.11.refs_4_, ...), custom_call_target="tpu_custom_call" | custom-call | tf_op jit(solution)/shard_map/add_exchange_0/pallas_call | solution.py:245
  98.6 2.2 %collective-permute-done.17.refs_8_ = f32[2,16,16,128]{3,2,1,0:T(8,128)S(1)} collective-permute-done((f32[2,16,16,128]{3,2,1,0:T(8,128)}, f32[2,16,16,128]{3,2,1,0:T(8,128)S(1)}, u32[]{:S(2)}, u32[]{:S(2)}) %collective-permute-start.17) | collective-permute-done | bytes 262176 | tf_op jit(solution)/shard_map/ppermute | solution.py:324
  100.8 0.7 copy-done.11
  101.5 6.6 %add_exchange_1.1.refs_21_ = f32[9,16,32,128]{3,2,1,0:T(8,128)} custom-call(s32[1]{0:T(128)} %bitcast.refs_0_._, s32[12]{0:T(128)} %get-tuple-element.56.refs_1_, s32[12]{0:T(128)} %get-tuple-element.55.refs_2_, f32[12]{0:T(128)} %convert_element_type.10.refs_3_, f32[12]{0:T(128)} %convert_element_type.11.refs_4_, ...), custom_call_target="tpu_custom_call", output_to_operand_aliasing={{}: (21, {})} | custom-call | tf_op jit(solution)/shard_map/add_exchange_1/pallas_call | solution.py:245
  108.1 3.2 %collective-permute-done.11.refs_8_ = f32[2,16,16,128]{3,2,1,0:T(8,128)S(1)} collective-permute-done((f32[2,16,16,128]{3,2,1,0:T(8,128)}, f32[2,16,16,128]{3,2,1,0:T(8,128)S(1)}, u32[]{:S(2)}, u32[]{:S(2)}) %collective-permute-start.11) | collective-permute-done | bytes 262176 | tf_op jit(solution)/shard_map/ppermute | solution.py:324
  112.0 7.2 %add_exchange_2.1 = f32[9,16,32,128]{3,2,1,0:T(8,128)} custom-call(s32[1]{0:T(128)} %bitcast.refs_0_._, s32[12]{0:T(128)} %get-tuple-element.56.refs_1_, s32[12]{0:T(128)} %get-tuple-element.55.refs_2_, f32[12]{0:T(128)} %convert_element_type.10.refs_3_, f32[12]{0:T(128)} %convert_element_type.11.refs_4_, ...), custom_call_target="tpu_custom_call", output_to_operand_aliasing={{}: (21, {})} | custom-call | tf_op jit(solution)/shard_map/add_exchange_2/pallas_call | solution.py:245
  119.2 1.5 fusion.19
  120.7 2.0 %collective-permute-start.25 = (f32[3,16,32,128]{3,2,1,0:T(8,128)S(1)}, f32[3,16,32,128]{3,2,1,0:T(8,128)S(1)}, u32[]{:S(2)}, u32[]{:S(2)}) collective-permute-start(f32[3,16,32,128]{3,2,1,0:T(8,128)S(1)} %get-tuple-element.58), channel_id=1, source_target_pairs={{24,0},{28,4},{0,8},{4,12},{8,16},{12,20},{16,24},{20,28},{25,1},{... | collective-permute-start | bytes 2359304 | tf_op jit(solution)/shard_map/ppermute | solution.py:22
  122.7 18.1 %collective-permute-done.24 = f32[3,16,32,128]{3,2,1,0:T(8,128)S(1)} collective-permute-done((f32[3,16,32,128]{3,2,1,0:T(8,128)S(1)}, f32[3,16,32,128]{3,2,1,0:T(8,128)S(1)}, u32[]{:S(2)}, u32[]{:S(2)}) %collective-permute-start.24) | collective-permute-done | bytes 786464 | tf_op jit(solution)/shard_map/ppermute | solution.py:22
  140.8 18.9 %collective-permute-done.25 = f32[3,16,32,128]{3,2,1,0:T(8,128)S(1)} collective-permute-done((f32[3,16,32,128]{3,2,1,0:T(8,128)S(1)}, f32[3,16,32,128]{3,2,1,0:T(8,128)S(1)}, u32[]{:S(2)}, u32[]{:S(2)}) %collective-permute-start.25) | collective-permute-done | bytes 786464 | tf_op jit(solution)/shard_map/ppermute | solution.py:22
  159.7 1.4 fusion.1
  161.1 1.0 reshape.81
  (104 shorter events, 7.2 us)
Async XLA Ops:
  0.0 7.5 %copy-start = (s32[24,24]{1,0:T(8,128)S(1)}, s32[24,24]{1,0:T(8,128)}, u32[]{:S(2)}) copy-start(s32[24,24]{1,0:T(8,128)} %param.20) | copy-start | bytes 6916
  0.0 7.4 %copy-start.22 = (s32[24]{0:T(128)S(1)}, s32[24]{0:T(128)}, u32[]{:S(2)}) copy-start(s32[24]{0:T(128)} %constant.126.clone) | copy-start | bytes 292
  0.0 7.4 %copy-start.25 = (s32[24]{0:T(128)S(1)}, s32[24]{0:T(128)}, u32[]{:S(2)}) copy-start(s32[24]{0:T(128)} %constant.127.clone) | copy-start | bytes 292
  0.0 7.4 %copy-start.26 = (s32[24]{0:T(128)S(1)}, s32[24]{0:T(128)}, u32[]{:S(2)}) copy-start(s32[24]{0:T(128)} %constant.128.clone) | copy-start | bytes 292
  0.0 8.2 %copy-start.21 = (s32[24,24]{1,0:T(8,128)S(1)}, s32[24,24]{1,0:T(8,128)}, u32[]{:S(2)}) copy-start(s32[24,24]{1,0:T(8,128)} %constant.129.clone) | copy-start | bytes 6916
  0.0 8.3 %copy-start.2 = (f32[3,16,4096]{2,1,0:T(8,128)S(1)}, f32[3,16,4096]{2,1,0:T(8,128)}, u32[]{:S(2)}) copy-start(f32[3,16,4096]{2,1,0:T(8,128)} %param.19) | copy-start | bytes 2359300
  2.0 10.6 %collective-permute-start = (f32[1,16,32,128]{3,2,1,0:T(8,128)}, f32[1,16,32,128]{3,2,1,0:T(8,128)S(1)}, u32[]{:S(2)}, u32[]{:S(2)}) collective-permute-start(f32[1,16,32,128]{3,2,1,0:T(8,128)} %bitcast.8), channel_id=1, source_target_pairs={{8,0},{12,4},{16,8},{20,12},{24,16},{28,20},{0,24},{4,28},{9,1},{1... | collective-permute-start | bytes 786440 | tf_op jit(solution)/shard_map/ppermute | solution.py:22
  5.6 2.9 %copy-start.24 = (s32[24]{0:T(128)S(1)}, s32[24]{0:T(128)}, u32[]{:S(2)}) copy-start(s32[24]{0:T(128)} %constant.131.clone) | copy-start | bytes 292
  6.4 11.9 %collective-permute-start.2 = (f32[1,16,32,128]{3,2,1,0:T(8,128)}, f32[1,16,32,128]{3,2,1,0:T(8,128)S(1)}, u32[]{:S(2)}, u32[]{:S(2)}) collective-permute-start(f32[1,16,32,128]{3,2,1,0:T(8,128)} %bitcast.12), channel_id=1, source_target_pairs={{8,0},{12,4},{16,8},{20,12},{24,16},{28,20},{0,24},{4,28},{9,1},{1... | collective-permute-start | bytes 786440 | tf_op jit(solution)/shard_map/ppermute | solution.py:22
  6.9 15.7 %collective-permute-start.4 = (f32[1,16,32,128]{3,2,1,0:T(8,128)S(1)}, f32[1,16,32,128]{3,2,1,0:T(8,128)S(1)}, u32[]{:S(2)}, u32[]{:S(2)}) collective-permute-start(f32[1,16,32,128]{3,2,1,0:T(8,128)S(1)} %bitcast.32), channel_id=1, source_target_pairs={{8,0},{12,4},{16,8},{20,12},{24,16},{28,20},{0,24},{4,28},{9,1},{1... | collective-permute-start | bytes 786440 | tf_op jit(solution)/shard_map/ppermute | solution.py:22
  14.4 9.6 %collective-permute-start.1 = (f32[1,16,32,128]{3,2,1,0:T(8,128)}, f32[1,16,32,128]{3,2,1,0:T(8,128)}, u32[]{:S(2)}, u32[]{:S(2)}) collective-permute-start(f32[1,16,32,128]{3,2,1,0:T(8,128)} %broadcast_select_fusion.2), channel_id=1, source_target_pairs={{0,4},{4,0},{8,12},{12,8},{16,20},{20,16},{24,28},{28,24},{1,5},{5... | collective-permute-start | bytes 786440 | tf_op jit(solution)/shard_map/ppermute | solution.py:294
  20.0 8.1 %collective-permute-start.3 = (f32[1,16,32,128]{3,2,1,0:T(8,128)}, f32[1,16,32,128]{3,2,1,0:T(8,128)}, u32[]{:S(2)}, u32[]{:S(2)}) collective-permute-start(f32[1,16,32,128]{3,2,1,0:T(8,128)} %broadcast_select_fusion.1), channel_id=1, source_target_pairs={{0,4},{4,0},{8,12},{12,8},{16,20},{20,16},{24,28},{28,24},{1,5},{5... | collective-permute-start | bytes 786440 | tf_op jit(solution)/shard_map/ppermute | solution.py:294
  23.4 8.8 %collective-permute-start.5 = (f32[1,16,32,128]{3,2,1,0:T(8,128)}, f32[1,16,32,128]{3,2,1,0:T(8,128)S(1)}, u32[]{:S(2)}, u32[]{:S(2)}) collective-permute-start(f32[1,16,32,128]{3,2,1,0:T(8,128)} %broadcast_select_fusion), channel_id=1, source_target_pairs={{0,4},{4,0},{8,12},{12,8},{16,20},{20,16},{24,28},{28,24},{1,5},{5... | collective-permute-start | bytes 786440 | tf_op jit(solution)/shard_map/ppermute | solution.py:294
  39.0 15.6 %collective-permute-start.18 = (f32[2,16,16,128]{3,2,1,0:T(8,128)}, f32[2,16,16,128]{3,2,1,0:T(8,128)S(1)}, u32[]{:S(2)}, u32[]{:S(2)}) collective-permute-start(f32[2,16,16,128]{3,2,1,0:T(8,128)} %get-tuple-element.46), channel_id=1, source_target_pairs={{1,0},{0,1},{3,2},{2,3},{5,4},{4,5},{7,6},{6,7},{9,8},{8,9},{11,10... | collective-permute-start | bytes 786440 | tf_op jit(solution)/shard_map/ppermute | solution.py:324
  39.1 15.6 %collective-permute-start.19 = (f32[2,16,16,128]{3,2,1,0:T(8,128)}, f32[2,16,16,128]{3,2,1,0:T(8,128)S(1)}, u32[]{:S(2)}, u32[]{:S(2)}) collective-permute-start(f32[2,16,16,128]{3,2,1,0:T(8,128)} %get-tuple-element.47), channel_id=1, source_target_pairs={{2,0},{3,1},{0,2},{1,3},{6,4},{7,5},{4,6},{5,7},{10,8},{11,9},{8,1... | collective-permute-start | bytes 786440 | tf_op jit(solution)/shard_map/ppermute | solution.py:324
  40.6 14.7 %collective-permute-start.20 = (f32[2,16,16,128]{3,2,1,0:T(8,128)}, f32[2,16,16,128]{3,2,1,0:T(8,128)S(1)}, u32[]{:S(2)}, u32[]{:S(2)}) collective-permute-start(f32[2,16,16,128]{3,2,1,0:T(8,128)} %get-tuple-element.48), channel_id=1, source_target_pairs={{3,0},{2,1},{1,2},{0,3},{7,4},{6,5},{5,6},{4,7},{11,8},{10,9},{9,1... | collective-permute-start | bytes 786440 | tf_op jit(solution)/shard_map/ppermute | solution.py:324
  46.6 6.1 %copy-start.30 = (f32[2,16,16,128]{3,2,1,0:T(8,128)S(1)}, f32[2,16,16,128]{3,2,1,0:T(8,128)}, u32[]{:S(2)}) copy-start(f32[2,16,16,128]{3,2,1,0:T(8,128)} %get-tuple-element.38) | copy-start | bytes 786436
  46.6 6.5 %copy-start.29 = (f32[2,16,16,128]{3,2,1,0:T(8,128)S(1)}, f32[2,16,16,128]{3,2,1,0:T(8,128)}, u32[]{:S(2)}) copy-start(f32[2,16,16,128]{3,2,1,0:T(8,128)} %get-tuple-element.39) | copy-start | bytes 786436
  46.6 8.0 %copy-start.28 = (f32[2,16,16,128]{3,2,1,0:T(8,128)S(1)}, f32[2,16,16,128]{3,2,1,0:T(8,128)}, u32[]{:S(2)}) copy-start(f32[2,16,16,128]{3,2,1,0:T(8,128)} %get-tuple-element.40) | copy-start | bytes 786436
  52.7 8.7 %copy-start.27 = (f32[2,16,16,128]{3,2,1,0:T(8,128)S(1)}, f32[2,16,16,128]{3,2,1,0:T(8,128)}, u32[]{:S(2)}) copy-start(f32[2,16,16,128]{3,2,1,0:T(8,128)} %get-tuple-element.32) | copy-start | bytes 786436
  52.7 8.7 %collective-permute-start.12 = (f32[2,16,16,128]{3,2,1,0:T(8,128)S(1)}, f32[2,16,16,128]{3,2,1,0:T(8,128)S(1)}, u32[]{:S(2)}, u32[]{:S(2)}) collective-permute-start(f32[2,16,16,128]{3,2,1,0:T(8,128)S(1)} %copy-done.30), channel_id=1, source_target_pairs={{1,0},{0,1},{3,2},{2,3},{5,4},{4,5},{7,6},{6,7},{9,8},{8,9},{11,10... | collective-permute-start | bytes 786440 | tf_op jit(solution)/shard_map/ppermute | solution.py:324
  53.1 9.2 %collective-permute-start.13 = (f32[2,16,16,128]{3,2,1,0:T(8,128)S(1)}, f32[2,16,16,128]{3,2,1,0:T(8,128)S(1)}, u32[]{:S(2)}, u32[]{:S(2)}) collective-permute-start(f32[2,16,16,128]{3,2,1,0:T(8,128)S(1)} %copy-done.29), channel_id=1, source_target_pairs={{2,0},{3,1},{0,2},{1,3},{6,4},{7,5},{4,6},{5,7},{10,8},{11,9},{8,1... | collective-permute-start | bytes 786440 | tf_op jit(solution)/shard_map/ppermute | solution.py:324
  54.6 3.2 %copy-start.16 = (f32[2,16,16,128]{3,2,1,0:T(8,128)}, f32[2,16,16,128]{3,2,1,0:T(8,128)S(1)}, u32[]{:S(2)}) copy-start(f32[2,16,16,128]{3,2,1,0:T(8,128)S(1)} %collective-permute-done.18.refs_1_) | copy-start | bytes 786436
  54.6 12.3 %collective-permute-start.14 = (f32[2,16,16,128]{3,2,1,0:T(8,128)S(1)}, f32[2,16,16,128]{3,2,1,0:T(8,128)S(1)}, u32[]{:S(2)}, u32[]{:S(2)}) collective-permute-start(f32[2,16,16,128]{3,2,1,0:T(8,128)S(1)} %copy-done.28), channel_id=1, source_target_pairs={{3,0},{2,1},{1,2},{0,3},{7,4},{6,5},{5,6},{4,7},{11,8},{10,9},{9,1... | collective-permute-start | bytes 786440 | tf_op jit(solution)/shard_map/ppermute | solution.py:324
  54.7 3.1 %copy-start.17 = (f32[2,16,16,128]{3,2,1,0:T(8,128)}, f32[2,16,16,128]{3,2,1,0:T(8,128)S(1)}, u32[]{:S(2)}) copy-start(f32[2,16,16,128]{3,2,1,0:T(8,128)S(1)} %collective-permute-done.19.refs_2_) | copy-start | bytes 786436
  54.7 16.5 %collective-permute-start.6 = (f32[2,16,16,128]{3,2,1,0:T(8,128)}, f32[2,16,16,128]{3,2,1,0:T(8,128)S(1)}, u32[]{:S(2)}, u32[]{:S(2)}) collective-permute-start(f32[2,16,16,128]{3,2,1,0:T(8,128)} %get-tuple-element.30), channel_id=1, source_target_pairs={{1,0},{0,1},{3,2},{2,3},{5,4},{4,5},{7,6},{6,7},{9,8},{8,9},{11,10... | collective-permute-start | bytes 786440 | tf_op jit(solution)/shard_map/ppermute | solution.py:324
  55.3 18.2 %collective-permute-start.7 = (f32[2,16,16,128]{3,2,1,0:T(8,128)}, f32[2,16,16,128]{3,2,1,0:T(8,128)S(1)}, u32[]{:S(2)}, u32[]{:S(2)}) collective-permute-start(f32[2,16,16,128]{3,2,1,0:T(8,128)} %get-tuple-element.31), channel_id=1, source_target_pairs={{2,0},{3,1},{0,2},{1,3},{6,4},{7,5},{4,6},{5,7},{10,8},{11,9},{8,1... | collective-permute-start | bytes 786440 | tf_op jit(solution)/shard_map/ppermute | solution.py:324
  61.4 6.3 %copy-start.14 = (f32[2,16,16,128]{3,2,1,0:T(8,128)}, f32[2,16,16,128]{3,2,1,0:T(8,128)S(1)}, u32[]{:S(2)}) copy-start(f32[2,16,16,128]{3,2,1,0:T(8,128)S(1)} %collective-permute-done.12.refs_1_) | copy-start | bytes 786436
  61.4 16.8 %collective-permute-start.8 = (f32[2,16,16,128]{3,2,1,0:T(8,128)S(1)}, f32[2,16,16,128]{3,2,1,0:T(8,128)S(1)}, u32[]{:S(2)}, u32[]{:S(2)}) collective-permute-start(f32[2,16,16,128]{3,2,1,0:T(8,128)S(1)} %copy-done.27), channel_id=1, source_target_pairs={{3,0},{2,1},{1,2},{0,3},{7,4},{6,5},{5,6},{4,7},{11,8},{10,9},{9,1... | collective-permute-start | bytes 786440 | tf_op jit(solution)/shard_map/ppermute | solution.py:324
  62.3 5.4 %copy-start.15 = (f32[2,16,16,128]{3,2,1,0:T(8,128)}, f32[2,16,16,128]{3,2,1,0:T(8,128)S(1)}, u32[]{:S(2)}) copy-start(f32[2,16,16,128]{3,2,1,0:T(8,128)S(1)} %collective-permute-done.13.refs_2_) | copy-start | bytes 786436
  62.3 20.2 %collective-permute-start.21 = (f32[2,16,16,128]{3,2,1,0:T(8,128)}, f32[2,16,16,128]{3,2,1,0:T(8,128)S(1)}, u32[]{:S(2)}, u32[]{:S(2)}) collective-permute-start(f32[2,16,16,128]{3,2,1,0:T(8,128)} %get-tuple-element.50), channel_id=1, source_target_pairs={{1,0},{0,1},{3,2},{2,3},{5,4},{4,5},{7,6},{6,7},{9,8},{8,9},{11,10... | collective-permute-start | bytes 786440 | tf_op jit(solution)/shard_map/ppermute | solution.py:324
  66.9 17.8 %collective-permute-start.22 = (f32[2,16,16,128]{3,2,1,0:T(8,128)}, f32[2,16,16,128]{3,2,1,0:T(8,128)S(1)}, u32[]{:S(2)}, u32[]{:S(2)}) collective-permute-start(f32[2,16,16,128]{3,2,1,0:T(8,128)} %get-tuple-element.51), channel_id=1, source_target_pairs={{2,0},{3,1},{0,2},{1,3},{6,4},{7,5},{4,6},{5,7},{10,8},{11,9},{8,1... | collective-permute-start | bytes 786440 | tf_op jit(solution)/shard_map/ppermute | solution.py:324
  71.2 7.7 %copy-start.12 = (f32[2,16,16,128]{3,2,1,0:T(8,128)}, f32[2,16,16,128]{3,2,1,0:T(8,128)S(1)}, u32[]{:S(2)}) copy-start(f32[2,16,16,128]{3,2,1,0:T(8,128)S(1)} %collective-permute-done.6.refs_1_) | copy-start | bytes 786436
  71.2 18.3 %collective-permute-start.23 = (f32[2,16,16,128]{3,2,1,0:T(8,128)}, f32[2,16,16,128]{3,2,1,0:T(8,128)S(1)}, u32[]{:S(2)}, u32[]{:S(2)}) collective-permute-start(f32[2,16,16,128]{3,2,1,0:T(8,128)} %get-tuple-element.52), channel_id=1, source_target_pairs={{3,0},{2,1},{1,2},{0,3},{7,4},{6,5},{5,6},{4,7},{11,8},{10,9},{9,1... | collective-permute-start | bytes 786440 | tf_op jit(solution)/shard_map/ppermute | solution.py:324
  73.5 5.4 %copy-start.13 = (f32[2,16,16,128]{3,2,1,0:T(8,128)}, f32[2,16,16,128]{3,2,1,0:T(8,128)S(1)}, u32[]{:S(2)}) copy-start(f32[2,16,16,128]{3,2,1,0:T(8,128)S(1)} %collective-permute-done.7.refs_2_) | copy-start | bytes 786436
  73.5 17.8 %collective-permute-start.15 = (f32[2,16,16,128]{3,2,1,0:T(8,128)}, f32[2,16,16,128]{3,2,1,0:T(8,128)S(1)}, u32[]{:S(2)}, u32[]{:S(2)}) collective-permute-start(f32[2,16,16,128]{3,2,1,0:T(8,128)} %get-tuple-element.42), channel_id=1, source_target_pairs={{1,0},{0,1},{3,2},{2,3},{5,4},{4,5},{7,6},{6,7},{9,8},{8,9},{11,10... | collective-permute-start | bytes 786440 | tf_op jit(solution)/shard_map/ppermute | solution.py:324
  78.2 20.4 %collective-permute-start.16 = (f32[2,16,16,128]{3,2,1,0:T(8,128)}, f32[2,16,16,128]{3,2,1,0:T(8,128)S(1)}, u32[]{:S(2)}, u32[]{:S(2)}) collective-permute-start(f32[2,16,16,128]{3,2,1,0:T(8,128)} %get-tuple-element.43), channel_id=1, source_target_pairs={{2,0},{3,1},{0,2},{1,3},{6,4},{7,5},{4,6},{5,7},{10,8},{11,9},{8,1... | collective-permute-start | bytes 786440 | tf_op jit(solution)/shard_map/ppermute | solution.py:324
  82.5 10.0 %copy-start.3 = (f32[2,16,16,128]{3,2,1,0:T(8,128)}, f32[2,16,16,128]{3,2,1,0:T(8,128)S(1)}, u32[]{:S(2)}) copy-start(f32[2,16,16,128]{3,2,1,0:T(8,128)S(1)} %collective-permute-done.21.refs_6_) | copy-start | bytes 786436
  82.5 18.3 %collective-permute-start.17 = (f32[2,16,16,128]{3,2,1,0:T(8,128)}, f32[2,16,16,128]{3,2,1,0:T(8,128)S(1)}, u32[]{:S(2)}, u32[]{:S(2)}) collective-permute-start(f32[2,16,16,128]{3,2,1,0:T(8,128)} %get-tuple-element.44), channel_id=1, source_target_pairs={{3,0},{2,1},{1,2},{0,3},{7,4},{6,5},{5,6},{4,7},{11,8},{10,9},{9,1... | collective-permute-start | bytes 786440 | tf_op jit(solution)/shard_map/ppermute | solution.py:324
  84.8 7.7 %copy-start.4 = (f32[2,16,16,128]{3,2,1,0:T(8,128)}, f32[2,16,16,128]{3,2,1,0:T(8,128)S(1)}, u32[]{:S(2)}) copy-start(f32[2,16,16,128]{3,2,1,0:T(8,128)S(1)} %collective-permute-done.22.refs_7_) | copy-start | bytes 786436
  84.8 23.3 %collective-permute-start.10 = (f32[2,16,16,128]{3,2,1,0:T(8,128)}, f32[2,16,16,128]{3,2,1,0:T(8,128)S(1)}, u32[]{:S(2)}, u32[]{:S(2)}) collective-permute-start(f32[2,16,16,128]{3,2,1,0:T(8,128)} %get-tuple-element.35), channel_id=1, source_target_pairs={{2,0},{3,1},{0,2},{1,3},{6,4},{7,5},{4,6},{5,7},{10,8},{11,9},{8,1... | collective-permute-start | bytes 786440 | tf_op jit(solution)/shard_map/ppermute | solution.py:324
  89.5 3.0 %copy-start.6 = (f32[2,16,16,128]{3,2,1,0:T(8,128)}, f32[2,16,16,128]{3,2,1,0:T(8,128)S(1)}, u32[]{:S(2)}) copy-start(f32[2,16,16,128]{3,2,1,0:T(8,128)S(1)} %collective-permute-done.23.refs_8_) | copy-start | bytes 786436
  89.5 21.7 %collective-permute-start.11 = (f32[2,16,16,128]{3,2,1,0:T(8,128)}, f32[2,16,16,128]{3,2,1,0:T(8,128)S(1)}, u32[]{:S(2)}, u32[]{:S(2)}) collective-permute-start(f32[2,16,16,128]{3,2,1,0:T(8,128)} %get-tuple-element.36), channel_id=1, source_target_pairs={{3,0},{2,1},{1,2},{0,3},{7,4},{6,5},{5,6},{4,7},{11,8},{10,9},{9,1... | collective-permute-start | bytes 786440 | tf_op jit(solution)/shard_map/ppermute | solution.py:324
  91.3 7.2 %copy-start.5 = (f32[2,16,16,128]{3,2,1,0:T(8,128)}, f32[2,16,16,128]{3,2,1,0:T(8,128)S(1)}, u32[]{:S(2)}) copy-start(f32[2,16,16,128]{3,2,1,0:T(8,128)S(1)} %collective-permute-done.15.refs_6_) | copy-start | bytes 786436
  91.3 19.9 %collective-permute-start.9 = (f32[2,16,16,128]{3,2,1,0:T(8,128)}, f32[2,16,16,128]{3,2,1,0:T(8,128)S(1)}, u32[]{:S(2)}, u32[]{:S(2)}) collective-permute-start(f32[2,16,16,128]{3,2,1,0:T(8,128)} %get-tuple-element.34), channel_id=1, source_target_pairs={{1,0},{0,1},{3,2},{2,3},{5,4},{4,5},{7,6},{6,7},{9,8},{8,9},{11,10... | collective-permute-start | bytes 786440 | tf_op jit(solution)/shard_map/ppermute | solution.py:324
  108.1 3.2 %copy-start.8 = (f32[2,16,16,128]{3,2,1,0:T(8,128)}, f32[2,16,16,128]{3,2,1,0:T(8,128)S(1)}, u32[]{:S(2)}) copy-start(f32[2,16,16,128]{3,2,1,0:T(8,128)S(1)} %collective-permute-done.10.refs_7_) | copy-start | bytes 786436
  120.7 20.1 %collective-permute-start.24 = (f32[3,16,32,128]{3,2,1,0:T(8,128)S(1)}, f32[3,16,32,128]{3,2,1,0:T(8,128)S(1)}, u32[]{:S(2)}, u32[]{:S(2)}) collective-permute-start(f32[3,16,32,128]{3,2,1,0:T(8,128)S(1)} %get-tuple-element.57), channel_id=1, source_target_pairs={{28,0},{0,4},{4,8},{8,12},{12,16},{16,20},{20,24},{24,28},{29,1},{... | collective-permute-start | bytes 2359304 | tf_op jit(solution)/shard_map/ppermute | solution.py:22
  120.7 39.0 %collective-permute-start.25 = (f32[3,16,32,128]{3,2,1,0:T(8,128)S(1)}, f32[3,16,32,128]{3,2,1,0:T(8,128)S(1)}, u32[]{:S(2)}, u32[]{:S(2)}) collective-permute-start(f32[3,16,32,128]{3,2,1,0:T(8,128)S(1)} %get-tuple-element.58), channel_id=1, source_target_pairs={{24,0},{28,4},{0,8},{4,12},{8,16},{12,20},{16,24},{20,28},{25,1},{... | collective-permute-start | bytes 2359304 | tf_op jit(solution)/shard_map/ppermute | solution.py:22
  (9 other events, 12.9 us)
